TPU v7x, 256 devices: a whole 4x4x8 slice. The times are simulated.
256 devices in a mesh: member: 32 (over x, z), domain: 8 (over y, core).
Axes of the slice: x: 4, y: 4, z: 8, core: 2. Of those that a mesh axis runs over, the one named last changes fastest.
Arguments:
- starting_tracer_fields: float32 [32, 2, 8, 512, 640], P('member', None, None, 'domain'), may hold values from -6 to 6
- surface_exchange_inputs: float32 [32, 2, 512, 640], P('member', None, 'domain'), may hold values from -4 to 4
- diffusivity: float32 [2, 8], replicated, may hold values from 0.04 to 0.2
- mixing: float32 [2, 7], replicated, may hold values from 0.02 to 0.1
- land_mask: int32 [512, 640], replicated, may hold values 0 or 1
- obs_index: int32 [8, 32, 256], P('domain'), may hold values from 0 to 1279
- obs_count: int32 [8, 32], P('domain'), may hold values from 1 to 256, as said below
- obs_value: float32 [8, 32, 256], P('domain'), may hold values from -8 to 8
- obs_error: float32 [8, 32, 256], P('domain'), may hold values from 1 to 16
Outputs:
- analysis: float32 [32, 2, 8, 512, 640], P('member', None, None, 'domain')
Inputs may be any that keep to these rules, and one draw needn't show every extreme that they name: `obs_index`: A cell of the tile's 2 x 640 surface cells, counted row by row. `obs_count`: slots below the count hold observations, the rest are unused; in every domain the last tile holds exactly 256.
All inputs are finite; a program needn't handle non-finite values.
Results may differ from a plain program's by a relative error of at most 0.0001.
Values sent between devices are 32-bit elements; how exact they have to be, the bound alone decides.
No kernel may reach another device: no remote copies, remote signals or barrier semaphores. Data moves between devices by JAX's collectives and lax.ppermute only.
A program may use at most 64 MiB of HBM per device.

v0:
```python
import jax
import jax.numpy as jnp
from jax import lax
from jax.sharding import PartitionSpec as P

STEPS = 2


def with_halo(shard, sides, width):
    for axis, dim in sides:
        size, length = (lax.axis_size(axis), shard.shape[dim])
        up = [(i, (i + 1) % size) for i in range(size - 1)]
        down = [(j, i) for i, j in up]
        last = lax.slice_in_dim(shard, length - width, length, axis=dim)
        initial = lax.slice_in_dim(shard, 0, width, axis=dim)
        before = lax.ppermute(last, axis, up)
        after = lax.ppermute(initial, axis, down)
        shard = jnp.concatenate([before, shard, after], axis=dim)
    return shard


def sent_to_all(shard, axis):
    copies = jnp.broadcast_to(shard, (lax.axis_size(axis), *shard.shape))
    return lax.all_to_all(copies, axis, split_axis=0, concat_axis=0, tiled=True)


def taken_together(shard, axis):
    everything = sent_to_all(shard, axis)
    return jnp.sum(everything, axis=0)


def together(arrays, axis):
    line, at, finished = (jnp.concatenate([a.reshape(-1) for a in arrays]), 0, [])
    running = taken_together(line, axis)
    for a in arrays:
        finished.append(running[at : at + a.size].reshape(a.shape))
        at += a.size
    return tuple(finished)


def stencil(padded, mask_rows, diffusivity, mixing, surface_exchange_inputs):
    middle = padded[:, :, 1:-1]
    mask_mid = mask_rows[1:-1]
    upper_row = padded[:, :, 2:]
    lower_row = padded[:, :, :-2]
    east_cell = jnp.roll(middle, -1, axis=3)
    west_cell = jnp.roll(middle, 1, axis=3)
    lateral = mask_rows[2:] * (upper_row - middle) + mask_rows[:-2] * (lower_row - middle)
    lateral = lateral + jnp.roll(mask_mid, -1, axis=1) * (east_cell - middle)
    lateral = lateral + jnp.roll(mask_mid, 1, axis=1) * (west_cell - middle)
    downward_flux = mixing[:, :, None, None] * (middle[:, 1:] - middle[:, :-1])
    empty_level = jnp.zeros_like(middle[:, :1])
    vertical = jnp.concatenate([downward_flux, empty_level], axis=1) - jnp.concatenate(
        [empty_level, downward_flux], axis=1
    )
    tendency = diffusivity[:, :, None, None] * lateral + vertical
    tendency = tendency.at[:, 0].add(surface_exchange_inputs)
    return middle + mask_mid * tendency


def partial_sums(observed, values, errors, active):
    average = jnp.mean(observed, axis=0)
    anomaly = observed - average[None, :]
    weight_obs = active / errors
    gram = jnp.dot(anomaly * weight_obs[None, :], anomaly.T, precision=lax.Precision.HIGHEST)
    pull = jnp.dot(anomaly, weight_obs * (values - average), precision=lax.Precision.HIGHEST)
    return (gram, pull)


def transform(gram, pull):
    count = gram.shape[0]
    identity = jnp.eye(count, dtype=gram.dtype)
    factor = jnp.linalg.cholesky(gram + (count - 1.0) * identity)
    inverse = jax.scipy.linalg.solve_triangular(factor, identity, lower=True)
    mean_weight = jnp.dot(
        inverse.T,
        jnp.dot(inverse, pull, precision=lax.Precision.HIGHEST),
        precision=lax.Precision.HIGHEST,
    )
    weights = mean_weight[:, None] + jnp.sqrt(count - 1.0) * inverse.T
    return weights - jnp.mean(weights, axis=0, keepdims=True) + 1.0 / count


def update(kernel, tile_block, tile_mask):
    count = tile_block.shape[0]
    updated = jnp.einsum(
        "jm,jn->mn", kernel, tile_block.reshape(count, -1), precision=lax.Precision.HIGHEST
    )
    return jnp.where(tile_mask > 0, updated.reshape(tile_block.shape), tile_block)


def shards(
    starting_tracer_fields,
    surface_exchange_inputs,
    diffusivity,
    mixing,
    land_mask,
    obs_index,
    obs_count,
    obs_value,
    obs_error,
):
    ocean_state = starting_tracer_fields[0]
    row_count = ocean_state.shape[2]
    longitudes = ocean_state.shape[3]
    subregion_offset = lax.axis_index("domain")
    sea_mask = land_mask.astype(jnp.float32)
    padded_mask = jnp.pad(sea_mask, ((1, 1), (0, 0)))
    local_mask = lax.dynamic_slice_in_dim(
        padded_mask, subregion_offset * row_count, row_count + 2, 0
    )
    for _ in range(STEPS):
        padded = with_halo(ocean_state, (("domain", 2),), 1)
        ocean_state = stencil(padded, local_mask, diffusivity, mixing, surface_exchange_inputs[0])
    stacked = ocean_state.reshape(1, -1, row_count, longitudes)
    members = lax.axis_size("member")
    tile_rows = row_count // members
    tile_index = lax.axis_index("member")
    tile_mask = lax.dynamic_slice_in_dim(local_mask[1:-1], tile_index * tile_rows, tile_rows, 0)
    slot_rank = jnp.arange(obs_index.shape[2], dtype=jnp.int32)
    tile_block = lax.all_to_all(stacked, "member", split_axis=2, concat_axis=0, tiled=True)
    surface = tile_block[:, 0].reshape(members, -1)
    obs_slots = lax.dynamic_index_in_dim(obs_index[0], tile_index, 0, keepdims=False)
    observed = surface[:, obs_slots]
    limit = lax.dynamic_index_in_dim(obs_count[0], tile_index, 0, keepdims=False)
    active = (slot_rank < limit).astype(jnp.float32)
    values = lax.dynamic_index_in_dim(obs_value[0], tile_index, 0, keepdims=False)
    errors = lax.dynamic_index_in_dim(obs_error[0], tile_index, 0, keepdims=False)
    gram, pull = partial_sums(observed, values, errors, active)
    gram, pull = together((gram, pull), "member")
    kernel = transform(gram, pull)
    updated = update(kernel, tile_block, tile_mask)
    returned = lax.all_to_all(updated, "member", split_axis=0, concat_axis=2, tiled=True)
    return returned.reshape(starting_tracer_fields.shape)


def solution(mesh):
    placed = (
        P("member", None, None, "domain", None),
        P("member", None, "domain", None),
        P(),
        P(),
        P(),
        P("domain", None, None),
        P("domain", None),
        P("domain", None, None),
        P("domain", None, None),
    )
    return jax.shard_map(
        shards,
        mesh=mesh,
        in_specs=placed,
        out_specs=P("member", None, None, "domain", None),
        check_vma=False,
    )
```

profile of v0, /device:TPU:8, one launch (start us, length us, event | category | flops | bytes accessed | tf_op | source)
XLA Modules:
  0.0 224.4 jit_solution(5305788101618709194)
XLA Ops:
  0.0 1.1 fusion.64
  1.1 1.9 collective-permute-start
  3.1 2.4 %collective-permute-start.1 = (f32[2,8,1,640]{3,2,1,0:T(1,128)S(1)}, f32[2,8,1,640]{3,2,1,0:T(1,128)S(1)}, u32[]{:S(2)}, u32[]{:S(2)}) collective-permute-start(f32[2,8,1,640]{3,2,1,0:T(1,128)S(1)} %get-tuple-element.42), channel_id=1, source_target_pairs={{0,1},{1,2},{2,3},{3,4},{4,5},{5,6},{6,7},{8,9},{9,10},{10,11},{11... | collective-permute-start | bytes 122888 | tf_op jit(solution)/shard_map/ppermute | solution.py:16
  5.5 2.2 fusion.62
  7.7 4.9 %fusion.63 = (f32[2,8,64,639]{3,2,1,0:T(8,128)S(1)}, f32[2,8,64,639]{3,2,1,0:T(8,128)}) fusion(f32[2,8,64,640]{3,2,1,0:T(8,128)} %bitcast.79), kind=kLoop, calls=%fused_computation.109 | loop fusion | bytes 10469376 | tf_op jit(solution)/shard_map/jit(_roll_static)/slice | solution.py:47
  12.5 1.4 convert_element_type.13
  14.2 0.8 copy-done.2
  15.1 1.1 copy-done.1
  16.2 0.3 fusion.25
  16.6 1.3 copy-done.3
  18.0 2.5 %fusion.15 = f32[2,8,64,640]{3,2,1,0:T(8,128)S(1)} fusion(f32[2,8,64,640]{3,2,1,0:T(8,128)S(1)} %bitcast.81, f32[2,8,1,640]{3,2,1,0:T(1,128)S(1)} %collective-permute-done.1, f32[2,8,1,640]{3,2,1,0:T(1,128)S(1)} %collective-permute-done, f32[2,8,64,1]{3,2,1,0:T(8,128)S(1)} %copy-done.4, f32[2,8,64,639]{3,2,1,0:T(8,128)S(1)} %copy-done.3, ...), kind=kLoop, calls=%fused_computation.19 | loop fusion | flops 11796480 | bytes 13516864 | tf_op jit(solution)/shard_map/add | solution.py:56
  20.6 0.3 multiply_add_fusion.1
  21.0 0.3 fusion.24
  21.4 0.9 fusion.60
  22.3 3.7 %collective-permute-start.2 = (f32[2,8,1,640]{3,2,1,0:T(1,128)S(1)}, f32[2,8,1,640]{3,2,1,0:T(1,128)S(1)}, u32[]{:S(2)}, u32[]{:S(2)}) collective-permute-start(f32[2,8,1,640]{3,2,1,0:T(1,128)S(1)} %get-tuple-element.35), channel_id=1, source_target_pairs={{1,0},{2,1},{3,2},{4,3},{5,4},{6,5},{7,6},{9,8},{10,9},{11,10},{12... | collective-permute-start | bytes 122888 | tf_op jit(solution)/shard_map/ppermute | solution.py:17
  26.0 1.9 collective-permute-start.3
  27.9 0.2 fusion.59
  28.1 3.2 %collective-permute-done.3 = f32[2,8,1,640]{3,2,1,0:T(1,128)S(1)} collective-permute-done((f32[2,8,1,640]{3,2,1,0:T(1,128)S(1)}, f32[2,8,1,640]{3,2,1,0:T(1,128)S(1)}, u32[]{:S(2)}, u32[]{:S(2)}) %collective-permute-start.3) | collective-permute-done | bytes 40992 | tf_op jit(solution)/shard_map/ppermute | solution.py:16
  31.3 2.6 %fusion.6 = f32[2,8,64,640]{3,2,1,0:T(8,128)S(1)} fusion(f32[2,8,64,640]{3,2,1,0:T(8,128)S(1)} %multiply_add_fusion.1, f32[2,8,1,640]{3,2,1,0:T(1,128)S(1)} %collective-permute-done.3, f32[2,8,1,640]{3,2,1,0:T(1,128)S(1)} %collective-permute-done.2, f32[2,8,64,1]{3,2,1,0:T(8,128)S(1)} %get-tuple-element.32, f32[2,8,64,639]{3,2,1,0:T(8,128)S(1)} %get-tuple-element.34, ...), kind=kLoop, calls=%fused_computation.8 | loop fusion | flops 11796480 | bytes 13516864 | tf_op jit(solution)/shard_map/add | solution.py:56
  33.9 0.3 multiply_add_fusion
  34.3 3.0 %copy.47 = f32[1,16,64,640]{3,1,0,2:T(8,128)} copy(f32[1,16,64,640]{3,2,1,0:T(8,128)S(1)} %bitcast.85) | data formatting | bytes 5242880 | tf_op jit(solution)/shard_map/reshape | solution.py:115
  37.3 10.8 %all-to-all-start = ((f32[1,16,64,640]{3,1,0,2:T(8,128)}), f32[1,16,64,640]{3,1,0,2:T(8,128)S(1)}, u32[]{:S(2)}, u32[]{:S(2)}) async-start(f32[1,16,64,640]{3,1,0,2:T(8,128)} %copy.47), calls=%async_computation | async-start | bytes 5242880 | tf_op jit(solution)/shard_map/all_to_all | solution.py:121
  48.1 0.6 constant_dynamic-slice_fusion.2
  48.7 0.7 compare_select_fusion
  49.4 0.7 constant_dynamic-slice_fusion
  50.1 60.9 %all-to-all-done = f32[1,16,64,640]{3,1,0,2:T(8,128)S(1)} async-done(((f32[1,16,64,640]{3,1,0,2:T(8,128)}), f32[1,16,64,640]{3,1,0,2:T(8,128)S(1)}, u32[]{:S(2)}, u32[]{:S(2)}) %all-to-all-start) | async-done | bytes 2621472 | tf_op jit(solution)/shard_map/all_to_all | solution.py:121
  111.0 1.5 copy.74
  112.5 0.7 slice.240
  113.2 1.1 copy.60
  114.4 0.7 gather_fusion
  115.2 0.6 subtract_multiply_fusion
  115.8 0.2 convolution_bitcast_fusion.2
  116.0 0.5 fusion.32
  116.6 0.7 broadcast_in_dim.7
  117.4 4.2 %all-to-all-start.1 = ((f32[32,1,1056]{2,1,0:T(1,128)}), f32[32,1,1056]{2,1,0:T(1,128)S(1)}, u32[]{:S(2)}, u32[]{:S(2)}) async-start(f32[32,1,1056]{2,1,0:T(1,128)} %broadcast_in_dim.7), calls=%async_computation.1 | async-start | bytes 294912 | tf_op jit(solution)/shard_map/all_to_all | solution.py:24
  121.6 0.9 fusion.53
  122.5 2.8 %copy.53 = f32[32,1,16,2,640]{4,3,2,0,1:T(2,128)} copy(f32[32,1,16,2,640]{4,2,3,0,1:T(8,128)S(1)} %bitcast.83) | data formatting | bytes 5242880 | tf_op jit(solution)/shard_map/all_to_all | solution.py:121
  125.3 4.5 %reshape.173 = f32[32,20480]{1,0:T(8,128)} reshape(f32[32,1,16,2,640]{4,3,2,0,1:T(2,128)} %copy.53) | data formatting | bytes 5242880 | tf_op jit(solution)/shard_map/reshape | solution.py:87
  129.8 4.6 %dot_general.24 = f32[16,2,640,32]{2,1,0,3:T(2,128)} reshape(f32[20480,32]{0,1:T(8,128)} %bitcast.86) | data formatting | bytes 5242880 | tf_op jit(solution)/shard_map/jm,jn->mn/dot_general | solution.py:86
  134.7 2.9 %cholesky.17 = f32[32,32]{1,0:T(8,128)S(1)} custom-call(f32[32,32]{1,0:T(8,128)S(1)} %fusion.44), custom_call_target="Cholesky" | custom-call | tf_op jit(solution)/shard_map/jit(cholesky)/cholesky | solution.py:73
  137.6 0.6 compare_reduce_fusion
  138.3 0.6 fusion.38
  138.8 2.4 %custom-call.7 = f32[1,32,32]{1,2,0:T(8,128)S(1)} custom-call(f32[1,32,32]{2,1,0:T(8,128)S(1)} %fusion.38), custom_call_target="InvertDiagBlocksLowerTriangular" | custom-call | tf_op jit(solution)/shard_map/jit(_solve_triangular)/triangular_solve | solution.py:74
  141.3 0.2 fusion.42
  141.9 6.9 %fusion.26 = f32[32,16,2,640]{3,0,2,1:T(8,128)S(1)} fusion(f32[16,2,640,32]{2,1,0,3:T(2,128)} %dot_general.24, pred[2,640]{1,0:T(4,128)(4,1)S(1)} %fusion.53, f32[32,32]{0,1:T(8,128)S(1)} %fusion.42, f32[32]{0:T(128)S(1)} %broadcast_multiply_fusion.1, f32[32]{0:T(128)S(1)} %convolution_bitcast_fusion, f32[1,16,32,2,640]{4,1,3,2,0:T(8,128)S(1)} %bitcast.84), kind=kOutput, calls=%fused_computation.40 | convolution fusion | flops 252317696 | bytes 7869952 | tf_op jit(solution)/shard_map/jm,jn->mn/dot_general | solution.py:86
  148.9 2.0 copy.56
  150.9 71.0 %all_to_all.39 = f32[32,16,2,640]{3,2,1,0:T(2,128)S(1)} all-to-all(f32[32,16,2,640]{3,2,1,0:T(2,128)S(1)} %copy.56), channel_id=1, replica_groups=mesh['member'=32,'domain'=8] {'member'}, dimensions={0} | all-to-all | bytes 5242880 | tf_op jit(solution)/shard_map/all_to_all | solution.py:133
  222.1 2.3 %copy.58 = f32[1,2,8,64,640]{4,3,2,1,0:T(8,128)} copy(f32[1,2,8,64,640]{4,2,1,3,0:T(8,128)S(1)} %bitcast.87) | data formatting | bytes 5242880 | tf_op jit(solution)/shard_map/reshape | solution.py:134
  (40 shorter events, 1.7 us)
Async XLA Ops:
  0.0 48.1 %copy-start = (s32[1,32]{1,0:T(1,128)S(1)}, s32[1,32]{1,0:T(1,128)}, u32[]{:S(2)}) copy-start(s32[1,32]{1,0:T(1,128)} %param.19) | copy-start | bytes 388
  1.1 15.5 %collective-permute-start = (f32[2,8,1,640]{3,2,1,0:T(1,128)S(1)}, f32[2,8,1,640]{3,2,1,0:T(1,128)S(1)}, u32[]{:S(2)}, u32[]{:S(2)}) collective-permute-start(f32[2,8,1,640]{3,2,1,0:T(1,128)S(1)} %get-tuple-element.41), channel_id=1, source_target_pairs={{1,0},{2,1},{3,2},{4,3},{5,4},{6,5},{7,6},{9,8},{10,9},{11,10},{12... | collective-permute-start | bytes 122888 | tf_op jit(solution)/shard_map/ppermute | solution.py:17
  3.1 13.5 %collective-permute-start.1 = (f32[2,8,1,640]{3,2,1,0:T(1,128)S(1)}, f32[2,8,1,640]{3,2,1,0:T(1,128)S(1)}, u32[]{:S(2)}, u32[]{:S(2)}) collective-permute-start(f32[2,8,1,640]{3,2,1,0:T(1,128)S(1)} %get-tuple-element.42), channel_id=1, source_target_pairs={{0,1},{1,2},{2,3},{3,4},{4,5},{5,6},{6,7},{8,9},{9,10},{10,11},{11... | collective-permute-start | bytes 122888 | tf_op jit(solution)/shard_map/ppermute | solution.py:16
  13.9 1.1 copy-start.2
  13.9 2.2 copy-start.1
  13.9 2.2 copy-start.6
  16.2 1.7 copy-start.3
  16.2 1.8 copy-start.4
  16.2 1.8 copy-start.7
  18.0 2.6 %copy-start.5 = (f32[1,2,64,640]{3,2,1,0:T(8,128)S(1)}, f32[1,2,64,640]{3,2,1,0:T(8,128)}, u32[]{:S(2)}) copy-start(f32[1,2,64,640]{3,2,1,0:T(8,128)} %param.14) | copy-start | bytes 983044
  22.3 5.8 %collective-permute-start.2 = (f32[2,8,1,640]{3,2,1,0:T(1,128)S(1)}, f32[2,8,1,640]{3,2,1,0:T(1,128)S(1)}, u32[]{:S(2)}, u32[]{:S(2)}) collective-permute-start(f32[2,8,1,640]{3,2,1,0:T(1,128)S(1)} %get-tuple-element.35), channel_id=1, source_target_pairs={{1,0},{2,1},{3,2},{4,3},{5,4},{6,5},{7,6},{9,8},{10,9},{11,10},{12... | collective-permute-start | bytes 122888 | tf_op jit(solution)/shard_map/ppermute | solution.py:17
  26.0 5.3 %collective-permute-start.3 = (f32[2,8,1,640]{3,2,1,0:T(1,128)S(1)}, f32[2,8,1,640]{3,2,1,0:T(1,128)S(1)}, u32[]{:S(2)}, u32[]{:S(2)}) collective-permute-start(f32[2,8,1,640]{3,2,1,0:T(1,128)S(1)} %get-tuple-element.36), channel_id=1, source_target_pairs={{0,1},{1,2},{2,3},{3,4},{4,5},{5,6},{6,7},{8,9},{9,10},{10,11},{11... | collective-permute-start | bytes 122888 | tf_op jit(solution)/shard_map/ppermute | solution.py:16
  37.3 73.7 %all-to-all-start = ((f32[1,16,64,640]{3,1,0,2:T(8,128)}), f32[1,16,64,640]{3,1,0,2:T(8,128)S(1)}, u32[]{:S(2)}, u32[]{:S(2)}) async-start(f32[1,16,64,640]{3,1,0,2:T(8,128)} %copy.47), calls=%async_computation | async-start | bytes 5242880 | tf_op jit(solution)/shard_map/all_to_all | solution.py:121
  117.4 17.0 %all-to-all-start.1 = ((f32[32,1,1056]{2,1,0:T(1,128)}), f32[32,1,1056]{2,1,0:T(1,128)S(1)}, u32[]{:S(2)}, u32[]{:S(2)}) async-start(f32[32,1,1056]{2,1,0:T(1,128)} %broadcast_in_dim.7), calls=%async_computation.1 | async-start | bytes 294912 | tf_op jit(solution)/shard_map/all_to_all | solution.py:24
where the time goes:
time: 225 us; the launch traced here: 224 us
  blocking collectives  71 us (32%)
  waiting for transfers between devices  64.1 us (28%)
  local copies, waits for them, and re-layouts  38.7 us (17%)
  starting transfers between devices  24.9 us (11%)
  other arithmetic  17.1 us (8%)
  matrix products  8.21 us (4%)
    all_to_all x1, blocking collectives, shards(): lax.all_to_all(updated, 'member', split_axis=0, concat_axis=2, tiled=True)  71 us
    all_to_all x1, waiting for transfers between devices, shards(): lax.all_to_all(stacked, 'member', split_axis=2, concat_axis=0, tiled=True)  60.9 us
    all_to_all x1, starting transfers between devices, shards(): lax.all_to_all(stacked, 'member', split_axis=2, concat_axis=0, tiled=True)  10.8 us
    slice x4, local copies, waits for them, and re-layouts, stencil(): west_cell = jnp.roll(middle, 1, axis=3)  8.15 us
    dot_general x1, matrix products, update(): jnp.einsum('jm,jn->mn', kernel, tile_block.reshape(count, -1), precision=...  6.94 us
    ppermute x2, starting transfers between devices, with_halo(): after = lax.ppermute(initial, axis, down)  5.6 us
    add x2, other arithmetic, stencil(): tendency = diffusivity[:, :, None, None] * lateral + vertical  5.1 us
    dot_general x1, local copies, waits for them, and re-layouts, update(): jnp.einsum('jm,jn->mn', kernel, tile_block.reshape(count, -1), precision=...  4.61 us
  transfers between devices with their start and end apart: 6, of which 2 were waited for; matrix products, arithmetic and copies ran while one was open for 11% of the time, Pallas kernels for 0%

commit v1 on v0

v1 whole, which is shorter than its diff:
```python
import functools

import jax
import jax.numpy as jnp
from jax import lax
from jax.experimental import pallas as pl
from jax.experimental.pallas import tpu as pltpu
from jax.sharding import PartitionSpec as P

FIELDS = 2
LEVELS = 8
LANES = 128
HALO = 2


def stencil_rows(src, dst, first, last, field, mask, crowd, flux, coef):
    lateral, above, below = coef
    vertical = above + below
    top = lax.broadcasted_iota(jnp.int32, above.shape, 0) == 0

    def row(r, _):
        x = src[r]
        sea = mask[pl.ds(r, 1), :]
        wet = sea * x
        width = x.shape[1]
        around = mask[pl.ds(r + 1, 1), :] * src[r + 1] + mask[pl.ds(r - 1, 1), :] * src[r - 1]
        around = around + pltpu.roll(wet, 1, 1) + pltpu.roll(wet, width - 1, 1)
        up = pltpu.roll(x, LEVELS - 1, 0)
        down = pltpu.roll(x, 1, 0)
        source = jnp.where(top, flux[pl.ds(r - 1, 1), :], 0.0)
        change = lateral * around + above * up + below * down
        change = change - (lateral * crowd[pl.ds(r, 1), :] + vertical) * x + source
        dst(r, x + sea * change)
        return 0

    lax.fori_loop(first, last, row, 0, unroll=2)


def forecast_kernel(field, x_ref, before_ref, after_ref, flux_ref, mask_ref, diff_ref, mix_ref,
                    *rest):
    if field == 0:
        index_ref, out_ref, observed_ref, now, later, crowd, flux, surface = rest
    else:
        _, out_ref, now, later, crowd, flux = rest
    rows, width = x_ref.shape[3], x_ref.shape[4]
    tall = rows + 2 * HALO
    blocks = width // LANES
    level = lax.broadcasted_iota(jnp.int32, (LEVELS, width), 0)

    lateral = jnp.zeros((LEVELS, width), jnp.float32)
    above = jnp.zeros((LEVELS, width), jnp.float32)
    below = jnp.zeros((LEVELS, width), jnp.float32)
    for l in range(LEVELS):
        lateral = jnp.where(level == l, diff_ref[field, l], lateral)
        if l < LEVELS - 1:
            above = jnp.where(level == l, mix_ref[field, l], above)
            below = jnp.where(level == l + 1, mix_ref[field, l], below)
    coef = (lateral, above, below)

    sea = mask_ref[1 : tall - 1, :]
    crowd[1 : tall - 1, :] = (
        mask_ref[0 : tall - 2, :] + mask_ref[2:tall, :]
        + pltpu.roll(sea, 1, 1) + pltpu.roll(sea, width - 1, 1)
    )
    flux[0:1, :] = before_ref[field, HALO * LEVELS : HALO * LEVELS + 1, :]
    flux[1 : rows + 1, :] = flux_ref[0, 0]
    flux[rows + 1 : rows + 2, :] = after_ref[field, HALO * LEVELS : HALO * LEVELS + 1, :]
    for h in range(HALO):
        now[h] = before_ref[field, h * LEVELS : (h + 1) * LEVELS, :]
        now[HALO + rows + h] = after_ref[field, h * LEVELS : (h + 1) * LEVELS, :]

    def turn(b, _):
        start = pl.multiple_of(b * 8, 8)
        now[pl.ds(HALO + start, 8)] = jnp.swapaxes(x_ref[0, 0, :, pl.ds(start, 8), :], 0, 1)
        return 0

    lax.fori_loop(0, rows // 8, turn, 0)

    def keep(r, value):
        later[r] = value

    stencil_rows(now, keep, 1, tall - 1, field, mask_ref, crowd, flux, coef)

    def emit(r, value):
        row = r - HALO
        tile = row // 2
        side = row % 2
        for j in range(blocks):
            out_ref[tile, side * blocks + j] = value[:, j * LANES : (j + 1) * LANES]
        if field == 0:
            surface[side, pl.ds(tile, 1), :] = value[0:1, :]

    stencil_rows(later, emit, HALO, HALO + rows, field, mask_ref, crowd, flux, coef)

    if field == 0:
        tiles = rows // 2
        slots = index_ref.shape[2]
        for g in range(tiles // 8):
            for h in range(slots // LANES):
                where = index_ref[0, g * 8 : (g + 1) * 8, h * LANES : (h + 1) * LANES]
                block, lane = where >> 7, where & (LANES - 1)
                found = jnp.zeros((8, LANES), jnp.float32)
                for q in range(2 * blocks):
                    s, j = divmod(q, blocks)
                    source = surface[s, g * 8 : (g + 1) * 8, j * LANES : (j + 1) * LANES]
                    taken = jnp.take_along_axis(source, lane, axis=1, mode="promise_in_bounds")
                    found = jnp.where(block == q, taken, found)
                observed_ref[g * 8 : (g + 1) * 8, h, :] = found


def gram_kernel(tile_ref, seen_ref, value_ref, error_ref, count_ref, _, out_ref):
    tile = tile_ref[0]
    halves = seen_ref.shape[1]
    members = seen_ref.shape[0]
    slot = lax.broadcasted_iota(jnp.int32, (1, LANES), 1)
    total = jnp.zeros((members + 8, members), jnp.float32)
    for h in range(halves):
        seen = seen_ref[:, h, :]
        average = jnp.mean(seen, axis=0, keepdims=True)
        anomaly = seen - average
        span = slice(h * LANES, (h + 1) * LANES)
        own = lax.broadcasted_iota(jnp.int32, (value_ref.shape[1], LANES), 0) == tile
        value = jnp.sum(jnp.where(own, value_ref[0, :, span], 0.0), axis=0, keepdims=True)
        error = jnp.sum(jnp.where(own, error_ref[0, :, span], 0.0), axis=0, keepdims=True)
        active = jnp.where(slot + h * LANES < count_ref[0, tile], 1.0, 0.0)
        weight = active / error
        drift = weight * (value - average)
        left = jnp.concatenate([anomaly * weight, jnp.broadcast_to(drift, (8, LANES))], axis=0)
        total = total + lax.dot_general(
            left, anomaly, (((1,), (1,)), ((), ())),
            precision=lax.Precision.HIGHEST, preferred_element_type=jnp.float32,
        )
    packed = jnp.concatenate([total[g * 8 : (g + 1) * 8] for g in range(4)], axis=1)
    pull = jnp.concatenate([total[members : members + 8]] * 4, axis=1)
    row = lax.broadcasted_iota(jnp.int32, packed.shape, 0)
    lane = lax.broadcasted_iota(jnp.int32, packed.shape, 1)
    corner = (lane >= 16) & (lane < 32)
    packed = jnp.where(corner & (row == 0), pltpu.roll(pull, 16, 1), packed)
    packed = jnp.where(corner & (row == 1), pull, packed)
    out_ref[...] = jnp.broadcast_to(packed[None, None], out_ref.shape)


def ensemble_kernel(packed, wide):
    count = 32
    lane = lax.broadcasted_iota(jnp.int32, (count, LANES), 1)
    row = lax.broadcasted_iota(jnp.int32, (count, LANES), 0)
    gram = jnp.concatenate(
        [packed if g == 0 else pltpu.roll(packed, LANES - g * count, 1) for g in range(4)], axis=0
    )
    pull = jnp.where(
        lane[0:1] < 16,
        pltpu.roll(packed[0:8], LANES - 16, 1)[0:1],
        packed[1:2],
    )
    gram = gram + jnp.where(lane == row, count - 1.0, 0.0)
    columns = [jnp.broadcast_to(gram[:, k : k + 1], (count, LANES)) for k in range(count)]
    work = jnp.where(lane == row, 1.0, 0.0)
    for k in range(count):
        base = (k // 8) * 8
        column = columns[k][base:]
        pivot = jnp.broadcast_to(column[k - base : k - base + 1], (8, LANES))
        scale = lax.rsqrt(pivot)
        scale = scale * (1.5 - 0.5 * pivot * scale * scale)
        head = scale[0:1]
        lead = work[k : k + 1] * head
        column = column * head
        below = row[base:] > k
        factor = jnp.where(below, column, 0.0)
        rest = jnp.where(row[base:] == k, lead, work[base:] - factor * lead)
        work = rest if base == 0 else jnp.concatenate([work[:base], rest], axis=0)
        for c in range(k + 1, count):
            cbase = (c // 8) * 8
            ratio = column[c - base : c - base + 1]
            old = columns[c]
            fresh = old[cbase:] - column[cbase - base :] * ratio
            columns[c] = fresh if cbase == 0 else jnp.concatenate([old[:cbase], fresh], axis=0)
    inverse = work
    gained = jnp.sum(inverse * pull, axis=1, keepdims=True)
    mean_weight = jnp.sum(inverse * gained, axis=0, keepdims=True)
    live = lane < count
    weights = jnp.where(live, mean_weight + jnp.sqrt(count - 1.0) * inverse, 0.0)
    centre = jnp.sum(weights, axis=1, keepdims=True) * (1.0 / count)
    return jnp.where(live, weights - centre + 1.0 / count, 0.0)


def mix_kernel(gram_ref, data_ref, mask_ref, out_ref, high, low):
    members, blocks = data_ref.shape[0], data_ref.shape[1]
    deep = members * LEVELS

    @pl.when(pl.program_id(0) == 0)
    def _():
        kernel = ensemble_kernel(jnp.sum(gram_ref[:, 0], axis=0), LANES)[:, :members]
        major = kernel.astype(jnp.bfloat16)
        minor = (kernel - major.astype(jnp.float32)).astype(jnp.bfloat16)
        spread = (
            lax.broadcasted_iota(jnp.int32, (deep, members), 0) // LEVELS
            == lax.broadcasted_iota(jnp.int32, (deep, members), 1)
        ).astype(jnp.bfloat16)
        same = (
            lax.broadcasted_iota(jnp.int32, (deep, deep), 0) % LEVELS
            == lax.broadcasted_iota(jnp.int32, (deep, deep), 1) % LEVELS
        )
        for part, target in ((major, high), (minor, low)):
            tall = jnp.dot(spread, part, preferred_element_type=jnp.float32).astype(jnp.bfloat16)
            full = lax.dot_general(
                tall, spread, (((1,), (1,)), ((), ())), preferred_element_type=jnp.float32
            )
            target[...] = jnp.where(same, full, 0.0).astype(jnp.bfloat16)

    data = jnp.concatenate([data_ref[:, b].reshape(deep, LANES) for b in range(blocks)], axis=1)
    major = data.astype(jnp.bfloat16)
    minor = (data - major.astype(jnp.float32)).astype(jnp.bfloat16)
    mixed = jnp.dot(high[...], major, preferred_element_type=jnp.float32)
    mixed = mixed + jnp.dot(high[...], minor, preferred_element_type=jnp.float32)
    mixed = mixed + jnp.dot(low[...], major, preferred_element_type=jnp.float32)
    ocean = mask_ref[pl.ds(pl.program_id(0) % 2, 1), :] > 0.0
    mixed = jnp.where(ocean, mixed, data)
    for b in range(blocks):
        out_ref[:, b] = mixed[:, b * LANES : (b + 1) * LANES].reshape(members, LEVELS, LANES)


def settle_kernel(back_ref, out_ref):
    blocks = out_ref.shape[4] // LANES
    for f in range(FIELDS):
        for j in range(blocks):
            rows = []
            for t in range(4):
                for s in range(2):
                    rows.append(back_ref[t, (f * 2 + s) * blocks + j])
            turned = jnp.swapaxes(jnp.stack(rows, axis=0), 0, 1)
            out_ref[0, f, :, :, j * LANES : (j + 1) * LANES] = turned


def shards(
    starting_tracer_fields,
    surface_exchange_inputs,
    diffusivity,
    mixing,
    land_mask,
    obs_index,
    obs_count,
    obs_value,
    obs_error,
):
    _, fields, levels, rows, width = starting_tracer_fields.shape
    members = lax.axis_size("member")
    domains = lax.axis_size("domain")
    blocks = width // LANES
    tiles = members
    per_field = 2 * blocks
    slabs = fields * per_field + 1
    tile = lax.axis_index("member")
    domain = lax.axis_index("domain")
    state, flux = starting_tracer_fields[0], surface_exchange_inputs[0]

    def edge(first, flux_row):
        lines = jnp.swapaxes(state[:, :, first : first + HALO], 1, 2)
        lines = lines.reshape(fields, HALO * levels, width)
        return jnp.concatenate([lines, flux[:, flux_row : flux_row + 1]], axis=1)

    up = [(i, i + 1) for i in range(domains - 1)]
    down = [(i + 1, i) for i in range(domains - 1)]
    before = lax.ppermute(edge(rows - HALO, rows - 1), "domain", up)
    after = lax.ppermute(edge(0, 0), "domain", down)

    padded = jnp.pad(land_mask, ((HALO, HALO), (0, 0)))
    mask = lax.dynamic_slice_in_dim(padded, domain * rows, rows + 2 * HALO, 0).astype(jnp.float32)
    tile_mask = lax.dynamic_slice_in_dim(mask, HALO + tile * 2, 2, 0)

    f32 = jnp.float32
    tall = rows + 2 * HALO
    bulk = jax.ShapeDtypeStruct((tiles, slabs, levels, LANES), f32)

    def whole(*shape):
        return pl.BlockSpec(shape, lambda i: (0,) * len(shape))

    def forecast(field, extra):
        in_specs = [
            pl.BlockSpec((1, 1, levels, rows, width), lambda i: (0, field, 0, 0, 0)),
            whole(fields, HALO * levels + 1, width),
            whole(fields, HALO * levels + 1, width),
            pl.BlockSpec((1, 1, rows, width), lambda i: (0, field, 0, 0)),
            whole(tall, width),
            pl.BlockSpec(memory_space=pltpu.SMEM),
            pl.BlockSpec(memory_space=pltpu.SMEM),
        ]
        out_shape = [bulk]
        out_specs = [pl.BlockSpec((tiles, per_field, levels, LANES), lambda i: (0, field, 0, 0))]
        scratch = [
            pltpu.VMEM((tall, levels, width), f32),
            pltpu.VMEM((tall, levels, width), f32),
            pltpu.VMEM((tall, width), f32),
            pltpu.VMEM((rows + 2, width), f32),
        ]
        alias = {}
        if field == 0:
            in_specs.append(whole(*obs_index.shape))
            slots = obs_index.shape[2]
            out_shape.append(jax.ShapeDtypeStruct((tiles, slots // LANES, LANES), f32))
            out_specs.append(whole(tiles, slots // LANES, LANES))
            scratch.append(pltpu.VMEM((2, tiles, width), f32))
        else:
            in_specs.append(pl.BlockSpec(memory_space=pl.ANY))
            alias = {7: 0}
        return pl.pallas_call(
            functools.partial(forecast_kernel, field),
            grid=(1,),
            out_shape=out_shape,
            in_specs=in_specs,
            out_specs=out_specs,
            scratch_shapes=scratch,
            input_output_aliases=alias,
            cost_estimate=pl.CostEstimate(
                flops=40_000_000, bytes_accessed=3_000_000, transcendentals=0
            ),
            name=f"forecast_{field}",
        )(
            starting_tracer_fields, before, after, surface_exchange_inputs, mask,
            diffusivity, mixing, extra,
        )

    sent, observed = forecast(0, obs_index)
    seen = lax.all_to_all(observed, "member", split_axis=0, concat_axis=0, tiled=True)
    (sent,) = forecast(1, sent)

    sent = pl.pallas_call(
        gram_kernel,
        grid=(1,),
        out_shape=bulk,
        in_specs=[
            pl.BlockSpec(memory_space=pltpu.SMEM),
            whole(*seen.shape),
            whole(*obs_value.shape),
            whole(*obs_error.shape),
            pl.BlockSpec(memory_space=pltpu.SMEM),
            pl.BlockSpec(memory_space=pl.ANY),
        ],
        out_specs=pl.BlockSpec((tiles, 1, levels, LANES), lambda i: (0, slabs - 1, 0, 0)),
        input_output_aliases={5: 0},
        name="gram",
    )(tile.reshape(1).astype(jnp.int32), seen, obs_value, obs_error, obs_count, sent)

    held = lax.all_to_all(sent, "member", split_axis=0, concat_axis=0, tiled=True)

    deep = members * levels
    updated = pl.pallas_call(
        mix_kernel,
        grid=(fields * 2,),
        out_shape=jax.ShapeDtypeStruct((members, slabs - 1, levels, LANES), f32),
        in_specs=[
            pl.BlockSpec((members, 1, levels, LANES), lambda i: (0, slabs - 1, 0, 0)),
            pl.BlockSpec((members, blocks, levels, LANES), lambda i: (0, i, 0, 0)),
            whole(2, width),
        ],
        out_specs=pl.BlockSpec((members, blocks, levels, LANES), lambda i: (0, i, 0, 0)),
        scratch_shapes=[
            pltpu.VMEM((deep, deep), jnp.bfloat16),
            pltpu.VMEM((deep, deep), jnp.bfloat16),
        ],
        name="mix",
    )(held, held, tile_mask)

    back = lax.all_to_all(updated, "member", split_axis=0, concat_axis=0, tiled=True)

    return pl.pallas_call(
        settle_kernel,
        grid=(rows // 8,),
        out_shape=jax.ShapeDtypeStruct(starting_tracer_fields.shape, f32),
        in_specs=[pl.BlockSpec((4, slabs - 1, levels, LANES), lambda i: (i, 0, 0, 0))],
        out_specs=pl.BlockSpec((1, fields, levels, 8, width), lambda i: (0, 0, 0, i, 0)),
        name="settle",
    )(back)


def solution(mesh):
    placed = (
        P("member", None, None, "domain", None),
        P("member", None, "domain", None),
        P(),
        P(),
        P(),
        P("domain", None, None),
        P("domain", None),
        P("domain", None, None),
        P("domain", None, None),
    )
    return jax.shard_map(
        shards,
        mesh=mesh,
        in_specs=placed,
        out_specs=P("member", None, None, "domain", None),
        check_vma=False,
    )
```

time: 225 us -> 205 us (0.911)
  Pallas kernels: 0 us -> 34.1 us
  local copies, waits for them, and re-layouts: 38.7 us -> 6.07 us
  other arithmetic: 17.1 us -> 1.67 us
  matrix products: 8.21 us -> 0 us
    pallas_call x0 -> x5, Pallas kernels: none -> 34.1 us  [the longest x2 20.1 us: forecast(): pl.pallas_call(functools.partial(forecast_kernel, field), grid=(1,), out_...]
    reshape x5 -> x0, local copies, waits for them, and re-layouts: 9.94 us -> none  [the longest x1 4.48 us: update(): tile_block.reshape(count, -1)]
    slice x11 -> x1, local copies, waits for them, and re-layouts: 10.3 us -> 0.81 us  [edge(): return jnp.concatenate([lines, flux[:, flux_row:flux_row + 1]], axis=1)]
    dot_general x5 -> x0, matrix products: 7.98 us -> none  [the longest x1 6.94 us: update(): jnp.einsum('jm,jn->mn', kernel, tile_block.reshape(count, -1), precision=...]
    another operation x5 -> x0, other arithmetic: 6.6 us -> none  [the longest x3 3.59 us: transform(): factor = jnp.linalg.cholesky(gram + (count - 1.0) * identity)]
    all_to_all x2, starting transfers between devices: 15 us -> 21 us  [the longest x1 11.3 us: shards(): lax.all_to_all(observed, 'member', split_axis=0, concat_axis=0, tiled=True)]
    add x5 -> x0, other arithmetic: 5.78 us -> none  [the longest x2 5.1 us: stencil(): tendency = diffusivity[:, :, None, None] * lateral + vertical]
    dot_general x1 -> x0, local copies, waits for them, and re-layouts: 4.61 us -> none  [update(): jnp.einsum('jm,jn->mn', kernel, tile_block.reshape(count, -1), precision=...]
  transfers between devices with their start and end apart: 6 -> 4, of which waited for: 2 -> 3; matrix products, arithmetic and copies ran while one was open for 11% -> 1% of each run, Pallas kernels for 0% -> 5%
where the time goes in v1:
time: 205 us; the launch traced here: 203 us
  blocking collectives  68.8 us (34%)
  waiting for transfers between devices  65.9 us (32%)
  Pallas kernels  34.1 us (17%)
  starting transfers between devices  26.6 us (13%)
  local copies, waits for them, and re-layouts  6.07 us (3%)
    all_to_all x1, blocking collectives, shards(): lax.all_to_all(updated, 'member', split_axis=0, concat_axis=0, tiled=True)  68.8 us
    all_to_all x1, waiting for transfers between devices, shards(): lax.all_to_all(sent, 'member', split_axis=0, concat_axis=0, tiled=True)  65 us
    pallas_call x2, Pallas kernels, forecast(): pl.pallas_call(functools.partial(forecast_kernel, field), grid=(1,), out_...  20.1 us
    all_to_all x1, starting transfers between devices, shards(): lax.all_to_all(observed, 'member', split_axis=0, concat_axis=0, tiled=True)  11.3 us
    all_to_all x1, starting transfers between devices, shards(): lax.all_to_all(sent, 'member', split_axis=0, concat_axis=0, tiled=True)  9.69 us
    pallas_call x1, Pallas kernels, shards(): pl.pallas_call(mix_kernel, grid=(fields * 2,), out_shape=jax.ShapeDtypeSt...  6.13 us
    pallas_call x1, Pallas kernels, shards(): pl.pallas_call(settle_kernel, grid=(rows // 8,), out_shape=jax.ShapeDtype...  6.01 us
  transfers between devices with their start and end apart: 4, of which 3 were waited for; matrix products, arithmetic and copies ran while one was open for 1% of the time, Pallas kernels for 5%

profile of v1, /device:TPU:8, one launch (start us, length us, event | category | flops | bytes accessed | tf_op | source)
XLA Modules:
  0.0 203.2 jit_solution(6661920384546909630)
XLA Ops:
  0.0 0.8 fusion.1
  0.8 1.1 slice_bitcast_fusion
  2.0 1.9 collective-permute-start
  3.9 3.6 %collective-permute-start.1 = (f32[2,17,640]{2,1,0:T(8,128)S(1)}, f32[2,17,640]{2,1,0:T(8,128)S(1)}, u32[]{:S(2)}, u32[]{:S(2)}) collective-permute-start(f32[2,17,640]{2,1,0:T(8,128)S(1)} %pad_maximum_fusion.1), channel_id=1, source_target_pairs={{1,0},{2,1},{3,2},{4,3},{5,4},{6,5},{7,6},{9,8},{10,9},{11,10},{12... | collective-permute-start | bytes 261128 | tf_op jit(solution)/shard_map/ppermute | solution.py:264
  7.6 1.6 fusion.mask_ref
  9.2 0.0 collective-permute-done.before_ref
  9.2 0.0 copy-start.1
  9.2 0.8 collective-permute-done.1.after_ref
  10.0 0.0 copy-done.1
  10.0 0.0 copy-start.2
  10.0 0.7 copy-done.2
  10.7 10.3 %forecast_0.1 = (f32[32,21,8,128]{3,2,1,0:T(8,128)}, f32[32,2,128]{2,1,0:T(2,128)}) custom-call(f32[1,2,8,64,640]{4,3,2,1,0:T(8,128)} %x_ref.3, f32[2,17,640]{2,1,0:T(8,128)} %copy-done.1, f32[2,17,640]{2,1,0:T(8,128)} %copy-done.2, f32[1,2,64,640]{3,2,1,0:T(8,128)} %flux_ref.3, f32[68,640]{1,0:T(8,128)} %fusion.mask_ref, f32[2,8]{1,0:T(2,128)} %diff_ref.3, ...), custom_call_target="tpu_custom_call" | custom-call | flops 40000000 | bytes 3000000 | tf_op jit(solution)/shard_map/forecast_0/pallas_call | solution.py:305
  20.9 11.3 %all-to-all-start = ((f32[32,2,128]{2,1,0:T(2,128)}), f32[32,2,128]{2,1,0:T(2,128)S(1)}, u32[]{:S(2)}, u32[]{:S(2)}) async-start(f32[32,2,128]{2,1,0:T(2,128)} %get-tuple-element.7), calls=%async_computation | async-start | bytes 65536 | tf_op jit(solution)/shard_map/all_to_all | solution.py:323
  32.3 9.8 %forecast_1.1._ = f32[32,21,8,128]{3,2,1,0:T(8,128)} custom-call(f32[1,2,8,64,640]{4,3,2,1,0:T(8,128)} %x_ref.3, f32[2,17,640]{2,1,0:T(8,128)} %copy-done.1, f32[2,17,640]{2,1,0:T(8,128)} %copy-done.2, f32[1,2,64,640]{3,2,1,0:T(8,128)} %flux_ref.3, f32[68,640]{1,0:T(8,128)} %fusion.mask_ref, f32[2,8]{1,0:T(2,128)} %diff_ref.3, ...), custom_call_target="tpu_custom_call", output_to_operand_aliasing={{}: (7, {})} | custom-call | flops 40000000 | bytes 3000000 | tf_op jit(solution)/shard_map/forecast_1/pallas_call | solution.py:305
  42.1 0.1 all-to-all-done.seen_ref
  42.2 0.0 copy-start.3
  42.2 0.6 copy-done.3
  42.8 1.9 gram.1
  44.7 9.7 %all-to-all-start.1 = ((f32[32,21,8,128]{3,2,1,0:T(8,128)}), f32[32,21,8,128]{3,2,1,0:T(8,128)S(1)}, u32[]{:S(2)}, u32[]{:S(2)}) async-start(f32[32,21,8,128]{3,2,1,0:T(8,128)} %gram.1), calls=%async_computation.1 | async-start | bytes 5505024 | tf_op jit(solution)/shard_map/all_to_all | solution.py:343
  54.4 1.3 constant_dynamic-slice_fusion.mask_ref
  55.7 65.0 %all-to-all-done.1.gram_ref.data_ref = f32[32,21,8,128]{3,2,1,0:T(8,128)S(1)} async-done(((f32[32,21,8,128]{3,2,1,0:T(8,128)}), f32[32,21,8,128]{3,2,1,0:T(8,128)S(1)}, u32[]{:S(2)}, u32[]{:S(2)}) %all-to-all-start.1) | async-done | bytes 2752544 | tf_op jit(solution)/shard_map/all_to_all | solution.py:343
  120.7 0.0 copy-start
  120.7 1.5 copy-done
  122.3 6.1 %mix.1 = f32[32,20,8,128]{3,2,1,0:T(8,128)} custom-call(f32[32,21,8,128]{3,2,1,0:T(8,128)} %copy-done, f32[32,21,8,128]{3,2,1,0:T(8,128)} %copy-done, f32[2,640]{1,0:T(2,128)} %constant_dynamic-slice_fusion.mask_ref), custom_call_target="tpu_custom_call" | custom-call | tf_op jit(solution)/shard_map/mix/pallas_call | solution.py:346
  128.4 68.8 %all_to_all.15.back_ref = f32[32,20,8,128]{3,2,1,0:T(8,128)} all-to-all(f32[32,20,8,128]{3,2,1,0:T(8,128)} %mix.1), channel_id=1, replica_groups=mesh['member'=32,'domain'=8] {'member'}, dimensions={0} | all-to-all | bytes 5242880 | tf_op jit(solution)/shard_map/all_to_all | solution.py:363
  197.2 6.0 %settle.1 = f32[1,2,8,64,640]{4,3,2,1,0:T(8,128)} custom-call(f32[32,20,8,128]{3,2,1,0:T(8,128)} %all_to_all.15.back_ref), custom_call_target="tpu_custom_call" | custom-call | tf_op jit(solution)/shard_map/settle/pallas_call | solution.py:365
  (4 shorter events, 0.0 us)
Async XLA Ops:
  2.0 7.3 %collective-permute-start = (f32[2,17,640]{2,1,0:T(8,128)S(1)}, f32[2,17,640]{2,1,0:T(8,128)S(1)}, u32[]{:S(2)}, u32[]{:S(2)}) collective-permute-start(f32[2,17,640]{2,1,0:T(8,128)S(1)} %pad_maximum_fusion), channel_id=1, source_target_pairs={{0,1},{1,2},{2,3},{3,4},{4,5},{5,6},{6,7},{8,9},{9,10},{10,11},{11... | collective-permute-start | bytes 261128 | tf_op jit(solution)/shard_map/ppermute | solution.py:263
  3.9 6.1 %collective-permute-start.1 = (f32[2,17,640]{2,1,0:T(8,128)S(1)}, f32[2,17,640]{2,1,0:T(8,128)S(1)}, u32[]{:S(2)}, u32[]{:S(2)}) collective-permute-start(f32[2,17,640]{2,1,0:T(8,128)S(1)} %pad_maximum_fusion.1), channel_id=1, source_target_pairs={{1,0},{2,1},{3,2},{4,3},{5,4},{6,5},{7,6},{9,8},{10,9},{11,10},{12... | collective-permute-start | bytes 261128 | tf_op jit(solution)/shard_map/ppermute | solution.py:264
  9.2 0.8 copy-start.1
  10.0 0.7 copy-start.2
  20.9 21.2 %all-to-all-start = ((f32[32,2,128]{2,1,0:T(2,128)}), f32[32,2,128]{2,1,0:T(2,128)S(1)}, u32[]{:S(2)}, u32[]{:S(2)}) async-start(f32[32,2,128]{2,1,0:T(2,128)} %get-tuple-element.7), calls=%async_computation | async-start | bytes 65536 | tf_op jit(solution)/shard_map/all_to_all | solution.py:323
  42.2 0.6 copy-start.3
  44.7 76.0 %all-to-all-start.1 = ((f32[32,21,8,128]{3,2,1,0:T(8,128)}), f32[32,21,8,128]{3,2,1,0:T(8,128)S(1)}, u32[]{:S(2)}, u32[]{:S(2)}) async-start(f32[32,21,8,128]{3,2,1,0:T(8,128)} %gram.1), calls=%async_computation.1 | async-start | bytes 5505024 | tf_op jit(solution)/shard_map/all_to_all | solution.py:343
  120.7 1.5 copy-start

commit v2 on v1

--- a/solution.py
+++ b/solution.py
@@ -11,6 +11,7 @@
 LEVELS = 8
 LANES = 128
 HALO = 2
+UNROLL = 6
 
 
 def stencil_rows(src, dst, first, last, field, mask, crowd, flux, coef):
@@ -33,15 +34,15 @@
         dst(r, x + sea * change)
         return 0
 
-    lax.fori_loop(first, last, row, 0, unroll=2)
+    lax.fori_loop(first, last, row, 0, unroll=UNROLL)
 
 
 def forecast_kernel(field, x_ref, before_ref, after_ref, flux_ref, mask_ref, diff_ref, mix_ref,
                     *rest):
     if field == 0:
-        index_ref, out_ref, observed_ref, now, later, crowd, flux, surface = rest
+        index_ref, out_ref, observed_ref, now, later, crowd, flux, packed, sems, surface = rest
     else:
-        _, out_ref, now, later, crowd, flux = rest
+        _, out_ref, now, later, crowd, flux, packed, sems = rest
     rows, width = x_ref.shape[3], x_ref.shape[4]
     tall = rows + 2 * HALO
     blocks = width // LANES
@@ -63,7 +64,7 @@
         + pltpu.roll(sea, 1, 1) + pltpu.roll(sea, width - 1, 1)
     )
     flux[0:1, :] = before_ref[field, HALO * LEVELS : HALO * LEVELS + 1, :]
-    flux[1 : rows + 1, :] = flux_ref[0, 0]
+    flux[1 : rows + 1, :] = flux_ref[0, field]
     flux[rows + 1 : rows + 2, :] = after_ref[field, HALO * LEVELS : HALO * LEVELS + 1, :]
     for h in range(HALO):
         now[h] = before_ref[field, h * LEVELS : (h + 1) * LEVELS, :]
@@ -71,7 +72,7 @@
 
     def turn(b, _):
         start = pl.multiple_of(b * 8, 8)
-        now[pl.ds(HALO + start, 8)] = jnp.swapaxes(x_ref[0, 0, :, pl.ds(start, 8), :], 0, 1)
+        now[pl.ds(HALO + start, 8)] = jnp.swapaxes(x_ref[0, field, :, pl.ds(start, 8), :], 0, 1)
         return 0
 
     lax.fori_loop(0, rows // 8, turn, 0)
@@ -86,11 +87,24 @@
         tile = row // 2
         side = row % 2
         for j in range(blocks):
-            out_ref[tile, side * blocks + j] = value[:, j * LANES : (j + 1) * LANES]
+            packed[tile, side * blocks + j] = value[:, j * LANES : (j + 1) * LANES]
         if field == 0:
             surface[side, pl.ds(tile, 1), :] = value[0:1, :]
 
-    stencil_rows(later, emit, HALO, HALO + rows, field, mask_ref, crowd, flux, coef)
+    groups = sems.shape[0]
+    share = rows // groups
+    copies = []
+    for g in range(groups):
+        first = HALO + g * share
+        stencil_rows(later, emit, first, first + share, field, mask_ref, crowd, flux, coef)
+        part = pl.ds(g * share // 2, share // 2)
+        copy = pltpu.make_async_copy(
+            packed.at[part],
+            out_ref.at[part, pl.ds(field * 2 * blocks, 2 * blocks)],
+            sems.at[g],
+        )
+        copy.start()
+        copies.append(copy)
 
     if field == 0:
         tiles = rows // 2
@@ -106,9 +120,11 @@
                     taken = jnp.take_along_axis(source, lane, axis=1, mode="promise_in_bounds")
                     found = jnp.where(block == q, taken, found)
                 observed_ref[g * 8 : (g + 1) * 8, h, :] = found
-
-
-def gram_kernel(tile_ref, seen_ref, value_ref, error_ref, count_ref, _, out_ref):
+    for copy in copies:
+        copy.wait()
+
+
+def gram_kernel(tile_ref, seen_ref, value_ref, error_ref, count_ref, _, out_ref, spread, sem):
     tile = tile_ref[0]
     halves = seen_ref.shape[1]
     members = seen_ref.shape[0]
@@ -137,7 +153,10 @@
     corner = (lane >= 16) & (lane < 32)
     packed = jnp.where(corner & (row == 0), pltpu.roll(pull, 16, 1), packed)
     packed = jnp.where(corner & (row == 1), pull, packed)
-    out_ref[...] = jnp.broadcast_to(packed[None, None], out_ref.shape)
+    spread[...] = jnp.broadcast_to(packed[None, None], spread.shape)
+    copy = pltpu.make_async_copy(spread, out_ref.at[:, pl.ds(out_ref.shape[1] - 1, 1)], sem)
+    copy.start()
+    copy.wait()
 
 
 def ensemble_kernel(packed, wide):
@@ -183,52 +202,63 @@
     return jnp.where(live, weights - centre + 1.0 / count, 0.0)
 
 
-def mix_kernel(gram_ref, data_ref, mask_ref, out_ref, high, low):
-    members, blocks = data_ref.shape[0], data_ref.shape[1]
+def mix_kernel(data_ref, mask_ref, out_ref, high, low):
+    members, slabs = data_ref.shape[0], data_ref.shape[1]
+    blocks = mask_ref.shape[1] // LANES
     deep = members * LEVELS
 
-    @pl.when(pl.program_id(0) == 0)
-    def _():
-        kernel = ensemble_kernel(jnp.sum(gram_ref[:, 0], axis=0), LANES)[:, :members]
-        major = kernel.astype(jnp.bfloat16)
-        minor = (kernel - major.astype(jnp.float32)).astype(jnp.bfloat16)
-        spread = (
-            lax.broadcasted_iota(jnp.int32, (deep, members), 0) // LEVELS
-            == lax.broadcasted_iota(jnp.int32, (deep, members), 1)
-        ).astype(jnp.bfloat16)
-        same = (
-            lax.broadcasted_iota(jnp.int32, (deep, deep), 0) % LEVELS
-            == lax.broadcasted_iota(jnp.int32, (deep, deep), 1) % LEVELS
+    kernel = ensemble_kernel(jnp.sum(data_ref[:, slabs - 1], axis=0), LANES)[:, :members]
+    major = kernel.astype(jnp.bfloat16)
+    minor = (kernel - major.astype(jnp.float32)).astype(jnp.bfloat16)
+    spread = (
+        lax.broadcasted_iota(jnp.int32, (deep, members), 0) // LEVELS
+        == lax.broadcasted_iota(jnp.int32, (deep, members), 1)
+    ).astype(jnp.bfloat16)
+    same = (
+        lax.broadcasted_iota(jnp.int32, (deep, deep), 0) % LEVELS
+        == lax.broadcasted_iota(jnp.int32, (deep, deep), 1) % LEVELS
+    )
+    for part, target in ((major, high), (minor, low)):
+        tall = jnp.dot(spread, part, preferred_element_type=jnp.float32).astype(jnp.bfloat16)
+        full = lax.dot_general(
+            tall, spread, (((1,), (1,)), ((), ())), preferred_element_type=jnp.float32
         )
-        for part, target in ((major, high), (minor, low)):
-            tall = jnp.dot(spread, part, preferred_element_type=jnp.float32).astype(jnp.bfloat16)
-            full = lax.dot_general(
-                tall, spread, (((1,), (1,)), ((), ())), preferred_element_type=jnp.float32
+        target[...] = jnp.where(same, full, 0.0).astype(jnp.bfloat16)
+
+    def strip(i, _):
+        first = i * blocks
+        data = jnp.concatenate(
+            [data_ref[:, first + b].reshape(deep, LANES) for b in range(blocks)], axis=1
+        )
+        major = data.astype(jnp.bfloat16)
+        minor = (data - major.astype(jnp.float32)).astype(jnp.bfloat16)
+        mixed = jnp.dot(high[...], major, preferred_element_type=jnp.float32)
+        mixed = mixed + jnp.dot(high[...], minor, preferred_element_type=jnp.float32)
+        mixed = mixed + jnp.dot(low[...], major, preferred_element_type=jnp.float32)
+        ocean = mask_ref[pl.ds(i % 2, 1), :] > 0.0
+        mixed = jnp.where(ocean, mixed, data)
+        for b in range(blocks):
+            out_ref[:, first + b] = mixed[:, b * LANES : (b + 1) * LANES].reshape(
+                members, LEVELS, LANES
             )
-            target[...] = jnp.where(same, full, 0.0).astype(jnp.bfloat16)
-
-    data = jnp.concatenate([data_ref[:, b].reshape(deep, LANES) for b in range(blocks)], axis=1)
-    major = data.astype(jnp.bfloat16)
-    minor = (data - major.astype(jnp.float32)).astype(jnp.bfloat16)
-    mixed = jnp.dot(high[...], major, preferred_element_type=jnp.float32)
-    mixed = mixed + jnp.dot(high[...], minor, preferred_element_type=jnp.float32)
-    mixed = mixed + jnp.dot(low[...], major, preferred_element_type=jnp.float32)
-    ocean = mask_ref[pl.ds(pl.program_id(0) % 2, 1), :] > 0.0
-    mixed = jnp.where(ocean, mixed, data)
-    for b in range(blocks):
-        out_ref[:, b] = mixed[:, b * LANES : (b + 1) * LANES].reshape(members, LEVELS, LANES)
+        return 0
+
+    lax.fori_loop(0, FIELDS * 2, strip, 0)
 
 
 def settle_kernel(back_ref, out_ref):
     blocks = out_ref.shape[4] // LANES
+    share = out_ref.shape[3] // 2
+    first = pl.program_id(0) * share
     for f in range(FIELDS):
         for j in range(blocks):
-            rows = []
-            for t in range(4):
-                for s in range(2):
-                    rows.append(back_ref[t, (f * 2 + s) * blocks + j])
-            turned = jnp.swapaxes(jnp.stack(rows, axis=0), 0, 1)
-            out_ref[0, f, :, :, j * LANES : (j + 1) * LANES] = turned
+            for half in range(share // 4):
+                rows = []
+                for t in range(4):
+                    for s in range(2):
+                        rows.append(back_ref[first + half * 4 + t, (f * 2 + s) * blocks + j])
+                turned = jnp.swapaxes(jnp.stack(rows, axis=0), 0, 1)
+                out_ref[0, f, :, half * 8 : (half + 1) * 8, j * LANES : (j + 1) * LANES] = turned
 
 
 def shards(
@@ -271,45 +301,40 @@
     tall = rows + 2 * HALO
     bulk = jax.ShapeDtypeStruct((tiles, slabs, levels, LANES), f32)
 
-    def whole(*shape):
-        return pl.BlockSpec(shape, lambda i: (0,) * len(shape))
+    vmem = pl.BlockSpec(memory_space=pltpu.VMEM)
+    smem = pl.BlockSpec(memory_space=pltpu.SMEM)
+    anywhere = pl.BlockSpec(memory_space=pl.ANY)
 
     def forecast(field, extra):
-        in_specs = [
-            pl.BlockSpec((1, 1, levels, rows, width), lambda i: (0, field, 0, 0, 0)),
-            whole(fields, HALO * levels + 1, width),
-            whole(fields, HALO * levels + 1, width),
-            pl.BlockSpec((1, 1, rows, width), lambda i: (0, field, 0, 0)),
-            whole(tall, width),
-            pl.BlockSpec(memory_space=pltpu.SMEM),
-            pl.BlockSpec(memory_space=pltpu.SMEM),
-        ]
+        in_specs = [vmem] * 5 + [smem] * 2
         out_shape = [bulk]
-        out_specs = [pl.BlockSpec((tiles, per_field, levels, LANES), lambda i: (0, field, 0, 0))]
+        out_specs = [anywhere]
         scratch = [
             pltpu.VMEM((tall, levels, width), f32),
             pltpu.VMEM((tall, levels, width), f32),
             pltpu.VMEM((tall, width), f32),
             pltpu.VMEM((rows + 2, width), f32),
+            pltpu.VMEM((tiles, per_field, levels, LANES), f32),
+            pltpu.SemaphoreType.DMA((4,)),
         ]
         alias = {}
         if field == 0:
-            in_specs.append(whole(*obs_index.shape))
+            in_specs.append(vmem)
             slots = obs_index.shape[2]
             out_shape.append(jax.ShapeDtypeStruct((tiles, slots // LANES, LANES), f32))
-            out_specs.append(whole(tiles, slots // LANES, LANES))
+            out_specs.append(vmem)
             scratch.append(pltpu.VMEM((2, tiles, width), f32))
         else:
-            in_specs.append(pl.BlockSpec(memory_space=pl.ANY))
+            in_specs.append(anywhere)
             alias = {7: 0}
         return pl.pallas_call(
             functools.partial(forecast_kernel, field),
-            grid=(1,),
             out_shape=out_shape,
             in_specs=in_specs,
             out_specs=out_specs,
             scratch_shapes=scratch,
             input_output_aliases=alias,
+            compiler_params=pltpu.CompilerParams(vmem_limit_bytes=16 << 20),
             cost_estimate=pl.CostEstimate(
                 flops=40_000_000, bytes_accessed=3_000_000, transcendentals=0
             ),
@@ -325,18 +350,15 @@
 
     sent = pl.pallas_call(
         gram_kernel,
-        grid=(1,),
         out_shape=bulk,
-        in_specs=[
-            pl.BlockSpec(memory_space=pltpu.SMEM),
-            whole(*seen.shape),
-            whole(*obs_value.shape),
-            whole(*obs_error.shape),
-            pl.BlockSpec(memory_space=pltpu.SMEM),
-            pl.BlockSpec(memory_space=pl.ANY),
+        in_specs=[smem, vmem, vmem, vmem, smem, anywhere],
+        out_specs=anywhere,
+        scratch_shapes=[
+            pltpu.VMEM((tiles, 1, levels, LANES), f32),
+            pltpu.SemaphoreType.DMA,
         ],
-        out_specs=pl.BlockSpec((tiles, 1, levels, LANES), lambda i: (0, slabs - 1, 0, 0)),
         input_output_aliases={5: 0},
+        compiler_params=pltpu.CompilerParams(vmem_limit_bytes=8 << 20),
         name="gram",
     )(tile.reshape(1).astype(jnp.int32), seen, obs_value, obs_error, obs_count, sent)
 
@@ -345,29 +367,26 @@
     deep = members * levels
     updated = pl.pallas_call(
         mix_kernel,
-        grid=(fields * 2,),
         out_shape=jax.ShapeDtypeStruct((members, slabs - 1, levels, LANES), f32),
-        in_specs=[
-            pl.BlockSpec((members, 1, levels, LANES), lambda i: (0, slabs - 1, 0, 0)),
-            pl.BlockSpec((members, blocks, levels, LANES), lambda i: (0, i, 0, 0)),
-            whole(2, width),
-        ],
-        out_specs=pl.BlockSpec((members, blocks, levels, LANES), lambda i: (0, i, 0, 0)),
+        in_specs=[vmem, vmem],
+        out_specs=vmem,
         scratch_shapes=[
             pltpu.VMEM((deep, deep), jnp.bfloat16),
             pltpu.VMEM((deep, deep), jnp.bfloat16),
         ],
+        compiler_params=pltpu.CompilerParams(vmem_limit_bytes=16 << 20),
         name="mix",
-    )(held, held, tile_mask)
+    )(held, tile_mask)
 
     back = lax.all_to_all(updated, "member", split_axis=0, concat_axis=0, tiled=True)
 
     return pl.pallas_call(
         settle_kernel,
-        grid=(rows // 8,),
+        grid=(rows // 16,),
         out_shape=jax.ShapeDtypeStruct(starting_tracer_fields.shape, f32),
-        in_specs=[pl.BlockSpec((4, slabs - 1, levels, LANES), lambda i: (i, 0, 0, 0))],
-        out_specs=pl.BlockSpec((1, fields, levels, 8, width), lambda i: (0, 0, 0, i, 0)),
+        in_specs=[vmem],
+        out_specs=pl.BlockSpec((1, fields, levels, 16, width), lambda i: (0, 0, 0, i, 0)),
+        compiler_params=pltpu.CompilerParams(vmem_limit_bytes=16 << 20),
         name="settle",
     )(back)
 

time: 205 us -> 191 us (0.932)
  Pallas kernels: 34.1 us -> 20.2 us
  waiting for transfers between devices: 65.9 us -> 71.4 us
  starting transfers between devices: 26.6 us -> 23.1 us
    pallas_call x5, Pallas kernels: 34.1 us -> 20.2 us  [the longest x2 13.3 us: forecast(): pl.pallas_call(functools.partial(forecast_kernel, field), out_shape=out_s...]
    all_to_all x1, waiting for transfers between devices: 0.1 us -> 3.65 us  [shards(): lax.all_to_all(observed, 'member', split_axis=0, concat_axis=0, tiled=True)]
    all_to_all x1, starting transfers between devices: 9.69 us -> 6.18 us  [shards(): lax.all_to_all(sent, 'member', split_axis=0, concat_axis=0, tiled=True)]
  transfers between devices with their start and end apart: 4 -> 4, of which waited for: 3 -> 3; matrix products, arithmetic and copies ran while one was open for 1% -> 1% of each run, Pallas kernels for 5% -> 3%
where the time goes in v2:
time: 191 us; the launch traced here: 189 us
  waiting for transfers between devices  71.4 us (37%)
  blocking collectives  68.4 us (36%)
  starting transfers between devices  23.1 us (12%)
  Pallas kernels  20.2 us (11%)
  local copies, waits for them, and re-layouts  5.14 us (3%)
    all_to_all x1, blocking collectives, shards(): lax.all_to_all(updated, 'member', split_axis=0, concat_axis=0, tiled=True)  68.4 us
    all_to_all x1, waiting for transfers between devices, shards(): lax.all_to_all(sent, 'member', split_axis=0, concat_axis=0, tiled=True)  66.3 us
    pallas_call x2, Pallas kernels, forecast(): pl.pallas_call(functools.partial(forecast_kernel, field), out_shape=out_s...  13.3 us
    all_to_all x1, starting transfers between devices, shards(): lax.all_to_all(observed, 'member', split_axis=0, concat_axis=0, tiled=True)  11.3 us
    all_to_all x1, starting transfers between devices, shards(): lax.all_to_all(sent, 'member', split_axis=0, concat_axis=0, tiled=True)  6.18 us
  transfers between devices with their start and end apart: 4, of which 3 were waited for; matrix products, arithmetic and copies ran while one was open for 1% of the time, Pallas kernels for 3%

profile of v2, /device:TPU:8, one launch (start us, length us, event | category | flops | bytes accessed | tf_op | source)
XLA Modules:
  0.0 189.3 jit_solution(6514171260104998960)
XLA Ops:
  0.0 0.0 copy-start.2
  0.0 0.0 copy-start.3
  0.0 0.9 fusion.1
  0.9 1.1 slice_bitcast_fusion
  2.0 1.9 %collective-permute-start = (f32[2,17,640]{2,1,0:T(8,128)S(1)}, f32[2,17,640]{2,1,0:T(8,128)S(1)}, u32[]{:S(2)}, u32[]{:S(2)}) collective-permute-start(f32[2,17,640]{2,1,0:T(8,128)S(1)} %pad_maximum_fusion), channel_id=1, source_target_pairs={{0,1},{1,2},{2,3},{3,4},{4,5},{5,6},{6,7},{8,9},{9,10},{10,11},{11... | collective-permute-start | bytes 261128 | tf_op jit(solution)/shard_map/ppermute | solution.py:293
  4.0 3.6 %collective-permute-start.1 = (f32[2,17,640]{2,1,0:T(8,128)S(1)}, f32[2,17,640]{2,1,0:T(8,128)S(1)}, u32[]{:S(2)}, u32[]{:S(2)}) collective-permute-start(f32[2,17,640]{2,1,0:T(8,128)S(1)} %pad_maximum_fusion.1), channel_id=1, source_target_pairs={{1,0},{2,1},{3,2},{4,3},{5,4},{6,5},{7,6},{9,8},{10,9},{11,10},{12... | collective-permute-start | bytes 261128 | tf_op jit(solution)/shard_map/ppermute | solution.py:294
  7.7 1.0 fusion.mask_ref
  8.6 0.0 collective-permute-done.before_ref
  8.6 1.4 collective-permute-done.1.after_ref
  10.1 0.0 copy-done.2
  10.1 0.0 copy-done.3
  10.1 0.0 copy-start
  10.1 1.7 copy-done
  11.8 0.0 copy-start.6
  11.8 0.7 copy-done.6
  12.5 0.0 copy-start.7
  12.5 0.7 copy-done.7
  13.2 0.0 copy-start.1
  13.2 7.0 %forecast_0.1 = (f32[32,21,8,128]{3,2,1,0:T(8,128)}, f32[32,2,128]{2,1,0:T(2,128)}) custom-call(f32[1,2,8,64,640]{4,3,2,1,0:T(8,128)S(1)} %copy-done, f32[2,17,640]{2,1,0:T(8,128)S(1)} %collective-permute-done.before_ref, f32[2,17,640]{2,1,0:T(8,128)S(1)} %collective-permute-done.1.after_ref, f32[1,2,64,640]{3,2,1,0:T(8,128)S(1)} %copy-done.2, ...), custom_call_target="tpu_custom_call" | custom-call | flops 40000000 | bytes 3000000 | tf_op jit(solution)/shard_map/forecast_0/pallas_call | solution.py:330
  20.2 11.3 %all-to-all-start = ((f32[32,2,128]{2,1,0:T(2,128)}), f32[32,2,128]{2,1,0:T(2,128)S(1)}, u32[]{:S(2)}, u32[]{:S(2)}) async-start(f32[32,2,128]{2,1,0:T(2,128)} %get-tuple-element.7), calls=%async_computation | async-start | bytes 65536 | tf_op jit(solution)/shard_map/all_to_all | solution.py:348
  31.6 0.0 copy-done.1
  31.6 0.0 copy-start.4
  31.6 0.0 copy-start.5
  31.6 0.0 copy-start.8
  31.6 6.2 %forecast_1.1._ = f32[32,21,8,128]{3,2,1,0:T(8,128)} custom-call(f32[1,2,8,64,640]{4,3,2,1,0:T(8,128)S(1)} %copy-done.1, f32[2,17,640]{2,1,0:T(8,128)S(1)} %collective-permute-done.before_ref, f32[2,17,640]{2,1,0:T(8,128)S(1)} %collective-permute-done.1.after_ref, f32[1,2,64,640]{3,2,1,0:T(8,128)S(1)} %copy-done.2, ...), custom_call_target="tpu_custom_call", output_to_operand_aliasing={{}: (7, {})} | custom-call | flops 40000000 | bytes 3000000 | tf_op jit(solution)/shard_map/forecast_1/pallas_call | solution.py:330
  37.8 3.6 %all-to-all-done.seen_ref = f32[32,2,128]{2,1,0:T(2,128)S(1)} async-done(((f32[32,2,128]{2,1,0:T(2,128)}), f32[32,2,128]{2,1,0:T(2,128)S(1)}, u32[]{:S(2)}, u32[]{:S(2)}) %all-to-all-start) | async-done | bytes 32800 | tf_op jit(solution)/shard_map/all_to_all | solution.py:348
  41.5 0.0 copy-done.4
  41.5 0.0 copy-done.5
  41.5 0.0 copy-done.8
  41.5 1.6 gram.1
  43.1 6.2 %all-to-all-start.1 = ((f32[32,21,8,128]{3,2,1,0:T(8,128)}), f32[32,21,8,128]{3,2,1,0:T(8,128)S(1)}, u32[]{:S(2)}, u32[]{:S(2)}) async-start(f32[32,21,8,128]{3,2,1,0:T(8,128)} %gram.1), calls=%async_computation.1 | async-start | bytes 5505024 | tf_op jit(solution)/shard_map/all_to_all | solution.py:365
  49.3 66.3 %all-to-all-done.1.data_ref = f32[32,21,8,128]{3,2,1,0:T(8,128)S(1)} async-done(((f32[32,21,8,128]{3,2,1,0:T(8,128)}), f32[32,21,8,128]{3,2,1,0:T(8,128)S(1)}, u32[]{:S(2)}, u32[]{:S(2)}) %all-to-all-start.1) | async-done | bytes 2752544 | tf_op jit(solution)/shard_map/all_to_all | solution.py:365
  115.6 3.2 %mix.1 = f32[32,20,8,128]{3,2,1,0:T(8,128)S(1)} custom-call(f32[32,21,8,128]{3,2,1,0:T(8,128)S(1)} %all-to-all-done.1.data_ref, f32[2,640]{1,0:T(2,128)S(1)} %constant_dynamic-slice_fusion.mask_ref), custom_call_target="tpu_custom_call" | custom-call | tf_op jit(solution)/shard_map/mix/pallas_call | solution.py:368
  118.8 68.4 %all_to_all.15.back_ref = f32[32,20,8,128]{3,2,1,0:T(8,128)S(1)} all-to-all(f32[32,20,8,128]{3,2,1,0:T(8,128)S(1)} %mix.1), channel_id=1, replica_groups=mesh['member'=32,'domain'=8] {'member'}, dimensions={0} | all-to-all | bytes 5242880 | tf_op jit(solution)/shard_map/all_to_all | solution.py:381
  187.2 2.1 %settle.1 = f32[1,2,8,64,640]{4,3,2,1,0:T(8,128)} custom-call(f32[32,20,8,128]{3,2,1,0:T(8,128)S(1)} %all_to_all.15.back_ref), custom_call_target="tpu_custom_call" | custom-call | tf_op jit(solution)/shard_map/settle/pallas_call | solution.py:383
  (5 shorter events, 0.1 us)
Async XLA Ops:
  0.0 10.1 %copy-start.2 = (f32[1,2,64,640]{3,2,1,0:T(8,128)S(1)}, f32[1,2,64,640]{3,2,1,0:T(8,128)}, u32[]{:S(2)}) copy-start(f32[1,2,64,640]{3,2,1,0:T(8,128)} %flux_ref.3) | copy-start | bytes 983044
  0.0 10.1 %copy-start.3 = (s32[1,32,256]{2,1,0:T(8,128)S(1)}, s32[1,32,256]{2,1,0:T(8,128)}, u32[]{:S(2)}) copy-start(s32[1,32,256]{2,1,0:T(8,128)} %rest_0_.1) | copy-start | bytes 98308
  2.0 6.6 %collective-permute-start = (f32[2,17,640]{2,1,0:T(8,128)S(1)}, f32[2,17,640]{2,1,0:T(8,128)S(1)}, u32[]{:S(2)}, u32[]{:S(2)}) collective-permute-start(f32[2,17,640]{2,1,0:T(8,128)S(1)} %pad_maximum_fusion), channel_id=1, source_target_pairs={{0,1},{1,2},{2,3},{3,4},{4,5},{5,6},{6,7},{8,9},{9,10},{10,11},{11... | collective-permute-start | bytes 261128 | tf_op jit(solution)/shard_map/ppermute | solution.py:293
  4.0 6.1 %collective-permute-start.1 = (f32[2,17,640]{2,1,0:T(8,128)S(1)}, f32[2,17,640]{2,1,0:T(8,128)S(1)}, u32[]{:S(2)}, u32[]{:S(2)}) collective-permute-start(f32[2,17,640]{2,1,0:T(8,128)S(1)} %pad_maximum_fusion.1), channel_id=1, source_target_pairs={{1,0},{2,1},{3,2},{4,3},{5,4},{6,5},{7,6},{9,8},{10,9},{11,10},{12... | collective-permute-start | bytes 261128 | tf_op jit(solution)/shard_map/ppermute | solution.py:294
  10.1 1.7 copy-start
  11.8 0.7 copy-start.6
  12.5 0.7 copy-start.7
  13.2 18.4 %copy-start.1 = (f32[1,2,8,64,640]{4,3,2,1,0:T(8,128)S(1)}, f32[1,2,8,64,640]{4,3,2,1,0:T(8,128)}, u32[]{:S(2)}) copy-start(f32[1,2,8,64,640]{4,3,2,1,0:T(8,128)} %x_ref.3) | copy-start | bytes 7864324
  20.2 21.3 %all-to-all-start = ((f32[32,2,128]{2,1,0:T(2,128)}), f32[32,2,128]{2,1,0:T(2,128)S(1)}, u32[]{:S(2)}, u32[]{:S(2)}) async-start(f32[32,2,128]{2,1,0:T(2,128)} %get-tuple-element.7), calls=%async_computation | async-start | bytes 65536 | tf_op jit(solution)/shard_map/all_to_all | solution.py:348
  31.6 9.9 %copy-start.4 = (f32[1,32,256]{2,1,0:T(8,128)S(1)}, f32[1,32,256]{2,1,0:T(8,128)}, u32[]{:S(2)}) copy-start(f32[1,32,256]{2,1,0:T(8,128)} %value_ref.1) | copy-start | bytes 98308
  31.6 9.9 %copy-start.5 = (f32[1,32,256]{2,1,0:T(8,128)S(1)}, f32[1,32,256]{2,1,0:T(8,128)}, u32[]{:S(2)}) copy-start(f32[1,32,256]{2,1,0:T(8,128)} %error_ref.1) | copy-start | bytes 98308
  31.6 9.9 %copy-start.8 = (s32[1,32]{1,0:T(1,128)S(1)}, s32[1,32]{1,0:T(1,128)}, u32[]{:S(2)}) copy-start(s32[1,32]{1,0:T(1,128)} %count_ref.1) | copy-start | bytes 388
  43.1 72.5 %all-to-all-start.1 = ((f32[32,21,8,128]{3,2,1,0:T(8,128)}), f32[32,21,8,128]{3,2,1,0:T(8,128)S(1)}, u32[]{:S(2)}, u32[]{:S(2)}) async-start(f32[32,21,8,128]{3,2,1,0:T(8,128)} %gram.1), calls=%async_computation.1 | async-start | bytes 5505024 | tf_op jit(solution)/shard_map/all_to_all | solution.py:365

commit v3 on v2

v3 whole, which is shorter than its diff:
```python
import functools

import jax
import jax.numpy as jnp
from jax import lax
from jax.experimental import pallas as pl
from jax.experimental.pallas import tpu as pltpu
from jax.sharding import PartitionSpec as P

FIELDS = 2
LEVELS = 8
LANES = 128
HALO = 2
UNROLL = 10


def spread_row(row):
    return jnp.broadcast_to(row, (LEVELS, row.shape[1]))


def prepare_kernel(field, x_ref, flux_ref, mask_ref, *rest):
    turned, wet, source, sea8, crowd8, held, sems = rest[-7:]
    rows, width = turned.shape[0], turned.shape[2]
    tall = rows + 2 * HALO
    parts = rows // 8
    copies = []
    for p in range(parts):
        span = pl.ds(p * 8, 8)
        copy = pltpu.make_async_copy(
            x_ref.at[0, field, :, span, :], held.at[:, span, :], sems.at[p]
        )
        copy.start()
        copies.append(copy)
    sea = mask_ref[1 : tall - 1, :]
    crowd = (
        mask_ref[0 : tall - 2, :] + mask_ref[2:tall, :]
        + pltpu.roll(sea, 1, 1) + pltpu.roll(sea, width - 1, 1)
    )
    for r in range(tall):
        sea8[r] = spread_row(mask_ref[r : r + 1, :])
    for r in range(1, tall - 1):
        crowd8[r] = spread_row(crowd[r - 1 : r, :])
    top = lax.broadcasted_iota(jnp.int32, (LEVELS, width), 0) == 0
    for p in range(parts):
        copies[p].wait()
        start = p * 8
        flipped = jnp.swapaxes(held[:, start : start + 8, :], 0, 1)
        for k in range(8):
            r = start + k
            turned[r] = flipped[k]
            wet[r] = flipped[k] * sea8[r + HALO]
            source[r] = jnp.where(top, spread_row(flux_ref[0, field, r : r + 1, :]), 0.0)


def forecast_kernel(field, turned, wet, source, sea8, crowd8, before_ref, after_ref,
                    diff_ref, mix_ref, *rest):
    if field == 0:
        index_ref, out_ref, done_ref, first, moist, packed, sems, surface = rest
        done_ref[...] = jnp.zeros_like(done_ref)
    else:
        out_ref, first, moist, packed, sems = rest
    rows, width = turned.shape[0], turned.shape[2]
    tall = rows + 2 * HALO
    blocks = width // LANES

    level = lax.broadcasted_iota(jnp.int32, (LEVELS, LEVELS), 0)
    lane = lax.broadcasted_iota(jnp.int32, (LEVELS, LEVELS), 1)
    diff = diff_ref[field : field + 1, :]
    mix = jnp.concatenate([mix_ref[field : field + 1, :], jnp.zeros((1, 1), jnp.float32)], axis=1)

    def along(table, shift):
        column = jnp.sum(jnp.where(lane + shift == level, table, 0.0), axis=1, keepdims=True)
        return jnp.concatenate([jnp.broadcast_to(column, (LEVELS, LANES))] * blocks, axis=1)

    lateral, above, below = along(diff, 0), along(mix, 0), along(mix, 1)
    vertical = above + below

    def stepped(r, x, y, north, south, gain):
        sea = sea8[r]
        around = north + south + pltpu.roll(y, 1, 1) + pltpu.roll(y, width - 1, 1)
        change = lateral * (around - crowd8[r] * x) - vertical * x + gain
        change = change + above * pltpu.roll(x, LEVELS - 1, 0)
        change = change + below * pltpu.roll(x, 1, 0)
        return x + sea * change

    def near(r):
        if r < HALO:
            x = before_ref[field, r * LEVELS : (r + 1) * LEVELS, :]
        elif r >= HALO + rows:
            h = r - HALO - rows
            x = after_ref[field, h * LEVELS : (h + 1) * LEVELS, :]
        else:
            return turned[r - HALO], wet[r - HALO]
        return x, x * sea8[r]

    top = lax.broadcasted_iota(jnp.int32, (LEVELS, width), 0) == 0

    def gain_at(r):
        if HALO <= r < HALO + rows:
            return source[r - HALO]
        ref = before_ref if r < HALO else after_ref
        line = ref[field, HALO * LEVELS : HALO * LEVELS + 1, :]
        return jnp.where(top, spread_row(line), 0.0)

    def keep(r, value):
        first[r] = value
        moist[r] = value * sea8[r]

    def inner(r, _):
        i = r - HALO
        keep(r, stepped(r, turned[i], wet[i], wet[i - 1], wet[i + 1], source[i]))
        return 0

    body = (tall - 6) // UNROLL * UNROLL
    for r in (1, 2, *range(3 + body, tall - 1)):
        x, y = near(r)
        keep(r, stepped(r, x, y, near(r - 1)[1], near(r + 1)[1], gain_at(r)))
    lax.fori_loop(3, 3 + body, inner, 0, unroll=UNROLL)

    def outer(tile, _):
        for side in range(2):
            r = HALO + 2 * tile + side
            value = stepped(r, first[r], moist[r], moist[r - 1], moist[r + 1], source[r - HALO])
            for j in range(blocks):
                packed[tile, side * blocks + j] = value[:, j * LANES : (j + 1) * LANES]
            if field == 0:
                surface[side, pl.ds(tile, 1), :] = value[0:1, :]
        return 0

    tiles = rows // 2
    groups = 4
    share = tiles // groups
    copies = []
    for g in range(groups):
        lax.fori_loop(g * share, (g + 1) * share, outer, 0, unroll=4)
        part = (pl.ds(g * share, share), pl.ds(0, 2 * blocks))
        copies.append(pltpu.make_async_copy(packed.at[part], out_ref.at[part], sems.at[g]))
        copies[-1].start()

    if field == 0:
        slots = index_ref.shape[2]
        for g in range(tiles // 8):
            for h in range(slots // LANES):
                where = index_ref[0, g * 8 : (g + 1) * 8, h * LANES : (h + 1) * LANES]
                block, lanes = where >> 7, where & (LANES - 1)
                found = jnp.zeros((8, LANES), jnp.float32)
                for q in range(2 * blocks):
                    s, j = divmod(q, blocks)
                    piece = surface[s, g * 8 : (g + 1) * 8, j * LANES : (j + 1) * LANES]
                    taken = jnp.take_along_axis(piece, lanes, axis=1, mode="promise_in_bounds")
                    found = jnp.where(block == q, taken, found)
                packed[g * 8 : (g + 1) * 8, 2 * blocks, h, :] = found
        part = (slice(None), pl.ds(2 * blocks, 1))
        copies.append(pltpu.make_async_copy(packed.at[part], out_ref.at[part], sems.at[groups]))
        copies[-1].start()
    for copy in copies:
        copy.wait()


def gram_kernel(tile_ref, held_ref, value_ref, error_ref, count_ref, _, out_ref, spread, sem):
    tile = tile_ref[0]
    members, per_field = held_ref.shape[0], held_ref.shape[1] - 1
    halves = value_ref.shape[2] // LANES
    slot = lax.broadcasted_iota(jnp.int32, (1, LANES), 1)
    total = jnp.zeros((members + 8, members), jnp.float32)
    for h in range(halves):
        seen = held_ref[:, per_field, h, :]
        average = jnp.mean(seen, axis=0, keepdims=True)
        anomaly = seen - average
        span = slice(h * LANES, (h + 1) * LANES)
        own = lax.broadcasted_iota(jnp.int32, (value_ref.shape[1], LANES), 0) == tile
        value = jnp.sum(jnp.where(own, value_ref[0, :, span], 0.0), axis=0, keepdims=True)
        error = jnp.sum(jnp.where(own, error_ref[0, :, span], 0.0), axis=0, keepdims=True)
        active = jnp.where(slot + h * LANES < count_ref[0, tile], 1.0, 0.0)
        weight = active / error
        drift = weight * (value - average)
        left = jnp.concatenate([anomaly * weight, jnp.broadcast_to(drift, (8, LANES))], axis=0)
        total = total + lax.dot_general(
            left, anomaly, (((1,), (1,)), ((), ())),
            precision=lax.Precision.HIGHEST, preferred_element_type=jnp.float32,
        )
    packed = jnp.concatenate([total[g * 8 : (g + 1) * 8] for g in range(4)], axis=1)
    pull = jnp.concatenate([total[members : members + 8]] * 4, axis=1)
    row = lax.broadcasted_iota(jnp.int32, packed.shape, 0)
    lane = lax.broadcasted_iota(jnp.int32, packed.shape, 1)
    corner = (lane >= 16) & (lane < 32)
    packed = jnp.where(corner & (row == 0), pltpu.roll(pull, 16, 1), packed)
    packed = jnp.where(corner & (row == 1), pull, packed)
    for m in range(members):
        spread[m, 0] = packed
    copy = pltpu.make_async_copy(spread, out_ref.at[:, pl.ds(per_field, 1)], sem)
    copy.start()
    copy.wait()


def ensemble_kernel(packed, wide):
    count = 32
    lane = lax.broadcasted_iota(jnp.int32, (count, LANES), 1)
    row = lax.broadcasted_iota(jnp.int32, (count, LANES), 0)
    gram = jnp.concatenate(
        [packed if g == 0 else pltpu.roll(packed, LANES - g * count, 1) for g in range(4)], axis=0
    )
    pull = jnp.where(
        lane[0:1] < 16,
        pltpu.roll(packed[0:8], LANES - 16, 1)[0:1],
        packed[1:2],
    )
    gram = gram + jnp.where(lane == row, count - 1.0, 0.0)
    columns = [jnp.broadcast_to(gram[:, k : k + 1], (count, LANES)) for k in range(count)]
    work = jnp.where(lane == row, 1.0, 0.0)
    for k in range(count):
        base = (k // 8) * 8
        column = columns[k][base:]
        pivot = jnp.broadcast_to(column[k - base : k - base + 1], (8, LANES))
        scale = lax.rsqrt(pivot)
        scale = scale * (1.5 - 0.5 * pivot * scale * scale)
        head = scale[0:1]
        lead = work[k : k + 1] * head
        column = column * head
        below = row[base:] > k
        factor = jnp.where(below, column, 0.0)
        rest = jnp.where(row[base:] == k, lead, work[base:] - factor * lead)
        work = rest if base == 0 else jnp.concatenate([work[:base], rest], axis=0)
        for c in range(k + 1, count):
            cbase = (c // 8) * 8
            ratio = column[c - base : c - base + 1]
            old = columns[c]
            fresh = old[cbase:] - column[cbase - base :] * ratio
            columns[c] = fresh if cbase == 0 else jnp.concatenate([old[:cbase], fresh], axis=0)
    inverse = work
    gained = jnp.sum(inverse * pull, axis=1, keepdims=True)
    mean_weight = jnp.sum(inverse * gained, axis=0, keepdims=True)
    live = lane < count
    weights = jnp.where(live, mean_weight + jnp.sqrt(count - 1.0) * inverse, 0.0)
    centre = jnp.sum(weights, axis=1, keepdims=True) * (1.0 / count)
    return jnp.where(live, weights - centre + 1.0 / count, 0.0)


def mix_kernel(data0_ref, data1_ref, mask_ref, out_ref, high, low):
    members, per_field = data0_ref.shape[0], data0_ref.shape[1] - 1
    blocks = mask_ref.shape[1] // LANES
    deep = members * LEVELS

    kernel = ensemble_kernel(jnp.sum(data1_ref[:, per_field], axis=0), LANES)[:, :members]
    major = kernel.astype(jnp.bfloat16)
    minor = (kernel - major.astype(jnp.float32)).astype(jnp.bfloat16)
    spread = (
        lax.broadcasted_iota(jnp.int32, (deep, members), 0) // LEVELS
        == lax.broadcasted_iota(jnp.int32, (deep, members), 1)
    ).astype(jnp.bfloat16)
    same = (
        lax.broadcasted_iota(jnp.int32, (deep, deep), 0) % LEVELS
        == lax.broadcasted_iota(jnp.int32, (deep, deep), 1) % LEVELS
    )
    for part, target in ((major, high), (minor, low)):
        tall = jnp.dot(spread, part, preferred_element_type=jnp.float32).astype(jnp.bfloat16)
        full = lax.dot_general(
            tall, spread, (((1,), (1,)), ((), ())), preferred_element_type=jnp.float32
        )
        target[...] = jnp.where(same, full, 0.0).astype(jnp.bfloat16)

    for f, data_ref in ((0, data0_ref), (1, data1_ref)):

        def strip(i, _, f=f, data_ref=data_ref):
            first = i * blocks
            data = jnp.concatenate(
                [data_ref[:, first + b].reshape(deep, LANES) for b in range(blocks)], axis=1
            )
            major = data.astype(jnp.bfloat16)
            minor = (data - major.astype(jnp.float32)).astype(jnp.bfloat16)
            mixed = jnp.dot(high[...], major, preferred_element_type=jnp.float32)
            mixed = mixed + jnp.dot(high[...], minor, preferred_element_type=jnp.float32)
            mixed = mixed + jnp.dot(low[...], major, preferred_element_type=jnp.float32)
            ocean = mask_ref[pl.ds(i, 1), :] > 0.0
            mixed = jnp.where(ocean, mixed, data)
            for b in range(blocks):
                out_ref[:, f * per_field + first + b] = mixed[
                    :, b * LANES : (b + 1) * LANES
                ].reshape(members, LEVELS, LANES)
            return 0

        lax.fori_loop(0, 2, strip, 0)


def settle_kernel(back_ref, out_ref):
    blocks = out_ref.shape[4] // LANES
    share = out_ref.shape[3] // 2
    first = pl.program_id(0) * share
    for f in range(FIELDS):
        for j in range(blocks):
            for half in range(share // 4):
                rows = []
                for t in range(4):
                    for s in range(2):
                        rows.append(back_ref[first + half * 4 + t, (f * 2 + s) * blocks + j])
                turned = jnp.swapaxes(jnp.stack(rows, axis=0), 0, 1)
                out_ref[0, f, :, half * 8 : (half + 1) * 8, j * LANES : (j + 1) * LANES] = turned


def shards(
    starting_tracer_fields,
    surface_exchange_inputs,
    diffusivity,
    mixing,
    land_mask,
    obs_index,
    obs_count,
    obs_value,
    obs_error,
):
    _, fields, levels, rows, width = starting_tracer_fields.shape
    members = lax.axis_size("member")
    domains = lax.axis_size("domain")
    blocks = width // LANES
    tiles = members
    per_field = 2 * blocks
    tile = lax.axis_index("member")
    domain = lax.axis_index("domain")
    state, flux = starting_tracer_fields[0], surface_exchange_inputs[0]

    def edge(first, flux_row):
        lines = jnp.swapaxes(state[:, :, first : first + HALO], 1, 2)
        lines = lines.reshape(fields, HALO * levels, width)
        return jnp.concatenate([lines, flux[:, flux_row : flux_row + 1]], axis=1)

    up = [(i, i + 1) for i in range(domains - 1)]
    down = [(i + 1, i) for i in range(domains - 1)]
    before = lax.ppermute(edge(rows - HALO, rows - 1), "domain", up)
    after = lax.ppermute(edge(0, 0), "domain", down)

    padded = jnp.pad(land_mask, ((HALO, HALO), (0, 0)))
    mask = lax.dynamic_slice_in_dim(padded, domain * rows, rows + 2 * HALO, 0).astype(jnp.float32)
    tile_mask = lax.dynamic_slice_in_dim(mask, HALO + tile * 2, 2, 0)

    f32 = jnp.float32
    tall = rows + 2 * HALO
    vmem = pl.BlockSpec(memory_space=pltpu.VMEM)
    smem = pl.BlockSpec(memory_space=pltpu.SMEM)
    anywhere = pl.BlockSpec(memory_space=pl.ANY)
    hbm = pl.BlockSpec(memory_space=pltpu.HBM)

    def params(mib):
        return pltpu.CompilerParams(vmem_limit_bytes=mib << 20)

    band = jax.ShapeDtypeStruct((rows, levels, width), f32)
    shell = jax.ShapeDtypeStruct((tall, levels, width), f32)
    bulk = jax.ShapeDtypeStruct((tiles, per_field + 1, levels, LANES), f32)
    mark = jax.ShapeDtypeStruct((levels, LANES), f32)

    def prepare(field, *after_this):
        return pl.pallas_call(
            functools.partial(prepare_kernel, field),
            out_shape=[band, band, band, shell, shell],
            in_specs=[hbm, vmem, vmem] + [anywhere] * len(after_this),
            out_specs=[vmem] * 5,
            scratch_shapes=[
                pltpu.VMEM((levels, rows, width), f32),
                pltpu.SemaphoreType.DMA((rows // 8,)),
            ],
            compiler_params=params(8),
            cost_estimate=pl.CostEstimate(
                flops=20_000_000, bytes_accessed=3_000_000, transcendentals=0
            ),
            name=f"prepare_{field}",
        )(
            pltpu.with_memory_space_constraint(starting_tracer_fields, pltpu.HBM),
            surface_exchange_inputs, mask, *after_this,
        )

    def forecast(field, prepared, *extra):
        scratch = [
            pltpu.VMEM((tall, levels, width), f32),
            pltpu.VMEM((tall, levels, width), f32),
            pltpu.VMEM(bulk.shape, f32),
            pltpu.SemaphoreType.DMA((5,)),
        ]
        if field == 0:
            scratch.append(pltpu.VMEM((2, tiles, width), f32))
        return pl.pallas_call(
            functools.partial(forecast_kernel, field),
            out_shape=[bulk, mark] if field == 0 else bulk,
            in_specs=[vmem] * (9 + len(extra)),
            out_specs=[anywhere, vmem] if field == 0 else anywhere,
            scratch_shapes=scratch,
            compiler_params=params(8),
            cost_estimate=pl.CostEstimate(
                flops=40_000_000, bytes_accessed=3_000_000, transcendentals=0
            ),
            name=f"forecast_{field}",
        )(*prepared, before, after, diffusivity, mixing, *extra)

    sent0, done0 = forecast(0, prepare(0), obs_index)
    held0 = lax.all_to_all(sent0, "member", split_axis=0, concat_axis=0, tiled=True)
    sent1 = forecast(1, prepare(1, done0))
    sent1 = pl.pallas_call(
        gram_kernel,
        out_shape=bulk,
        in_specs=[smem, vmem, vmem, vmem, smem, anywhere],
        out_specs=anywhere,
        scratch_shapes=[
            pltpu.VMEM((tiles, 1, levels, LANES), f32),
            pltpu.SemaphoreType.DMA,
        ],
        input_output_aliases={5: 0},
        compiler_params=params(4),
        name="gram",
    )(tile.reshape(1).astype(jnp.int32), held0, obs_value, obs_error, obs_count, sent1)
    held1 = lax.all_to_all(sent1, "member", split_axis=0, concat_axis=0, tiled=True)

    deep = members * levels
    updated = pl.pallas_call(
        mix_kernel,
        out_shape=jax.ShapeDtypeStruct((members, fields * per_field, levels, LANES), f32),
        in_specs=[vmem, vmem, vmem],
        out_specs=vmem,
        scratch_shapes=[
            pltpu.VMEM((deep, deep), jnp.bfloat16),
            pltpu.VMEM((deep, deep), jnp.bfloat16),
        ],
        compiler_params=params(16),
        name="mix",
    )(held0, held1, tile_mask)

    back = lax.all_to_all(updated, "member", split_axis=0, concat_axis=0, tiled=True)

    return pl.pallas_call(
        settle_kernel,
        grid=(rows // 16,),
        out_shape=jax.ShapeDtypeStruct(starting_tracer_fields.shape, f32),
        in_specs=[vmem],
        out_specs=pl.BlockSpec((1, fields, levels, 16, width), lambda i: (0, 0, 0, i, 0)),
        compiler_params=params(16),
        name="settle",
    )(back)


def solution(mesh):
    placed = (
        P("member", None, None, "domain", None),
        P("member", None, "domain", None),
        P(),
        P(),
        P(),
        P("domain", None, None),
        P("domain", None),
        P("domain", None, None),
        P("domain", None, None),
    )
    return jax.shard_map(
        shards,
        mesh=mesh,
        in_specs=placed,
        out_specs=P("member", None, None, "domain", None),
        check_vma=False,
    )
```

time: 191 us -> 181 us (0.948)
  local copies, waits for them, and re-layouts: 5.14 us -> 2.07 us
  waiting for transfers between devices: 71.4 us -> 68.6 us
  Pallas kernels: 20.2 us -> 18 us
    unnamed x18, local copies, waits for them, and re-layouts: 3.13 us -> 0.05 us
    pallas_call x3 -> x5, Pallas kernels: 16.4 us -> 14.2 us  [the longest x2 7.92 us: forecast(): pl.pallas_call(functools.partial(forecast_kernel, field), out_shape=[bulk...]
  transfers between devices with their start and end apart: 4 -> 4, of which waited for: 3 -> 2; matrix products, arithmetic and copies ran while one was open for 1% -> 1% of each run, Pallas kernels for 3% -> 4%
where the time goes in v3:
time: 181 us
  waiting for transfers between devices  68.6 us (38%)
  blocking collectives  67.4 us (37%)
  starting transfers between devices  23.5 us (13%)
  Pallas kernels  18 us (10%)
  local copies, waits for them, and re-layouts  2.07 us (1%)
    all_to_all x1, blocking collectives, shards(): lax.all_to_all(updated, 'member', split_axis=0, concat_axis=0, tiled=True)  67.4 us
    all_to_all x1, waiting for transfers between devices, shards(): lax.all_to_all(sent1, 'member', split_axis=0, concat_axis=0, tiled=True)  36.9 us
    all_to_all x1, waiting for transfers between devices, shards(): lax.all_to_all(sent0, 'member', split_axis=0, concat_axis=0, tiled=True)  31.7 us
    all_to_all x1, starting transfers between devices, shards(): lax.all_to_all(sent0, 'member', split_axis=0, concat_axis=0, tiled=True)  11.3 us
    pallas_call x2, Pallas kernels, forecast(): pl.pallas_call(functools.partial(forecast_kernel, field), out_shape=[bulk...  7.92 us
    all_to_all x1, starting transfers between devices, shards(): lax.all_to_all(sent1, 'member', split_axis=0, concat_axis=0, tiled=True)  6.57 us
    ppermute x1, starting transfers between devices, shards(): after = lax.ppermute(edge(0, 0), 'domain', down)  3.64 us
  transfers between devices with their start and end apart: 4, of which 2 were waited for; matrix products, arithmetic and copies ran while one was open for 1% of the time, Pallas kernels for 4%

profile of v3, /device:TPU:8, one launch (start us, length us, event | category | flops | bytes accessed | tf_op | source)
XLA Modules:
  0.0 180.8 jit_solution(5483882094157855262)
XLA Ops:
  0.0 0.0 copy-start
  0.0 0.9 fusion.1
  0.9 1.1 slice_bitcast_fusion
  2.0 1.9 %collective-permute-start = (f32[2,17,640]{2,1,0:T(8,128)S(1)}, f32[2,17,640]{2,1,0:T(8,128)S(1)}, u32[]{:S(2)}, u32[]{:S(2)}) collective-permute-start(f32[2,17,640]{2,1,0:T(8,128)S(1)} %pad_maximum_fusion), channel_id=1, source_target_pairs={{0,1},{1,2},{2,3},{3,4},{4,5},{5,6},{6,7},{8,9},{9,10},{10,11},{11... | collective-permute-start | bytes 261128 | tf_op jit(solution)/shard_map/ppermute | solution.py:328
  4.0 3.6 %collective-permute-start.1 = (f32[2,17,640]{2,1,0:T(8,128)S(1)}, f32[2,17,640]{2,1,0:T(8,128)S(1)}, u32[]{:S(2)}, u32[]{:S(2)}) collective-permute-start(f32[2,17,640]{2,1,0:T(8,128)S(1)} %pad_maximum_fusion.1), channel_id=1, source_target_pairs={{1,0},{2,1},{3,2},{4,3},{5,4},{6,5},{7,6},{9,8},{10,9},{11,10},{12... | collective-permute-start | bytes 261128 | tf_op jit(solution)/shard_map/ppermute | solution.py:329
  7.7 1.0 fusion.mask_ref
  8.6 0.0 copy-done
  8.6 0.0 copy-start.3
  8.7 0.0 copy-start.6
  8.7 0.0 copy-start.7
  8.7 1.5 prepare_0.1
  10.2 0.0 collective-permute-done.before_ref
  10.2 0.0 collective-permute-done.1.after_ref
  10.2 0.0 copy-start.1
  10.2 0.0 copy-done.3
  10.3 0.0 copy-done.6
  10.3 0.0 copy-done.7
  10.3 4.0 %forecast_0.1 = (f32[32,11,8,128]{3,2,1,0:T(8,128)}, f32[8,128]{1,0:T(8,128)S(1)}) custom-call(f32[64,8,640]{2,1,0:T(8,128)S(1)} %get-tuple-element.17.turned, f32[64,8,640]{2,1,0:T(8,128)S(1)} %get-tuple-element.18.wet, f32[64,8,640]{2,1,0:T(8,128)S(1)} %get-tuple-element.19.source, f32[68,8,640]{2,1,0:T(8,128)S(1)} %get-tuple-element.20.sea8, ...), custom_call_target="tpu_custom_call" | custom-call | flops 40000000 | bytes 3000000 | tf_op jit(solution)/shard_map/forecast_0/pallas_call | solution.py:379
  14.3 0.0 copy-done.1
  14.3 11.3 %all-to-all-start = ((f32[32,11,8,128]{3,2,1,0:T(8,128)}), f32[32,11,8,128]{3,2,1,0:T(8,128)S(1)}, u32[]{:S(2)}, u32[]{:S(2)}) async-start(f32[32,11,8,128]{3,2,1,0:T(8,128)} %get-tuple-element.22), calls=%async_computation | async-start | bytes 2883584 | tf_op jit(solution)/shard_map/all_to_all | solution.py:393
  25.7 0.0 copy-start.2
  25.7 1.6 prepare_1.1
  27.3 0.0 copy-done.2
  27.3 0.0 copy-start.4
  27.3 0.0 copy-start.5
  27.3 0.0 copy-start.8
  27.3 3.9 %forecast_1.1._ = f32[32,11,8,128]{3,2,1,0:T(8,128)} custom-call(f32[64,8,640]{2,1,0:T(8,128)S(1)} %get-tuple-element.24.turned, f32[64,8,640]{2,1,0:T(8,128)S(1)} %get-tuple-element.25.wet, f32[64,8,640]{2,1,0:T(8,128)S(1)} %get-tuple-element.26.source, f32[68,8,640]{2,1,0:T(8,128)S(1)} %get-tuple-element.27.sea8, ...), custom_call_target="tpu_custom_call" | custom-call | flops 40000000 | bytes 3000000 | tf_op jit(solution)/shard_map/forecast_1/pallas_call | solution.py:379
  31.2 31.7 %all-to-all-done.held_ref.data0_ref = f32[32,11,8,128]{3,2,1,0:T(8,128)S(1)} async-done(((f32[32,11,8,128]{3,2,1,0:T(8,128)}), f32[32,11,8,128]{3,2,1,0:T(8,128)S(1)}, u32[]{:S(2)}, u32[]{:S(2)}) %all-to-all-start) | async-done | bytes 1441824 | tf_op jit(solution)/shard_map/all_to_all | solution.py:393
  62.9 0.0 copy-done.4
  62.9 0.0 copy-done.5
  63.0 0.0 copy-done.8
  63.0 1.6 gram.1
  64.6 6.6 %all-to-all-start.1 = ((f32[32,11,8,128]{3,2,1,0:T(8,128)}), f32[32,11,8,128]{3,2,1,0:T(8,128)S(1)}, u32[]{:S(2)}, u32[]{:S(2)}) async-start(f32[32,11,8,128]{3,2,1,0:T(8,128)} %gram.1), calls=%async_computation.1 | async-start | bytes 2883584 | tf_op jit(solution)/shard_map/all_to_all | solution.py:408
  71.2 36.9 %all-to-all-done.1.data1_ref = f32[32,11,8,128]{3,2,1,0:T(8,128)S(1)} async-done(((f32[32,11,8,128]{3,2,1,0:T(8,128)}), f32[32,11,8,128]{3,2,1,0:T(8,128)S(1)}, u32[]{:S(2)}, u32[]{:S(2)}) %all-to-all-start.1) | async-done | bytes 1441824 | tf_op jit(solution)/shard_map/all_to_all | solution.py:408
  108.1 3.2 %mix.1 = f32[32,20,8,128]{3,2,1,0:T(8,128)S(1)} custom-call(f32[32,11,8,128]{3,2,1,0:T(8,128)S(1)} %all-to-all-done.held_ref.data0_ref, f32[32,11,8,128]{3,2,1,0:T(8,128)S(1)} %all-to-all-done.1.data1_ref, f32[2,640]{1,0:T(2,128)S(1)} %constant_dynamic-slice_fusion.mask_ref), custom_call_target="tpu_custom_call" | custom-call | tf_op jit(solution)/shard_map/mix/pallas_call | solution.py:411
  111.3 67.4 %all_to_all.15.back_ref = f32[32,20,8,128]{3,2,1,0:T(8,128)S(1)} all-to-all(f32[32,20,8,128]{3,2,1,0:T(8,128)S(1)} %mix.1), channel_id=1, replica_groups=mesh['member'=32,'domain'=8] {'member'}, dimensions={0} | all-to-all | bytes 5242880 | tf_op jit(solution)/shard_map/all_to_all | solution.py:424
  178.7 2.1 %settle.1 = f32[1,2,8,64,640]{4,3,2,1,0:T(8,128)} custom-call(f32[32,20,8,128]{3,2,1,0:T(8,128)S(1)} %all_to_all.15.back_ref), custom_call_target="tpu_custom_call" | custom-call | tf_op jit(solution)/shard_map/settle/pallas_call | solution.py:426
  (5 shorter events, 0.1 us)
Async XLA Ops:
  0.0 8.6 %copy-start = (f32[1,2,64,640]{3,2,1,0:T(8,128)S(1)}, f32[1,2,64,640]{3,2,1,0:T(8,128)}, u32[]{:S(2)}) copy-start(f32[1,2,64,640]{3,2,1,0:T(8,128)} %flux_ref.3) | copy-start | bytes 983044
  2.0 8.2 %collective-permute-start = (f32[2,17,640]{2,1,0:T(8,128)S(1)}, f32[2,17,640]{2,1,0:T(8,128)S(1)}, u32[]{:S(2)}, u32[]{:S(2)}) collective-permute-start(f32[2,17,640]{2,1,0:T(8,128)S(1)} %pad_maximum_fusion), channel_id=1, source_target_pairs={{0,1},{1,2},{2,3},{3,4},{4,5},{5,6},{6,7},{8,9},{9,10},{10,11},{11... | collective-permute-start | bytes 261128 | tf_op jit(solution)/shard_map/ppermute | solution.py:328
  4.0 6.2 %collective-permute-start.1 = (f32[2,17,640]{2,1,0:T(8,128)S(1)}, f32[2,17,640]{2,1,0:T(8,128)S(1)}, u32[]{:S(2)}, u32[]{:S(2)}) collective-permute-start(f32[2,17,640]{2,1,0:T(8,128)S(1)} %pad_maximum_fusion.1), channel_id=1, source_target_pairs={{1,0},{2,1},{3,2},{4,3},{5,4},{6,5},{7,6},{9,8},{10,9},{11,10},{12... | collective-permute-start | bytes 261128 | tf_op jit(solution)/shard_map/ppermute | solution.py:329
  8.6 1.6 copy-start.3
  8.7 1.6 copy-start.6
  8.7 1.6 copy-start.7
  10.2 4.1 %copy-start.1 = (f32[2,17,640]{2,1,0:T(8,128)}, f32[2,17,640]{2,1,0:T(8,128)S(1)}, u32[]{:S(2)}) copy-start(f32[2,17,640]{2,1,0:T(8,128)S(1)} %collective-permute-done.1.after_ref) | copy-start | bytes 261124
  14.3 48.6 %all-to-all-start = ((f32[32,11,8,128]{3,2,1,0:T(8,128)}), f32[32,11,8,128]{3,2,1,0:T(8,128)S(1)}, u32[]{:S(2)}, u32[]{:S(2)}) async-start(f32[32,11,8,128]{3,2,1,0:T(8,128)} %get-tuple-element.22), calls=%async_computation | async-start | bytes 2883584 | tf_op jit(solution)/shard_map/all_to_all | solution.py:393
  25.7 1.6 copy-start.2
  27.3 35.6 %copy-start.4 = (f32[1,32,256]{2,1,0:T(8,128)S(1)}, f32[1,32,256]{2,1,0:T(8,128)}, u32[]{:S(2)}) copy-start(f32[1,32,256]{2,1,0:T(8,128)} %value_ref.1) | copy-start | bytes 98308
  27.3 35.6 %copy-start.5 = (f32[1,32,256]{2,1,0:T(8,128)S(1)}, f32[1,32,256]{2,1,0:T(8,128)}, u32[]{:S(2)}) copy-start(f32[1,32,256]{2,1,0:T(8,128)} %error_ref.1) | copy-start | bytes 98308
  27.3 35.6 %copy-start.8 = (s32[1,32]{1,0:T(1,128)S(1)}, s32[1,32]{1,0:T(1,128)}, u32[]{:S(2)}) copy-start(s32[1,32]{1,0:T(1,128)} %count_ref.1) | copy-start | bytes 388
  64.6 43.5 %all-to-all-start.1 = ((f32[32,11,8,128]{3,2,1,0:T(8,128)}), f32[32,11,8,128]{3,2,1,0:T(8,128)S(1)}, u32[]{:S(2)}, u32[]{:S(2)}) async-start(f32[32,11,8,128]{3,2,1,0:T(8,128)} %gram.1), calls=%async_computation.1 | async-start | bytes 2883584 | tf_op jit(solution)/shard_map/all_to_all | solution.py:408

commit v4 on v3

--- a/solution.py
+++ b/solution.py
@@ -12,10 +12,83 @@
 LANES = 128
 HALO = 2
 UNROLL = 10
+PACKED = 9
+TAIL = 32
+ROOM = PACKED * LANES - TAIL
+SPILL = 2
 
 
 def spread_row(row):
     return jnp.broadcast_to(row, (LEVELS, row.shape[1]))
+
+
+def survey_kernel(mask_ref, cell_ref, place_ref, first_ref, head_ref, sea_ref):
+    tiles, cells = place_ref.shape
+    rows = 2 * tiles
+    blocks = cells // LANES
+    sea_ref[...] = mask_ref[HALO : HALO + rows, :]
+    sea = mask_ref[HALO : HALO + rows, :].astype(jnp.bfloat16)
+    pick = lax.broadcasted_iota(jnp.int32, (tiles, rows), 1) - 2 * lax.broadcasted_iota(
+        jnp.int32, (tiles, rows), 0
+    )
+    sides = [
+        jnp.dot((pick == s).astype(jnp.bfloat16), sea, preferred_element_type=jnp.float32)
+        for s in range(2)
+    ]
+    sea = jnp.concatenate(sides, axis=1)
+    land = (1.0 - sea).astype(jnp.bfloat16)
+    stacked = jnp.concatenate([land[:, b * LANES : (b + 1) * LANES] for b in range(blocks)], axis=0)
+    before = (
+        lax.broadcasted_iota(jnp.int32, (LANES, LANES), 0)
+        < lax.broadcasted_iota(jnp.int32, (LANES, LANES), 1)
+    ).astype(jnp.bfloat16)
+    within = jnp.dot(stacked, before, preferred_element_type=jnp.float32)
+    totals = jnp.dot(
+        stacked, jnp.ones((LANES, LANES), jnp.bfloat16), preferred_element_type=jnp.float32
+    )
+    offset = jnp.zeros((tiles, LANES), jnp.float32)
+    shifts = []
+    for b in range(blocks):
+        part = slice(b * tiles, (b + 1) * tiles)
+        shifts.append(within[part] + offset)
+        offset = offset + totals[part]
+    shift = jnp.concatenate(shifts, axis=1).astype(jnp.int32)
+    cell = lax.broadcasted_iota(jnp.int32, (tiles, cells), 1)
+    rank = cell - shift
+    place = jnp.where(rank < ROOM, rank, rank + TAIL)
+    place_ref[...] = jnp.where(sea > 0.0, place, -1)
+    lane = lax.broadcasted_iota(jnp.int32, first_ref.shape, 1)
+    first = jnp.zeros(first_ref.shape, jnp.int32)
+    for b in range(blocks):
+        head = place[:, b * LANES : b * LANES + 1]
+        head = (jnp.minimum(head >> 7, PACKED - 1) << 7) + (head & (LANES - 1))
+        first = jnp.where(lane == b, jnp.broadcast_to(head, first.shape), first)
+    number = lax.broadcasted_iota(jnp.int32, first.shape, 0)
+    first = first + number * (FIELDS * PACKED * LANES)
+    last = jnp.max(jnp.where(sea > 0.0, place, -1), axis=1, keepdims=True)
+    last = jnp.broadcast_to(jnp.max(last, axis=0, keepdims=True), first.shape)
+    spills = (last >= PACKED * LANES).astype(jnp.int32)
+    first_ref[...] = jnp.where(lane == LANES - 1, spills, first)
+    state = jnp.where(sea > 0.0, shift * 2048 + cell, 0)
+    for bit in range(11):
+        other = pltpu.roll(state, cells - (1 << bit), 1)
+        comes = (other & (2048 << bit)) != 0
+        goes = (state & (2048 << bit)) != 0
+        state = jnp.where(comes, other, jnp.where(goes, 0, state))
+    state = state & 2047
+    heads = jnp.zeros(head_ref.shape, jnp.int32)
+    reach = jnp.zeros((tiles, 1), jnp.int32)
+    for q in range(PACKED):
+        part = state[:, q * LANES : (q + 1) * LANES]
+        heads = jnp.where(lane == q, jnp.broadcast_to(part[:, 0:1], heads.shape), heads)
+        reach = jnp.maximum(reach, jnp.max(part, axis=1, keepdims=True) - part[:, 0:1])
+    wide = jnp.max(reach, axis=0, keepdims=True)
+    heads = heads + number * cells
+    heads = jnp.where(lane == PACKED, jnp.broadcast_to(wide, heads.shape), heads)
+    head_ref[...] = jnp.where(lane == PACKED + 1, spills, heads)
+    state = state + lax.broadcasted_iota(jnp.int32, state.shape, 0) * cells
+    cell_ref[:, : PACKED * LANES] = state[:, : PACKED * LANES]
+    cell_ref[:, PACKED * LANES :] = pltpu.roll(state, cells - ROOM, 1)[:, : SPILL * LANES]
 
 
 def prepare_kernel(field, x_ref, flux_ref, mask_ref, *rest):
@@ -54,11 +127,14 @@
 
 def forecast_kernel(field, turned, wet, source, sea8, crowd8, before_ref, after_ref,
                     diff_ref, mix_ref, *rest):
+    cell_ref, head_ref, rest = rest[0], rest[1], rest[2:]
     if field == 0:
-        index_ref, out_ref, done_ref, first, moist, packed, sems, surface = rest
+        index_ref, out_ref, spill_ref, done_ref, first, moist, plain, packed, heads, sems, surface, tails = rest
         done_ref[...] = jnp.zeros_like(done_ref)
     else:
-        out_ref, first, moist, packed, sems = rest
+        out_ref, spill_ref, first, moist, plain, packed, heads, sems = rest
+    table = pltpu.make_async_copy(head_ref, heads, sems.at[0])
+    table.start()
     rows, width = turned.shape[0], turned.shape[2]
     tall = rows + 2 * HALO
     blocks = width // LANES
@@ -122,24 +198,23 @@
             r = HALO + 2 * tile + side
             value = stepped(r, first[r], moist[r], moist[r - 1], moist[r + 1], source[r - HALO])
             for j in range(blocks):
-                packed[tile, side * blocks + j] = value[:, j * LANES : (j + 1) * LANES]
+                plain[tile * 2 * blocks + side * blocks + j] = value[:, j * LANES : (j + 1) * LANES]
             if field == 0:
                 surface[side, pl.ds(tile, 1), :] = value[0:1, :]
         return 0
 
     tiles = rows // 2
-    groups = 4
-    share = tiles // groups
-    copies = []
-    for g in range(groups):
-        lax.fori_loop(g * share, (g + 1) * share, outer, 0, unroll=4)
-        part = (pl.ds(g * share, share), pl.ds(0, 2 * blocks))
-        copies.append(pltpu.make_async_copy(packed.at[part], out_ref.at[part], sems.at[g]))
-        copies[-1].start()
+    lax.fori_loop(0, tiles, outer, 0, unroll=4)
+    table.wait()
+    lane_row = lax.broadcasted_iota(jnp.int32, (LEVELS, LANES), 1)
+
+    def take(piece, lanes):
+        return jnp.take_along_axis(piece, lanes, axis=1, mode="promise_in_bounds")
 
     if field == 0:
         slots = index_ref.shape[2]
         for g in range(tiles // 8):
+            pieces = []
             for h in range(slots // LANES):
                 where = index_ref[0, g * 8 : (g + 1) * 8, h * LANES : (h + 1) * LANES]
                 block, lanes = where >> 7, where & (LANES - 1)
@@ -147,24 +222,98 @@
                 for q in range(2 * blocks):
                     s, j = divmod(q, blocks)
                     piece = surface[s, g * 8 : (g + 1) * 8, j * LANES : (j + 1) * LANES]
-                    taken = jnp.take_along_axis(piece, lanes, axis=1, mode="promise_in_bounds")
-                    found = jnp.where(block == q, taken, found)
-                packed[g * 8 : (g + 1) * 8, 2 * blocks, h, :] = found
-        part = (slice(None), pl.ds(2 * blocks, 1))
-        copies.append(pltpu.make_async_copy(packed.at[part], out_ref.at[part], sems.at[groups]))
-        copies[-1].start()
-    for copy in copies:
+                    found = jnp.where(block == q, take(piece, lanes), found)
+                for k in range(LANES // TAIL):
+                    move = (LANES - TAIL - k * TAIL) % LANES
+                    pieces.append(pltpu.roll(found, move, 1) if move else found)
+            tails[g * 8 : (g + 1) * 8] = jnp.swapaxes(jnp.stack(pieces, axis=0), 0, 1)
+
+    def wanted_at(base, t, q):
+        row = cell_ref[pl.ds(base, 8), q * LANES : (q + 1) * LANES]
+        return spread_row(row[t : t + 1])
+
+    def chosen_from(tile, wanted, start):
+        own = tile * 2 * blocks
+        block, lanes = wanted >> 7, wanted & (LANES - 1)
+        chosen = take(plain[own + start], lanes)
+        for b in range(start + 1, 2 * blocks):
+            chosen = jnp.where(block == own + b, take(plain[own + b], lanes), chosen)
+        return chosen
+
+    def sent(base, group):
+        part = pl.ds(base, 8)
+        return pltpu.make_async_copy(
+            packed.at[part, pl.ds(0, PACKED)], out_ref.at[part, pl.ds(0, PACKED)], sems.at[group]
+        )
+
+    def pack(group, _, near):
+        base = pl.multiple_of(group * 8, 8)
+        for t in range(8):
+            tile = base + t
+            for q in range(PACKED):
+                wanted = wanted_at(base, t, q)
+                if near:
+                    head = heads[tile, q]
+                    b = head >> 7
+                    turn = lane_row >= (head & (LANES - 1))
+                    low, middle, high = plain[b], plain[b + 1], plain[b + 2]
+                    lanes = wanted & (LANES - 1)
+                    early = take(jnp.where(turn, low, middle), lanes)
+                    late = take(jnp.where(turn, middle, high), lanes)
+                    chosen = jnp.where(wanted - head < LANES, early, late)
+                else:
+                    chosen = chosen_from(tile, wanted, q)
+                if field == 0 and q == PACKED - 1:
+                    chosen = jnp.where(lane_row >= LANES - TAIL, tails[tile], chosen)
+                packed[tile, q] = chosen
+        sent(base, group).start()
+        return 0
+
+    groups = tiles // 8
+
+    @pl.when(heads[0, PACKED] < 2 * LANES)
+    def _():
+        lax.fori_loop(0, groups, functools.partial(pack, near=True), 0)
+
+    @pl.when(heads[0, PACKED] >= 2 * LANES)
+    def _():
+        lax.fori_loop(0, groups, functools.partial(pack, near=False), 0)
+
+    @pl.when(heads[0, PACKED + 1] > 0)
+    def _():
+        def late_cells(group, _):
+            base = pl.multiple_of(group * 8, 8)
+            for t in range(8):
+                for q in range(PACKED, PACKED + SPILL):
+                    packed[base + t, q] = chosen_from(
+                        base + t, wanted_at(base, t, q), ROOM // LANES
+                    )
+            return 0
+
+        lax.fori_loop(0, groups, late_cells, 0)
+        copy = pltpu.make_async_copy(
+            packed.at[:, pl.ds(PACKED, SPILL)], spill_ref, sems.at[groups]
+        )
+        copy.start()
         copy.wait()
+
+    for g in range(groups):
+        sent(g * 8, g).wait()
 
 
 def gram_kernel(tile_ref, held_ref, value_ref, error_ref, count_ref, _, out_ref, spread, sem):
     tile = tile_ref[0]
-    members, per_field = held_ref.shape[0], held_ref.shape[1] - 1
+    members = held_ref.shape[0]
     halves = value_ref.shape[2] // LANES
     slot = lax.broadcasted_iota(jnp.int32, (1, LANES), 1)
     total = jnp.zeros((members + 8, members), jnp.float32)
     for h in range(halves):
-        seen = held_ref[:, per_field, h, :]
+        seen = jnp.zeros((members, LANES), jnp.float32)
+        for k in range(LANES // TAIL):
+            piece = held_ref[:, PACKED - 1, h * (LANES // TAIL) + k, :]
+            move = (k + 1) * TAIL % LANES
+            piece = pltpu.roll(piece, move, 1) if move else piece
+            seen = jnp.where((slot >= k * TAIL) & (slot < (k + 1) * TAIL), piece, seen)
         average = jnp.mean(seen, axis=0, keepdims=True)
         anomaly = seen - average
         span = slice(h * LANES, (h + 1) * LANES)
@@ -188,7 +337,7 @@
     packed = jnp.where(corner & (row == 1), pull, packed)
     for m in range(members):
         spread[m, 0] = packed
-    copy = pltpu.make_async_copy(spread, out_ref.at[:, pl.ds(per_field, 1)], sem)
+    copy = pltpu.make_async_copy(spread, out_ref.at[:, pl.ds(PACKED, 1)], sem)
     copy.start()
     copy.wait()
 
@@ -236,12 +385,30 @@
     return jnp.where(live, weights - centre + 1.0 / count, 0.0)
 
 
-def mix_kernel(data0_ref, data1_ref, mask_ref, out_ref, high, low):
-    members, per_field = data0_ref.shape[0], data0_ref.shape[1] - 1
-    blocks = mask_ref.shape[1] // LANES
+def mixed(high, low, data):
+    major = data.astype(jnp.bfloat16)
+    minor = (data - major.astype(jnp.float32)).astype(jnp.bfloat16)
+    total = jnp.dot(high[...], major, preferred_element_type=jnp.float32)
+    total = total + jnp.dot(high[...], minor, preferred_element_type=jnp.float32)
+    return total + jnp.dot(low[...], major, preferred_element_type=jnp.float32)
+
+
+def mix_strip(high, low, data_ref, at, out_ref, to, blocks):
+    members = data_ref.shape[0]
     deep = members * LEVELS
-
-    kernel = ensemble_kernel(jnp.sum(data1_ref[:, per_field], axis=0), LANES)[:, :members]
+    data = jnp.concatenate(
+        [data_ref[:, at + b].reshape(deep, LANES) for b in range(blocks)], axis=1
+    )
+    result = mixed(high, low, data)
+    for b in range(blocks):
+        out_ref[:, to + b] = result[:, b * LANES : (b + 1) * LANES].reshape(members, LEVELS, LANES)
+
+
+def mix_kernel(data0_ref, data1_ref, out_ref, high, low, ready, sems):
+    members = data0_ref.shape[0]
+    deep = members * LEVELS
+
+    kernel = ensemble_kernel(jnp.sum(data1_ref[:, PACKED], axis=0), LANES)[:, :members]
     major = kernel.astype(jnp.bfloat16)
     minor = (kernel - major.astype(jnp.float32)).astype(jnp.bfloat16)
     spread = (
@@ -259,42 +426,84 @@
         )
         target[...] = jnp.where(same, full, 0.0).astype(jnp.bfloat16)
 
+    blocks = 3
+
+    def leaving(to, n):
+        part = (slice(None), pl.ds(to, blocks))
+        return pltpu.make_async_copy(ready.at[part], out_ref.at[part], sems.at[n])
+
     for f, data_ref in ((0, data0_ref), (1, data1_ref)):
 
         def strip(i, _, f=f, data_ref=data_ref):
-            first = i * blocks
-            data = jnp.concatenate(
-                [data_ref[:, first + b].reshape(deep, LANES) for b in range(blocks)], axis=1
-            )
-            major = data.astype(jnp.bfloat16)
-            minor = (data - major.astype(jnp.float32)).astype(jnp.bfloat16)
-            mixed = jnp.dot(high[...], major, preferred_element_type=jnp.float32)
-            mixed = mixed + jnp.dot(high[...], minor, preferred_element_type=jnp.float32)
-            mixed = mixed + jnp.dot(low[...], major, preferred_element_type=jnp.float32)
-            ocean = mask_ref[pl.ds(i, 1), :] > 0.0
-            mixed = jnp.where(ocean, mixed, data)
-            for b in range(blocks):
-                out_ref[:, f * per_field + first + b] = mixed[
-                    :, b * LANES : (b + 1) * LANES
-                ].reshape(members, LEVELS, LANES)
+            at = i * blocks
+            to = f * PACKED + at
+            mix_strip(high, low, data_ref, at, ready, to, blocks)
+            leaving(to, f * (PACKED // blocks) + i).start()
             return 0
 
-        lax.fori_loop(0, 2, strip, 0)
-
-
-def settle_kernel(back_ref, out_ref):
+        lax.fori_loop(0, PACKED // blocks, strip, 0)
+    for n in range(FIELDS * PACKED // blocks):
+        leaving(n * blocks, n).wait()
+
+
+def spill_kernel(data_ref, high, low, out_ref):
+    mix_strip(high, low, data_ref, 0, out_ref, 0, data_ref.shape[1])
+
+
+def settle_rows(spilled, first_ref, back_ref, spill_ref, place_ref, sea_ref, x_ref, out_ref):
     blocks = out_ref.shape[4] // LANES
-    share = out_ref.shape[3] // 2
-    first = pl.program_id(0) * share
-    for f in range(FIELDS):
-        for j in range(blocks):
-            for half in range(share // 4):
-                rows = []
-                for t in range(4):
-                    for s in range(2):
-                        rows.append(back_ref[first + half * 4 + t, (f * 2 + s) * blocks + j])
-                turned = jnp.swapaxes(jnp.stack(rows, axis=0), 0, 1)
-                out_ref[0, f, :, half * 8 : (half + 1) * 8, j * LANES : (j + 1) * LANES] = turned
+    start = pl.multiple_of(pl.program_id(0) * 8, 8)
+    end = back_ref.shape[0] - 1
+    lane_row = lax.broadcasted_iota(jnp.int32, (LEVELS, LANES), 1)
+
+    def take(source, lanes):
+        return jnp.take_along_axis(source, lanes, axis=1, mode="promise_in_bounds")
+
+    for j in range(blocks):
+        lanes_at = slice(j * LANES, (j + 1) * LANES)
+        wanted8 = [
+            place_ref[pl.ds(start, 8), b * LANES : (b + 1) * LANES] for b in (j, blocks + j)
+        ]
+        for half in range(2):
+            rows = ([], [])
+            for t in range(half * 4, half * 4 + 4):
+                for s in range(2):
+                    b = s * blocks + j
+                    wanted = spread_row(wanted8[s][t : t + 1])
+                    block, lanes = wanted >> 7, wanted & (LANES - 1)
+                    head = first_ref[start + t, b]
+                    at = head >> 7
+                    turn = lane_row >= (head & (LANES - 1))
+                    for f in range(FIELDS):
+                        low = back_ref[at + f * PACKED]
+                        high = back_ref[jnp.minimum(at + (f * PACKED + 1), end)]
+                        value = take(jnp.where(turn, low, high), lanes)
+                        if spilled and (b + 1) * LANES > ROOM:
+                            for o in range(SPILL):
+                                late = take(spill_ref[start + t, f * SPILL + o], lanes)
+                                value = jnp.where(block == PACKED + o, late, value)
+                        rows[f].append(value)
+            here = pl.ds(pl.multiple_of(2 * start + half * 8, 8), 8)
+            there = slice(half * 8, half * 8 + 8)
+            ocean = sea_ref[here, lanes_at] > 0.0
+            for f in range(FIELDS):
+                turned = jnp.swapaxes(jnp.stack(rows[f], axis=0), 0, 1)
+                for l in range(LEVELS):
+                    out_ref[0, f, l, there, lanes_at] = jnp.where(
+                        ocean, turned[l], x_ref[0, f, l, here, lanes_at]
+                    )
+
+
+def settle_kernel(first_ref, *refs):
+    late = first_ref[0, LANES - 1] > 0
+
+    @pl.when(late)
+    def _():
+        settle_rows(True, first_ref, *refs)
+
+    @pl.when(jnp.logical_not(late))
+    def _():
+        settle_rows(False, first_ref, *refs)
 
 
 def shards(
@@ -330,7 +539,6 @@
 
     padded = jnp.pad(land_mask, ((HALO, HALO), (0, 0)))
     mask = lax.dynamic_slice_in_dim(padded, domain * rows, rows + 2 * HALO, 0).astype(jnp.float32)
-    tile_mask = lax.dynamic_slice_in_dim(mask, HALO + tile * 2, 2, 0)
 
     f32 = jnp.float32
     tall = rows + 2 * HALO
@@ -344,8 +552,28 @@
 
     band = jax.ShapeDtypeStruct((rows, levels, width), f32)
     shell = jax.ShapeDtypeStruct((tall, levels, width), f32)
-    bulk = jax.ShapeDtypeStruct((tiles, per_field + 1, levels, LANES), f32)
+    i32 = jnp.int32
+    bulks = [pltpu.HBM((tiles, PACKED + f, levels, LANES), f32) for f in range(2)]
+    extra = pltpu.HBM((tiles, SPILL, levels, LANES), f32)
     mark = jax.ShapeDtypeStruct((levels, LANES), f32)
+
+    cell, place, first, heads, sea = pl.pallas_call(
+        survey_kernel,
+        out_shape=[
+            jax.ShapeDtypeStruct((tiles, (PACKED + SPILL) * LANES), i32),
+            pltpu.HBM((tiles, 2 * width), i32),
+            pltpu.HBM((tiles, LANES), i32),
+            jax.ShapeDtypeStruct((tiles, LANES), i32),
+            pltpu.HBM((rows, width), f32),
+        ],
+        in_specs=[vmem],
+        out_specs=[vmem] * 5,
+        compiler_params=params(8),
+        cost_estimate=pl.CostEstimate(
+            flops=20_000_000, bytes_accessed=500_000, transcendentals=0
+        ),
+        name="survey",
+    )(mask)
 
     def prepare(field, *after_this):
         return pl.pallas_call(
@@ -367,36 +595,46 @@
             surface_exchange_inputs, mask, *after_this,
         )
 
-    def forecast(field, prepared, *extra):
+    def forecast(field, prepared, *inputs):
         scratch = [
             pltpu.VMEM((tall, levels, width), f32),
             pltpu.VMEM((tall, levels, width), f32),
-            pltpu.VMEM(bulk.shape, f32),
-            pltpu.SemaphoreType.DMA((5,)),
+            pltpu.VMEM((tiles * per_field + 2, levels, LANES), f32),
+            pltpu.VMEM((tiles, PACKED + SPILL, levels, LANES), f32),
+            pltpu.SMEM((tiles, LANES), i32),
+            pltpu.SemaphoreType.DMA((tiles // 8 + 1,)),
         ]
+        out_shape = [bulks[field], extra]
+        out_specs = [hbm] * 2
         if field == 0:
             scratch.append(pltpu.VMEM((2, tiles, width), f32))
+            scratch.append(pltpu.VMEM((tiles, levels, LANES), f32))
+            out_shape.append(mark)
+            out_specs.append(vmem)
         return pl.pallas_call(
             functools.partial(forecast_kernel, field),
-            out_shape=[bulk, mark] if field == 0 else bulk,
-            in_specs=[vmem] * (9 + len(extra)),
-            out_specs=[anywhere, vmem] if field == 0 else anywhere,
+            out_shape=out_shape,
+            in_specs=[vmem] * (11 + len(inputs)),
+            out_specs=out_specs,
             scratch_shapes=scratch,
-            compiler_params=params(8),
+            compiler_params=params(10),
             cost_estimate=pl.CostEstimate(
                 flops=40_000_000, bytes_accessed=3_000_000, transcendentals=0
             ),
             name=f"forecast_{field}",
-        )(*prepared, before, after, diffusivity, mixing, *extra)
-
-    sent0, done0 = forecast(0, prepare(0), obs_index)
-    held0 = lax.all_to_all(sent0, "member", split_axis=0, concat_axis=0, tiled=True)
-    sent1 = forecast(1, prepare(1, done0))
+        )(*prepared, before, after, diffusivity, mixing, cell, heads, *inputs)
+
+    def exchanged(array):
+        return lax.all_to_all(array, "member", split_axis=0, concat_axis=0, tiled=True)
+
+    sent0, spill0, done0 = forecast(0, prepare(0), obs_index)
+    held0 = exchanged(sent0)
+    sent1, spill1 = forecast(1, prepare(1, done0))
     sent1 = pl.pallas_call(
         gram_kernel,
-        out_shape=bulk,
-        in_specs=[smem, vmem, vmem, vmem, smem, anywhere],
-        out_specs=anywhere,
+        out_shape=bulks[1],
+        in_specs=[smem, vmem, vmem, vmem, smem, hbm],
+        out_specs=hbm,
         scratch_shapes=[
             pltpu.VMEM((tiles, 1, levels, LANES), f32),
             pltpu.SemaphoreType.DMA,
@@ -405,33 +643,57 @@
         compiler_params=params(4),
         name="gram",
     )(tile.reshape(1).astype(jnp.int32), held0, obs_value, obs_error, obs_count, sent1)
-    held1 = lax.all_to_all(sent1, "member", split_axis=0, concat_axis=0, tiled=True)
+    held1 = exchanged(sent1)
 
     deep = members * levels
-    updated = pl.pallas_call(
+    half = jax.ShapeDtypeStruct((deep, deep), jnp.bfloat16)
+    updated, high, low = pl.pallas_call(
         mix_kernel,
-        out_shape=jax.ShapeDtypeStruct((members, fields * per_field, levels, LANES), f32),
-        in_specs=[vmem, vmem, vmem],
-        out_specs=vmem,
+        out_shape=[
+            pltpu.HBM((members, fields * PACKED, levels, LANES), f32), half, half
+        ],
+        in_specs=[vmem, vmem],
+        out_specs=[hbm, vmem, vmem],
         scratch_shapes=[
-            pltpu.VMEM((deep, deep), jnp.bfloat16),
-            pltpu.VMEM((deep, deep), jnp.bfloat16),
+            pltpu.VMEM((members, fields * PACKED, levels, LANES), f32),
+            pltpu.SemaphoreType.DMA((fields * PACKED // 3,)),
         ],
         compiler_params=params(16),
         name="mix",
-    )(held0, held1, tile_mask)
-
-    back = lax.all_to_all(updated, "member", split_axis=0, concat_axis=0, tiled=True)
-
+    )(held0, held1)
+    back = exchanged(updated)
+
+    def late(spill, high, low):
+        there = exchanged(spill)
+        there = pl.pallas_call(
+            spill_kernel,
+            out_shape=jax.ShapeDtypeStruct(there.shape, f32),
+            in_specs=[vmem] * 3,
+            out_specs=vmem,
+            compiler_params=params(16),
+            name="mix_spill",
+        )(there, high, low)
+        return exchanged(there)
+
+    def none(spill, high, low):
+        return spill
+
+    ocean = jnp.sum(land_mask, axis=1).reshape(-1, 2).sum(axis=1)
+    spill = jnp.concatenate([spill0, spill1], axis=1)
+    spill = lax.cond(jnp.max(ocean) > ROOM, late, none, spill, high, low)
+
+    bands = pl.BlockSpec((1, fields, levels, 16, width), lambda i: (0, 0, 0, i, 0))
     return pl.pallas_call(
         settle_kernel,
         grid=(rows // 16,),
         out_shape=jax.ShapeDtypeStruct(starting_tracer_fields.shape, f32),
-        in_specs=[vmem],
-        out_specs=pl.BlockSpec((1, fields, levels, 16, width), lambda i: (0, 0, 0, i, 0)),
-        compiler_params=params(16),
+        in_specs=[smem] + [vmem] * 5,
+        out_specs=bands,
+        compiler_params=params(12),
         name="settle",
-    )(back)
+    )(
+        first, back.reshape(-1, levels, LANES), spill, place, sea, starting_tracer_fields,
+    )
 
 
 def solution(mesh):

time: 181 us -> 175 us (0.967)
  waiting for transfers between devices: 68.6 us -> 53.9 us
  Pallas kernels: 18 us -> 26.6 us
  blocking collectives: 67.4 us -> 62.4 us
  local copies, waits for them, and re-layouts: 2.07 us -> 4.84 us
  other arithmetic: 1 us -> 3.25 us
    all_to_all x2, waiting for transfers between devices: 68.6 us -> 53.9 us  [exchanged(): lax.all_to_all(array, 'member', split_axis=0, concat_axis=0, tiled=True)]
    pallas_call x4 -> x5, Pallas kernels: 12.7 us -> 19.4 us  [the longest x2 11.4 us: forecast(): pl.pallas_call(functools.partial(forecast_kernel, field), out_shape=out_s...]
    all_to_all x1, blocking collectives: 67.4 us -> 62.4 us  [exchanged(): lax.all_to_all(array, 'member', split_axis=0, concat_axis=0, tiled=True)]
    pallas_call x1, Pallas kernels: 2.13 us -> 4.08 us  [shards(): pl.pallas_call(settle_kernel, grid=(rows // 16,), out_shape=jax.ShapeDtyp...]
  transfers between devices with their start and end apart: 4 -> 4, of which waited for: 2 -> 2; matrix products, arithmetic and copies ran while one was open for 1% -> 3% of each run, Pallas kernels for 4% -> 6%
where the time goes in v4:
time: 175 us; the launch traced here: 174 us
  blocking collectives  62.4 us (36%)
  waiting for transfers between devices  53.9 us (31%)
  Pallas kernels  26.6 us (15%)
  starting transfers between devices  22.1 us (13%)
  local copies, waits for them, and re-layouts  4.84 us (3%)
  other arithmetic  3.25 us (2%)
    all_to_all x1, blocking collectives, exchanged(): lax.all_to_all(array, 'member', split_axis=0, concat_axis=0, tiled=True)  62.4 us
    all_to_all x2, waiting for transfers between devices, exchanged(): lax.all_to_all(array, 'member', split_axis=0, concat_axis=0, tiled=True)  53.9 us
    all_to_all x2, starting transfers between devices, exchanged(): lax.all_to_all(array, 'member', split_axis=0, concat_axis=0, tiled=True)  16.5 us
    pallas_call x2, Pallas kernels, forecast(): pl.pallas_call(functools.partial(forecast_kernel, field), out_shape=out_s...  11.4 us
    pallas_call x1, Pallas kernels, shards(): pl.pallas_call(mix_kernel, out_shape=[pltpu.HBM((members, fields * PACKED...  4.32 us
    pallas_call x1, Pallas kernels, shards(): pl.pallas_call(settle_kernel, grid=(rows // 16,), out_shape=jax.ShapeDtyp...  4.08 us
    ppermute x1, starting transfers between devices, shards(): after = lax.ppermute(edge(0, 0), 'domain', down)  3.64 us
  transfers between devices with their start and end apart: 4, of which 2 were waited for; matrix products, arithmetic and copies ran while one was open for 3% of the time, Pallas kernels for 6%

profile of v4, /device:TPU:8, one launch (start us, length us, event | category | flops | bytes accessed | tf_op | source)
XLA Modules:
  0.0 173.9 jit_solution(13606769191285742788)
XLA Ops:
  0.0 1.1 slice_bitcast_fusion
  1.1 0.0 copy-start.1
  1.2 0.9 fusion.1
  2.0 1.9 %collective-permute-start = (f32[2,17,640]{2,1,0:T(8,128)S(1)}, f32[2,17,640]{2,1,0:T(8,128)S(1)}, u32[]{:S(2)}, u32[]{:S(2)}) collective-permute-start(f32[2,17,640]{2,1,0:T(8,128)S(1)} %pad_maximum_fusion), channel_id=1, source_target_pairs={{0,1},{1,2},{2,3},{3,4},{4,5},{5,6},{6,7},{8,9},{9,10},{10,11},{11... | collective-permute-start | bytes 261128 | tf_op jit(solution)/shard_map/ppermute | solution.py:537
  4.0 3.6 %collective-permute-start.1 = (f32[2,17,640]{2,1,0:T(8,128)S(1)}, f32[2,17,640]{2,1,0:T(8,128)S(1)}, u32[]{:S(2)}, u32[]{:S(2)}) collective-permute-start(f32[2,17,640]{2,1,0:T(8,128)S(1)} %pad_maximum_fusion.1), channel_id=1, source_target_pairs={{1,0},{2,1},{3,2},{4,3},{5,4},{6,5},{7,6},{9,8},{10,9},{11,10},{12... | collective-permute-start | bytes 261128 | tf_op jit(solution)/shard_map/ppermute | solution.py:538
  7.6 1.0 fusion.mask_ref
  8.6 1.9 %survey.1 = (s32[32,1408]{1,0:T(8,128)S(1)}, s32[32,1280]{1,0:T(8,128)}, s32[32,128]{1,0:T(8,128)}, s32[32,128]{1,0:T(8,128)S(1)}, f32[64,640]{1,0:T(8,128)}) custom-call(f32[68,640]{1,0:T(8,128)S(1)} %fusion.mask_ref), custom_call_target="tpu_custom_call" | custom-call | flops 20000000 | bytes 500000 | tf_op jit(solution)/shard_map/survey/pallas_call | solution.py:560
  10.5 0.0 copy-done.1
  10.5 0.0 copy-start.4
  10.5 0.0 copy-start.8
  10.6 0.0 copy-start.9
  10.6 1.5 prepare_0.1
  12.1 0.0 collective-permute-done.before_ref
  12.1 0.0 collective-permute-done.1.after_ref
  12.1 0.0 copy-done.4
  12.1 0.0 copy-done.8
  12.2 0.0 copy-done.9
  12.2 5.9 %forecast_0.1 = (f32[32,9,8,128]{3,2,1,0:T(8,128)}, f32[32,2,8,128]{3,2,1,0:T(8,128)}, f32[8,128]{1,0:T(8,128)S(1)}) custom-call(f32[64,8,640]{2,1,0:T(8,128)S(1)} %get-tuple-element.42.turned, f32[64,8,640]{2,1,0:T(8,128)S(1)} %get-tuple-element.43.wet, f32[64,8,640]{2,1,0:T(8,128)S(1)} %get-tuple-element.44.source, ...), custom_call_target="tpu_custom_call" | custom-call | flops 40000000 | bytes 3000000 | tf_op jit(solution)/shard_map/forecast_0/pallas_call | solution.py:614
  18.1 11.3 %all-to-all-start.2 = ((f32[32,9,8,128]{3,2,1,0:T(8,128)}), f32[32,9,8,128]{3,2,1,0:T(8,128)S(1)}, u32[]{:S(2)}, u32[]{:S(2)}) async-start(f32[32,9,8,128]{3,2,1,0:T(8,128)} %get-tuple-element.49), calls=%async_computation.2 | async-start | bytes 2359296 | tf_op jit(solution)/shard_map/all_to_all | solution.py:628
  29.4 1.6 prepare_1.1
  31.0 0.0 copy-start.5
  31.1 0.0 copy-start.6
  31.1 0.0 copy-start.10
  31.1 5.5 %forecast_1.1 = (f32[32,10,8,128]{3,2,1,0:T(8,128)}, f32[32,2,8,128]{3,2,1,0:T(8,128)}) custom-call(f32[64,8,640]{2,1,0:T(8,128)S(1)} %get-tuple-element.51.turned, f32[64,8,640]{2,1,0:T(8,128)S(1)} %get-tuple-element.52.wet, f32[64,8,640]{2,1,0:T(8,128)S(1)} %get-tuple-element.53.source, f32[68,8,640]{2,1,0:T(8,128)S(1)} %get-tuple-element.54.sea8, ...), custom_call_target="tpu_custom_call" | custom-call | flops 40000000 | bytes 3000000 | tf_op jit(solution)/shard_map/forecast_1/pallas_call | solution.py:614
  36.6 24.3 %all-to-all-done.2.held_ref.data0_ref = f32[32,9,8,128]{3,2,1,0:T(8,128)S(1)} async-done(((f32[32,9,8,128]{3,2,1,0:T(8,128)}), f32[32,9,8,128]{3,2,1,0:T(8,128)S(1)}, u32[]{:S(2)}, u32[]{:S(2)}) %all-to-all-start.2) | async-done | bytes 1179680 | tf_op jit(solution)/shard_map/all_to_all | solution.py:628
  60.9 0.0 copy-done.5
  60.9 0.0 copy-done.6
  60.9 0.0 copy-done.10
  60.9 1.7 gram.1
  62.6 5.2 %all-to-all-start.3 = ((f32[32,10,8,128]{3,2,1,0:T(8,128)}), f32[32,10,8,128]{3,2,1,0:T(8,128)S(1)}, u32[]{:S(2)}, u32[]{:S(2)}) async-start(f32[32,10,8,128]{3,2,1,0:T(8,128)} %gram.1), calls=%async_computation.3 | async-start | bytes 2621440 | tf_op jit(solution)/shard_map/all_to_all | solution.py:628
  67.8 0.0 copy-start.12
  67.8 1.5 reduce_sum.18
  69.3 0.1 reshape.19
  69.5 0.1 reduce_sum.19
  69.6 0.6 reduce_max.9
  70.8 0.0 copy-done.12
  70.8 1.0 constant_dynamic-update-slice_fusion
  71.8 29.6 %all-to-all-done.3.data1_ref = f32[32,10,8,128]{3,2,1,0:T(8,128)S(1)} async-done(((f32[32,10,8,128]{3,2,1,0:T(8,128)}), f32[32,10,8,128]{3,2,1,0:T(8,128)S(1)}, u32[]{:S(2)}, u32[]{:S(2)}) %all-to-all-start.3) | async-done | bytes 1310752 | tf_op jit(solution)/shard_map/all_to_all | solution.py:628
  101.4 4.3 %mix.1 = (f32[32,18,8,128]{3,2,1,0:T(8,128)}, bf16[256,256]{1,0:T(8,128)(2,1)S(1)}, bf16[256,256]{1,0:T(8,128)(2,1)S(1)}) custom-call(f32[32,9,8,128]{3,2,1,0:T(8,128)S(1)} %all-to-all-done.2.held_ref.data0_ref, f32[32,10,8,128]{3,2,1,0:T(8,128)S(1)} %all-to-all-done.3.data1_ref), custom_call_target="tpu_custom_call" | custom-call | tf_op jit(solution)/shard_map/mix/pallas_call | solution.py:650
  105.8 0.0 copy-start.11
  105.8 1.6 copy-done.11
  107.4 0.0 copy-start
  107.4 62.4 %all_to_all.25 = f32[32,18,8,128]{3,2,1,0:T(8,128)S(1)} all-to-all(f32[32,18,8,128]{3,2,1,0:T(8,128)S(1)} %copy-done.11), channel_id=1, replica_groups=mesh['member'=32,'domain'=8] {'member'}, dimensions={0} | all-to-all | bytes 4718592 | tf_op jit(solution)/shard_map/all_to_all | solution.py:628
  169.8 0.0 copy-done
  169.8 0.0 copy-done.2
  169.8 0.0 copy-done.3
  169.8 0.0 copy-done.7
  169.8 4.1 %settle.1 = f32[1,2,8,64,640]{4,3,2,1,0:T(8,128)} custom-call(s32[32,128]{1,0:T(8,128)S(1)} %copy-done.7, f32[576,8,128]{2,1,0:T(8,128)S(1)} %bitcast.15, f32[32,4,8,128]{3,2,1,0:T(8,128)S(1)} %get-tuple-element.68.refs_1_, s32[32,1280]{1,0:T(8,128)S(1)} %copy-done.2, f32[64,640]{1,0:T(8,128)S(1)} %copy-done.3, f32[1,2,8,64,640]{4,3,2,1,0:T(8,128)S(1)} %copy-done), custom_call_target="tpu_custom_call" | custom-call | tf_op jit(solution)/shard_map/settle/pallas_call | solution.py:686
  (9 shorter events, 0.1 us)
Async XLA Ops:
  1.1 9.4 %copy-start.1 = (f32[1,2,64,640]{3,2,1,0:T(8,128)S(1)}, f32[1,2,64,640]{3,2,1,0:T(8,128)}, u32[]{:S(2)}) copy-start(f32[1,2,64,640]{3,2,1,0:T(8,128)} %flux_ref.3) | copy-start | bytes 983044
  2.0 10.1 %collective-permute-start = (f32[2,17,640]{2,1,0:T(8,128)S(1)}, f32[2,17,640]{2,1,0:T(8,128)S(1)}, u32[]{:S(2)}, u32[]{:S(2)}) collective-permute-start(f32[2,17,640]{2,1,0:T(8,128)S(1)} %pad_maximum_fusion), channel_id=1, source_target_pairs={{0,1},{1,2},{2,3},{3,4},{4,5},{5,6},{6,7},{8,9},{9,10},{10,11},{11... | collective-permute-start | bytes 261128 | tf_op jit(solution)/shard_map/ppermute | solution.py:537
  4.0 8.1 %collective-permute-start.1 = (f32[2,17,640]{2,1,0:T(8,128)S(1)}, f32[2,17,640]{2,1,0:T(8,128)S(1)}, u32[]{:S(2)}, u32[]{:S(2)}) collective-permute-start(f32[2,17,640]{2,1,0:T(8,128)S(1)} %pad_maximum_fusion.1), channel_id=1, source_target_pairs={{1,0},{2,1},{3,2},{4,3},{5,4},{6,5},{7,6},{9,8},{10,9},{11,10},{12... | collective-permute-start | bytes 261128 | tf_op jit(solution)/shard_map/ppermute | solution.py:538
  10.5 1.6 copy-start.4
  10.5 1.6 copy-start.8
  10.6 1.6 copy-start.9
  18.1 42.8 %all-to-all-start.2 = ((f32[32,9,8,128]{3,2,1,0:T(8,128)}), f32[32,9,8,128]{3,2,1,0:T(8,128)S(1)}, u32[]{:S(2)}, u32[]{:S(2)}) async-start(f32[32,9,8,128]{3,2,1,0:T(8,128)} %get-tuple-element.49), calls=%async_computation.2 | async-start | bytes 2359296 | tf_op jit(solution)/shard_map/all_to_all | solution.py:628
  31.0 29.8 %copy-start.5 = (f32[1,32,256]{2,1,0:T(8,128)S(1)}, f32[1,32,256]{2,1,0:T(8,128)}, u32[]{:S(2)}) copy-start(f32[1,32,256]{2,1,0:T(8,128)} %value_ref.1) | copy-start | bytes 98308
  31.1 29.8 %copy-start.6 = (f32[1,32,256]{2,1,0:T(8,128)S(1)}, f32[1,32,256]{2,1,0:T(8,128)}, u32[]{:S(2)}) copy-start(f32[1,32,256]{2,1,0:T(8,128)} %error_ref.1) | copy-start | bytes 98308
  31.1 29.8 %copy-start.10 = (s32[1,32]{1,0:T(1,128)S(1)}, s32[1,32]{1,0:T(1,128)}, u32[]{:S(2)}) copy-start(s32[1,32]{1,0:T(1,128)} %count_ref.1) | copy-start | bytes 388
  62.6 38.8 %all-to-all-start.3 = ((f32[32,10,8,128]{3,2,1,0:T(8,128)}), f32[32,10,8,128]{3,2,1,0:T(8,128)S(1)}, u32[]{:S(2)}, u32[]{:S(2)}) async-start(f32[32,10,8,128]{3,2,1,0:T(8,128)} %gram.1), calls=%async_computation.3 | async-start | bytes 2621440 | tf_op jit(solution)/shard_map/all_to_all | solution.py:628
  67.8 3.0 %copy-start.12 = (f32[32,2,8,128]{3,2,1,0:T(8,128)S(1)}, f32[32,2,8,128]{3,2,1,0:T(8,128)}, u32[]{:S(2)}) copy-start(f32[32,2,8,128]{3,2,1,0:T(8,128)} %get-tuple-element.58) | copy-start | bytes 786436
  105.8 1.7 copy-start.11
  107.4 62.4 %copy-start = (f32[1,2,8,64,640]{4,3,2,1,0:T(8,128)S(1)}, f32[1,2,8,64,640]{4,3,2,1,0:T(8,128)}, u32[]{:S(2)}) copy-start(f32[1,2,8,64,640]{4,3,2,1,0:T(8,128)} %refs_4_.1) | copy-start | bytes 7864324
  107.4 62.4 %copy-start.2 = (s32[32,1280]{1,0:T(8,128)S(1)}, s32[32,1280]{1,0:T(8,128)}, u32[]{:S(2)}) copy-start(s32[32,1280]{1,0:T(8,128)} %get-tuple-element.62.refs_2_) | copy-start | bytes 491524
  107.4 62.4 %copy-start.3 = (f32[64,640]{1,0:T(8,128)S(1)}, f32[64,640]{1,0:T(8,128)}, u32[]{:S(2)}) copy-start(f32[64,640]{1,0:T(8,128)} %get-tuple-element.63.refs_3_) | copy-start | bytes 491524
  107.4 62.4 %copy-start.7 = (s32[32,128]{1,0:T(8,128)S(1)}, s32[32,128]{1,0:T(8,128)}, u32[]{:S(2)}) copy-start(s32[32,128]{1,0:T(8,128)} %get-tuple-element.41.first_ref) | copy-start | bytes 49156

commit v5 on v4

--- a/solution.py
+++ b/solution.py
@@ -22,11 +22,9 @@
     return jnp.broadcast_to(row, (LEVELS, row.shape[1]))
 
 
-def survey_kernel(mask_ref, cell_ref, place_ref, first_ref, head_ref, sea_ref):
-    tiles, cells = place_ref.shape
+def ranked(mask_ref, tiles, cells):
     rows = 2 * tiles
     blocks = cells // LANES
-    sea_ref[...] = mask_ref[HALO : HALO + rows, :]
     sea = mask_ref[HALO : HALO + rows, :].astype(jnp.bfloat16)
     pick = lax.broadcasted_iota(jnp.int32, (tiles, rows), 1) - 2 * lax.broadcasted_iota(
         jnp.int32, (tiles, rows), 0
@@ -52,23 +50,40 @@
         part = slice(b * tiles, (b + 1) * tiles)
         shifts.append(within[part] + offset)
         offset = offset + totals[part]
-    shift = jnp.concatenate(shifts, axis=1).astype(jnp.int32)
-    cell = lax.broadcasted_iota(jnp.int32, (tiles, cells), 1)
-    rank = cell - shift
+    return sea, jnp.concatenate(shifts, axis=1).astype(jnp.int32)
+
+
+def placed_cells(sea, shift):
+    rank = lax.broadcasted_iota(jnp.int32, shift.shape, 1) - shift
     place = jnp.where(rank < ROOM, rank, rank + TAIL)
-    place_ref[...] = jnp.where(sea > 0.0, place, -1)
+    return place, jnp.where(sea > 0.0, place, -1)
+
+
+def spilling(marked, shape):
+    last = jnp.max(jnp.max(marked, axis=1, keepdims=True), axis=0, keepdims=True)
+    return (jnp.broadcast_to(last, shape) >= PACKED * LANES).astype(jnp.int32)
+
+
+def locate_kernel(mask_ref, _, place_ref, first_ref, sea_ref):
+    tiles, cells = place_ref.shape
+    sea_ref[...] = mask_ref[HALO : HALO + 2 * tiles, :]
+    place, marked = placed_cells(*ranked(mask_ref, tiles, cells))
+    place_ref[...] = marked
     lane = lax.broadcasted_iota(jnp.int32, first_ref.shape, 1)
     first = jnp.zeros(first_ref.shape, jnp.int32)
-    for b in range(blocks):
+    for b in range(cells // LANES):
         head = place[:, b * LANES : b * LANES + 1]
         head = (jnp.minimum(head >> 7, PACKED - 1) << 7) + (head & (LANES - 1))
         first = jnp.where(lane == b, jnp.broadcast_to(head, first.shape), first)
     number = lax.broadcasted_iota(jnp.int32, first.shape, 0)
     first = first + number * (FIELDS * PACKED * LANES)
-    last = jnp.max(jnp.where(sea > 0.0, place, -1), axis=1, keepdims=True)
-    last = jnp.broadcast_to(jnp.max(last, axis=0, keepdims=True), first.shape)
-    spills = (last >= PACKED * LANES).astype(jnp.int32)
-    first_ref[...] = jnp.where(lane == LANES - 1, spills, first)
+    first_ref[...] = jnp.where(lane == LANES - 1, spilling(marked, first.shape), first)
+
+
+def survey_kernel(mask_ref, cell_ref, head_ref):
+    tiles, cells = cell_ref.shape[0], 2 * mask_ref.shape[1]
+    sea, shift = ranked(mask_ref, tiles, cells)
+    cell = lax.broadcasted_iota(jnp.int32, shift.shape, 1)
     state = jnp.where(sea > 0.0, shift * 2048 + cell, 0)
     for bit in range(11):
         other = pltpu.roll(state, cells - (1 << bit), 1)
@@ -77,6 +92,8 @@
         state = jnp.where(comes, other, jnp.where(goes, 0, state))
     state = state & 2047
     heads = jnp.zeros(head_ref.shape, jnp.int32)
+    lane = lax.broadcasted_iota(jnp.int32, heads.shape, 1)
+    number = lax.broadcasted_iota(jnp.int32, heads.shape, 0)
     reach = jnp.zeros((tiles, 1), jnp.int32)
     for q in range(PACKED):
         part = state[:, q * LANES : (q + 1) * LANES]
@@ -85,7 +102,8 @@
     wide = jnp.max(reach, axis=0, keepdims=True)
     heads = heads + number * cells
     heads = jnp.where(lane == PACKED, jnp.broadcast_to(wide, heads.shape), heads)
-    head_ref[...] = jnp.where(lane == PACKED + 1, spills, heads)
+    _, marked = placed_cells(sea, shift)
+    head_ref[...] = jnp.where(lane == PACKED + 1, spilling(marked, heads.shape), heads)
     state = state + lax.broadcasted_iota(jnp.int32, state.shape, 0) * cells
     cell_ref[:, : PACKED * LANES] = state[:, : PACKED * LANES]
     cell_ref[:, PACKED * LANES :] = pltpu.roll(state, cells - ROOM, 1)[:, : SPILL * LANES]
@@ -301,7 +319,9 @@
         sent(g * 8, g).wait()
 
 
-def gram_kernel(tile_ref, held_ref, value_ref, error_ref, count_ref, _, out_ref, spread, sem):
+def gram_kernel(
+    tile_ref, held_ref, value_ref, error_ref, count_ref, _, out_ref, sums_ref, spread, sem
+):
     tile = tile_ref[0]
     members = held_ref.shape[0]
     halves = value_ref.shape[2] // LANES
@@ -335,6 +355,7 @@
     corner = (lane >= 16) & (lane < 32)
     packed = jnp.where(corner & (row == 0), pltpu.roll(pull, 16, 1), packed)
     packed = jnp.where(corner & (row == 1), pull, packed)
+    sums_ref[...] = packed
     for m in range(members):
         spread[m, 0] = packed
     copy = pltpu.make_async_copy(spread, out_ref.at[:, pl.ds(PACKED, 1)], sem)
@@ -404,11 +425,10 @@
         out_ref[:, to + b] = result[:, b * LANES : (b + 1) * LANES].reshape(members, LEVELS, LANES)
 
 
-def mix_kernel(data0_ref, data1_ref, out_ref, high, low, ready, sems):
-    members = data0_ref.shape[0]
+def widen(total, high, low):
+    members = total.shape[1] // 4
     deep = members * LEVELS
-
-    kernel = ensemble_kernel(jnp.sum(data1_ref[:, PACKED], axis=0), LANES)[:, :members]
+    kernel = ensemble_kernel(total, LANES)[:, :members]
     major = kernel.astype(jnp.bfloat16)
     minor = (kernel - major.astype(jnp.float32)).astype(jnp.bfloat16)
     spread = (
@@ -426,31 +446,37 @@
         )
         target[...] = jnp.where(same, full, 0.0).astype(jnp.bfloat16)
 
+
+def mix_kernel(data0_ref, data1_ref, out_ref, high, low):
+    widen(jnp.sum(data1_ref[:, PACKED], axis=0), high, low)
     blocks = 3
-
-    def leaving(to, n):
-        part = (slice(None), pl.ds(to, blocks))
-        return pltpu.make_async_copy(ready.at[part], out_ref.at[part], sems.at[n])
-
     for f, data_ref in ((0, data0_ref), (1, data1_ref)):
 
         def strip(i, _, f=f, data_ref=data_ref):
             at = i * blocks
-            to = f * PACKED + at
-            mix_strip(high, low, data_ref, at, ready, to, blocks)
-            leaving(to, f * (PACKED // blocks) + i).start()
+            mix_strip(high, low, data_ref, at, out_ref, f * PACKED + at, blocks)
             return 0
 
         lax.fori_loop(0, PACKED // blocks, strip, 0)
-    for n in range(FIELDS * PACKED // blocks):
-        leaving(n * blocks, n).wait()
-
-
-def spill_kernel(data_ref, high, low, out_ref):
+
+
+def spill_kernel(sums_ref, data_ref, out_ref, high, low):
+    widen(jnp.sum(sums_ref[:, 0], axis=0), high, low)
     mix_strip(high, low, data_ref, 0, out_ref, 0, data_ref.shape[1])
 
 
-def settle_rows(spilled, first_ref, back_ref, spill_ref, place_ref, sea_ref, x_ref, out_ref):
+def census_kernel(mask_ref, _, most_ref):
+    rows = jnp.sum(mask_ref[...].astype(jnp.float32), axis=1, keepdims=True)
+    rows = jnp.broadcast_to(rows, (rows.shape[0], LANES))
+    pairs = rows + pltpu.roll(rows, rows.shape[0] - 1, 0)
+    even = lax.broadcasted_iota(jnp.int32, pairs.shape, 0) % 2 == 0
+    most = jnp.max(jnp.where(even, pairs, 0.0), axis=0, keepdims=True)
+    most_ref[...] = jnp.broadcast_to(most, most_ref.shape)
+
+
+def settle_rows(
+    spilled, first_ref, back_ref, spill0_ref, spill1_ref, place_ref, sea_ref, x_ref, out_ref
+):
     blocks = out_ref.shape[4] // LANES
     start = pl.multiple_of(pl.program_id(0) * 8, 8)
     end = back_ref.shape[0] - 1
@@ -480,7 +506,7 @@
                         value = take(jnp.where(turn, low, high), lanes)
                         if spilled and (b + 1) * LANES > ROOM:
                             for o in range(SPILL):
-                                late = take(spill_ref[start + t, f * SPILL + o], lanes)
+                                late = take((spill0_ref, spill1_ref)[f][start + t, o], lanes)
                                 value = jnp.where(block == PACKED + o, late, value)
                         rows[f].append(value)
             here = pl.ds(pl.multiple_of(2 * start + half * 8, 8), 8)
@@ -553,21 +579,21 @@
     band = jax.ShapeDtypeStruct((rows, levels, width), f32)
     shell = jax.ShapeDtypeStruct((tall, levels, width), f32)
     i32 = jnp.int32
-    bulks = [pltpu.HBM((tiles, PACKED + f, levels, LANES), f32) for f in range(2)]
+    bulks = [
+        pltpu.HBM((tiles, PACKED, levels, LANES), f32),
+        jax.ShapeDtypeStruct((tiles, PACKED + 1, levels, LANES), f32),
+    ]
     extra = pltpu.HBM((tiles, SPILL, levels, LANES), f32)
     mark = jax.ShapeDtypeStruct((levels, LANES), f32)
 
-    cell, place, first, heads, sea = pl.pallas_call(
+    cell, heads = pl.pallas_call(
         survey_kernel,
         out_shape=[
             jax.ShapeDtypeStruct((tiles, (PACKED + SPILL) * LANES), i32),
-            pltpu.HBM((tiles, 2 * width), i32),
-            pltpu.HBM((tiles, LANES), i32),
             jax.ShapeDtypeStruct((tiles, LANES), i32),
-            pltpu.HBM((rows, width), f32),
         ],
         in_specs=[vmem],
-        out_specs=[vmem] * 5,
+        out_specs=[vmem] * 2,
         compiler_params=params(8),
         cost_estimate=pl.CostEstimate(
             flops=20_000_000, bytes_accessed=500_000, transcendentals=0
@@ -605,7 +631,7 @@
             pltpu.SemaphoreType.DMA((tiles // 8 + 1,)),
         ]
         out_shape = [bulks[field], extra]
-        out_specs = [hbm] * 2
+        out_specs = [hbm if field == 0 else anywhere, hbm]
         if field == 0:
             scratch.append(pltpu.VMEM((2, tiles, width), f32))
             scratch.append(pltpu.VMEM((tiles, levels, LANES), f32))
@@ -629,12 +655,27 @@
 
     sent0, spill0, done0 = forecast(0, prepare(0), obs_index)
     held0 = exchanged(sent0)
-    sent1, spill1 = forecast(1, prepare(1, done0))
-    sent1 = pl.pallas_call(
+    place, first, sea = pl.pallas_call(
+        locate_kernel,
+        out_shape=[
+            pltpu.HBM((tiles, 2 * width), i32),
+            pltpu.HBM((tiles, LANES), i32),
+            pltpu.HBM((rows, width), f32),
+        ],
+        in_specs=[vmem, anywhere],
+        out_specs=[vmem] * 3,
+        compiler_params=params(8),
+        cost_estimate=pl.CostEstimate(
+            flops=20_000_000, bytes_accessed=500_000, transcendentals=0
+        ),
+        name="locate",
+    )(mask, done0)
+    sent1, spill1 = forecast(1, prepare(1, first))
+    sent1, sums = pl.pallas_call(
         gram_kernel,
-        out_shape=bulks[1],
-        in_specs=[smem, vmem, vmem, vmem, smem, hbm],
-        out_specs=hbm,
+        out_shape=[bulks[1], mark],
+        in_specs=[smem, vmem, vmem, vmem, smem, anywhere],
+        out_specs=[anywhere, vmem],
         scratch_shapes=[
             pltpu.VMEM((tiles, 1, levels, LANES), f32),
             pltpu.SemaphoreType.DMA,
@@ -643,56 +684,64 @@
         compiler_params=params(4),
         name="gram",
     )(tile.reshape(1).astype(jnp.int32), held0, obs_value, obs_error, obs_count, sent1)
+    deep = members * levels
+    halves = [pltpu.VMEM((deep, deep), jnp.bfloat16)] * 2
+
+    def late(spill0, spill1, sums):
+        there = exchanged(jnp.concatenate([spill0, spill1], axis=1))
+        parts = exchanged(jnp.broadcast_to(sums[None, None], (members, 1, *sums.shape)))
+        there = pl.pallas_call(
+            spill_kernel,
+            out_shape=jax.ShapeDtypeStruct(there.shape, f32),
+            in_specs=[vmem] * 2,
+            out_specs=vmem,
+            scratch_shapes=halves,
+            compiler_params=params(16),
+            name="mix_spill",
+        )(parts, there)
+        there = exchanged(there)
+        return there[:, :SPILL], there[:, SPILL:]
+
+    def none(spill0, spill1, sums):
+        return spill0, spill1
+
+    most = pl.pallas_call(
+        census_kernel,
+        out_shape=jax.ShapeDtypeStruct((levels, LANES), f32),
+        in_specs=[vmem, anywhere],
+        out_specs=vmem,
+        compiler_params=params(4),
+        cost_estimate=pl.CostEstimate(
+            flops=10_000_000, bytes_accessed=1_300_000, transcendentals=0
+        ),
+        name="census",
+    )(land_mask, done0)
+    spill0, spill1 = lax.cond(most[0, 0] > ROOM, late, none, spill0, spill1, sums)
+    sent1, spill0, spill1 = lax.optimization_barrier((sent1, spill0, spill1))
     held1 = exchanged(sent1)
 
-    deep = members * levels
-    half = jax.ShapeDtypeStruct((deep, deep), jnp.bfloat16)
-    updated, high, low = pl.pallas_call(
+    updated = pl.pallas_call(
         mix_kernel,
-        out_shape=[
-            pltpu.HBM((members, fields * PACKED, levels, LANES), f32), half, half
-        ],
+        out_shape=jax.ShapeDtypeStruct((members, fields * PACKED, levels, LANES), f32),
         in_specs=[vmem, vmem],
-        out_specs=[hbm, vmem, vmem],
-        scratch_shapes=[
-            pltpu.VMEM((members, fields * PACKED, levels, LANES), f32),
-            pltpu.SemaphoreType.DMA((fields * PACKED // 3,)),
-        ],
+        out_specs=vmem,
+        scratch_shapes=halves,
         compiler_params=params(16),
         name="mix",
     )(held0, held1)
     back = exchanged(updated)
-
-    def late(spill, high, low):
-        there = exchanged(spill)
-        there = pl.pallas_call(
-            spill_kernel,
-            out_shape=jax.ShapeDtypeStruct(there.shape, f32),
-            in_specs=[vmem] * 3,
-            out_specs=vmem,
-            compiler_params=params(16),
-            name="mix_spill",
-        )(there, high, low)
-        return exchanged(there)
-
-    def none(spill, high, low):
-        return spill
-
-    ocean = jnp.sum(land_mask, axis=1).reshape(-1, 2).sum(axis=1)
-    spill = jnp.concatenate([spill0, spill1], axis=1)
-    spill = lax.cond(jnp.max(ocean) > ROOM, late, none, spill, high, low)
 
     bands = pl.BlockSpec((1, fields, levels, 16, width), lambda i: (0, 0, 0, i, 0))
     return pl.pallas_call(
         settle_kernel,
         grid=(rows // 16,),
         out_shape=jax.ShapeDtypeStruct(starting_tracer_fields.shape, f32),
-        in_specs=[smem] + [vmem] * 5,
+        in_specs=[smem] + [vmem] * 6,
         out_specs=bands,
         compiler_params=params(12),
         name="settle",
     )(
-        first, back.reshape(-1, levels, LANES), spill, place, sea, starting_tracer_fields,
+        first, back.reshape(-1, levels, LANES), spill0, spill1, place, sea, starting_tracer_fields,
     )
 
 

time: 175 us -> 171 us (0.977)
  blocking collectives: 62.4 us -> 101 us
  waiting for transfers between devices: 53.9 us -> 21.9 us
  starting transfers between devices: 22.1 us -> 17 us
  other arithmetic: 3.25 us -> 0.99 us
    all_to_all x1 -> x2, blocking collectives: 62.4 us -> 101 us  [exchanged(): lax.all_to_all(array, 'member', split_axis=0, concat_axis=0, tiled=True)]
    all_to_all x2 -> x1, waiting for transfers between devices: 53.9 us -> 21.9 us  [exchanged(): lax.all_to_all(array, 'member', split_axis=0, concat_axis=0, tiled=True)]
    all_to_all x2 -> x1, starting transfers between devices: 16.5 us -> 11.5 us  [exchanged(): lax.all_to_all(array, 'member', split_axis=0, concat_axis=0, tiled=True)]
    pallas_call x2 -> x4, Pallas kernels: 6.02 us -> 5.93 us  [the longest x1 3.51 us: shards(): pl.pallas_call(mix_kernel, out_shape=jax.ShapeDtypeStruct((members, field...]
  transfers between devices with their start and end apart: 4 -> 3, of which waited for: 2 -> 1; matrix products, arithmetic and copies ran while one was open for 3% -> 1% of each run, Pallas kernels for 6% -> 6%
where the time goes in v5:
time: 171 us
  blocking collectives  101 us (59%)
  Pallas kernels  25.6 us (15%)
  waiting for transfers between devices  21.9 us (13%)
  starting transfers between devices  17 us (10%)
  local copies, waits for them, and re-layouts  3.27 us (2%)
    all_to_all x2, blocking collectives, exchanged(): lax.all_to_all(array, 'member', split_axis=0, concat_axis=0, tiled=True)  101 us
    all_to_all x1, waiting for transfers between devices, exchanged(): lax.all_to_all(array, 'member', split_axis=0, concat_axis=0, tiled=True)  21.9 us
    all_to_all x1, starting transfers between devices, exchanged(): lax.all_to_all(array, 'member', split_axis=0, concat_axis=0, tiled=True)  11.5 us
    pallas_call x2, Pallas kernels, forecast(): pl.pallas_call(functools.partial(forecast_kernel, field), out_shape=out_s...  10.9 us
    pallas_call x1, Pallas kernels, shards(): pl.pallas_call(settle_kernel, grid=(rows // 16,), out_shape=jax.ShapeDtyp...  4.24 us
    ppermute x1, starting transfers between devices, shards(): after = lax.ppermute(edge(0, 0), 'domain', down)  3.64 us
    pallas_call x1, Pallas kernels, shards(): pl.pallas_call(mix_kernel, out_shape=jax.ShapeDtypeStruct((members, field...  3.51 us
  transfers between devices with their start and end apart: 3, of which 1 were waited for; matrix products, arithmetic and copies ran while one was open for 1% of the time, Pallas kernels for 6%

profile of v5, /device:TPU:8, one launch (start us, length us, event | category | flops | bytes accessed | tf_op | source)
XLA Modules:
  0.0 170.9 jit_solution(195681866640881215)
XLA Ops:
  0.0 0.8 fusion.2
  0.8 0.0 copy-start.2
  0.8 1.2 slice_bitcast_fusion
  2.0 1.9 %collective-permute-start = (f32[2,17,640]{2,1,0:T(8,128)S(1)}, f32[2,17,640]{2,1,0:T(8,128)S(1)}, u32[]{:S(2)}, u32[]{:S(2)}) collective-permute-start(f32[2,17,640]{2,1,0:T(8,128)S(1)} %pad_maximum_fusion.1), channel_id=1, source_target_pairs={{0,1},{1,2},{2,3},{3,4},{4,5},{5,6},{6,7},{8,9},{9,10},{10,11},{11... | collective-permute-start | bytes 261128 | tf_op jit(solution)/shard_map/ppermute | solution.py:563
  4.0 3.6 %collective-permute-start.1 = (f32[2,17,640]{2,1,0:T(8,128)S(1)}, f32[2,17,640]{2,1,0:T(8,128)S(1)}, u32[]{:S(2)}, u32[]{:S(2)}) collective-permute-start(f32[2,17,640]{2,1,0:T(8,128)S(1)} %pad_maximum_fusion.2), channel_id=1, source_target_pairs={{1,0},{2,1},{3,2},{4,3},{5,4},{6,5},{7,6},{9,8},{10,9},{11,10},{12... | collective-permute-start | bytes 261128 | tf_op jit(solution)/shard_map/ppermute | solution.py:564
  7.7 1.0 fusion.mask_ref
  8.6 1.3 survey.1
  9.9 0.0 copy-done.2
  9.9 0.0 copy-start.10
  10.0 0.0 copy-start.11
  10.0 1.5 prepare_0.1
  11.5 0.0 collective-permute-done.before_ref
  11.5 0.0 collective-permute-done.1.after_ref
  11.5 0.0 copy-done.7
  11.6 0.0 copy-done.10
  11.6 0.0 copy-done.11
  11.6 5.9 %forecast_0.1 = (f32[32,9,8,128]{3,2,1,0:T(8,128)}, f32[32,2,8,128]{3,2,1,0:T(8,128)}, f32[8,128]{1,0:T(8,128)S(1)}) custom-call(f32[64,8,640]{2,1,0:T(8,128)S(1)} %get-tuple-element.45.turned, f32[64,8,640]{2,1,0:T(8,128)S(1)} %get-tuple-element.46.wet, f32[64,8,640]{2,1,0:T(8,128)S(1)} %get-tuple-element.47.source, ...), custom_call_target="tpu_custom_call" | custom-call | flops 40000000 | bytes 3000000 | tf_op jit(solution)/shard_map/forecast_0/pallas_call | solution.py:640
  17.5 0.0 copy-start.1
  17.5 11.5 %all-to-all-start.3 = ((f32[32,9,8,128]{3,2,1,0:T(8,128)}), f32[32,9,8,128]{3,2,1,0:T(8,128)S(1)}, u32[]{:S(2)}, u32[]{:S(2)}) async-start(f32[32,9,8,128]{3,2,1,0:T(8,128)} %get-tuple-element.54), calls=%async_computation.3 | async-start | bytes 2359296 | tf_op jit(solution)/shard_map/all_to_all | solution.py:654
  29.0 0.0 copy-done.1
  29.0 0.2 census.1
  29.1 0.5 slice.25
  30.2 1.2 locate.1
  31.4 0.7 copy-done.5
  32.1 1.6 prepare_1.1
  33.7 0.0 copy-start.8
  33.7 0.0 copy-start.9
  33.8 0.0 copy-start.12
  33.8 5.1 %forecast_1.1 = (f32[32,10,8,128]{3,2,1,0:T(8,128)S(1)}, f32[32,2,8,128]{3,2,1,0:T(8,128)}) custom-call(f32[64,8,640]{2,1,0:T(8,128)S(1)} %get-tuple-element.55.turned, f32[64,8,640]{2,1,0:T(8,128)S(1)} %get-tuple-element.56.wet, f32[64,8,640]{2,1,0:T(8,128)S(1)} %get-tuple-element.57.source, f32[68,8,640]{2,1,0:T(8,128)S(1)} %get-tuple-element.58.sea8, ...), custom_call_target="tpu_custom_call" | custom-call | flops 40000000 | bytes 3000000 | tf_op jit(solution)/shard_map/forecast_1/pallas_call | solution.py:640
  38.8 0.0 copy-start.13
  38.8 21.9 %all-to-all-done.3.held_ref.data0_ref = f32[32,9,8,128]{3,2,1,0:T(8,128)S(1)} async-done(((f32[32,9,8,128]{3,2,1,0:T(8,128)}), f32[32,9,8,128]{3,2,1,0:T(8,128)S(1)}, u32[]{:S(2)}, u32[]{:S(2)}) %all-to-all-start.3) | async-done | bytes 1179680 | tf_op jit(solution)/shard_map/all_to_all | solution.py:654
  60.7 0.0 copy-done.8
  60.7 0.0 copy-done.9
  60.7 0.0 copy-done.12
  60.7 1.0 gram.1
  61.8 0.0 copy-done.13
  61.8 39.7 %all_to_all.29.data1_ref = f32[32,10,8,128]{3,2,1,0:T(8,128)S(1)} all-to-all(f32[32,10,8,128]{3,2,1,0:T(8,128)S(1)} %get-tuple-element.67), channel_id=1, replica_groups=mesh['member'=32,'domain'=8] {'member'}, dimensions={0} | all-to-all | bytes 2621440 | tf_op jit(solution)/shard_map/all_to_all | solution.py:654
  101.5 3.5 %mix.1 = f32[32,18,8,128]{3,2,1,0:T(8,128)S(1)} custom-call(f32[32,9,8,128]{3,2,1,0:T(8,128)S(1)} %all-to-all-done.3.held_ref.data0_ref, f32[32,10,8,128]{3,2,1,0:T(8,128)S(1)} %all_to_all.29.data1_ref), custom_call_target="tpu_custom_call" | custom-call | tf_op jit(solution)/shard_map/mix/pallas_call | solution.py:723
  105.0 0.0 copy-start
  105.0 0.0 copy-start.3
  105.1 0.0 copy-start.4
  105.1 0.0 copy-start.6
  105.1 61.6 %all_to_all.30 = f32[32,18,8,128]{3,2,1,0:T(8,128)S(1)} all-to-all(f32[32,18,8,128]{3,2,1,0:T(8,128)S(1)} %mix.1), channel_id=1, replica_groups=mesh['member'=32,'domain'=8] {'member'}, dimensions={0} | all-to-all | bytes 4718592 | tf_op jit(solution)/shard_map/all_to_all | solution.py:654
  166.6 0.0 copy-done
  166.6 0.0 copy-done.3
  166.6 0.0 copy-done.4
  166.6 0.0 copy-done.6
  166.6 4.2 %settle.1 = f32[1,2,8,64,640]{4,3,2,1,0:T(8,128)} custom-call(s32[32,128]{1,0:T(8,128)S(1)} %copy-done.6, f32[576,8,128]{2,1,0:T(8,128)S(1)} %bitcast.16, f32[32,2,8,128]{3,2,1,0:T(8,128)S(1)} %get-tuple-element.68.refs_1_, f32[32,2,8,128]{3,2,1,0:T(8,128)} %get-tuple-element.69.refs_2_, s32[32,1280]{1,0:T(8,128)S(1)} %copy-done.3, f32[64,640]{1,0:T(8,128)S(1)} %copy-done.4, ...), custom_call_target="tpu_custom_call" | custom-call | tf_op jit(solution)/shard_map/settle/pallas_call | solution.py:735
  (7 shorter events, 0.1 us)
Async XLA Ops:
  0.8 9.1 %copy-start.2 = (f32[1,2,64,640]{3,2,1,0:T(8,128)S(1)}, f32[1,2,64,640]{3,2,1,0:T(8,128)}, u32[]{:S(2)}) copy-start(f32[1,2,64,640]{3,2,1,0:T(8,128)} %flux_ref.3) | copy-start | bytes 983044
  2.0 9.5 %collective-permute-start = (f32[2,17,640]{2,1,0:T(8,128)S(1)}, f32[2,17,640]{2,1,0:T(8,128)S(1)}, u32[]{:S(2)}, u32[]{:S(2)}) collective-permute-start(f32[2,17,640]{2,1,0:T(8,128)S(1)} %pad_maximum_fusion.1), channel_id=1, source_target_pairs={{0,1},{1,2},{2,3},{3,4},{4,5},{5,6},{6,7},{8,9},{9,10},{10,11},{11... | collective-permute-start | bytes 261128 | tf_op jit(solution)/shard_map/ppermute | solution.py:563
  4.0 7.5 %collective-permute-start.1 = (f32[2,17,640]{2,1,0:T(8,128)S(1)}, f32[2,17,640]{2,1,0:T(8,128)S(1)}, u32[]{:S(2)}, u32[]{:S(2)}) collective-permute-start(f32[2,17,640]{2,1,0:T(8,128)S(1)} %pad_maximum_fusion.2), channel_id=1, source_target_pairs={{1,0},{2,1},{3,2},{4,3},{5,4},{6,5},{7,6},{9,8},{10,9},{11,10},{12... | collective-permute-start | bytes 261128 | tf_op jit(solution)/shard_map/ppermute | solution.py:564
  9.9 1.6 copy-start.7
  9.9 1.6 copy-start.10
  10.0 1.6 copy-start.11
  17.5 11.5 %copy-start.1 = (s32[512,640]{1,0:T(8,128)S(1)}, s32[512,640]{1,0:T(8,128)}, u32[]{:S(2)}) copy-start(s32[512,640]{1,0:T(8,128)} %mask_ref.1) | copy-start | bytes 3932164
  17.5 43.2 %all-to-all-start.3 = ((f32[32,9,8,128]{3,2,1,0:T(8,128)}), f32[32,9,8,128]{3,2,1,0:T(8,128)S(1)}, u32[]{:S(2)}, u32[]{:S(2)}) async-start(f32[32,9,8,128]{3,2,1,0:T(8,128)} %get-tuple-element.54), calls=%async_computation.3 | async-start | bytes 2359296 | tf_op jit(solution)/shard_map/all_to_all | solution.py:654
  31.4 0.7 copy-start.5
  33.7 27.0 %copy-start.8 = (f32[1,32,256]{2,1,0:T(8,128)S(1)}, f32[1,32,256]{2,1,0:T(8,128)}, u32[]{:S(2)}) copy-start(f32[1,32,256]{2,1,0:T(8,128)} %value_ref.1) | copy-start | bytes 98308
  33.7 27.0 %copy-start.9 = (f32[1,32,256]{2,1,0:T(8,128)S(1)}, f32[1,32,256]{2,1,0:T(8,128)}, u32[]{:S(2)}) copy-start(f32[1,32,256]{2,1,0:T(8,128)} %error_ref.1) | copy-start | bytes 98308
  33.8 27.0 %copy-start.12 = (s32[1,32]{1,0:T(1,128)S(1)}, s32[1,32]{1,0:T(1,128)}, u32[]{:S(2)}) copy-start(s32[1,32]{1,0:T(1,128)} %count_ref.1) | copy-start | bytes 388
  38.8 23.0 %copy-start.13 = (f32[32,2,8,128]{3,2,1,0:T(8,128)S(1)}, f32[32,2,8,128]{3,2,1,0:T(8,128)}, u32[]{:S(2)}) copy-start(f32[32,2,8,128]{3,2,1,0:T(8,128)} %get-tuple-element.62) | copy-start | bytes 786436
  105.0 61.6 %copy-start = (f32[1,2,8,64,640]{4,3,2,1,0:T(8,128)S(1)}, f32[1,2,8,64,640]{4,3,2,1,0:T(8,128)}, u32[]{:S(2)}) copy-start(f32[1,2,8,64,640]{4,3,2,1,0:T(8,128)} %refs_5_.1) | copy-start | bytes 7864324
  105.0 61.6 %copy-start.3 = (s32[32,1280]{1,0:T(8,128)S(1)}, s32[32,1280]{1,0:T(8,128)}, u32[]{:S(2)}) copy-start(s32[32,1280]{1,0:T(8,128)} %get-tuple-element.70.refs_3_) | copy-start | bytes 491524
  105.1 61.6 %copy-start.4 = (f32[64,640]{1,0:T(8,128)S(1)}, f32[64,640]{1,0:T(8,128)}, u32[]{:S(2)}) copy-start(f32[64,640]{1,0:T(8,128)} %get-tuple-element.71.refs_4_) | copy-start | bytes 491524
  105.1 61.6 %copy-start.6 = (s32[32,128]{1,0:T(8,128)S(1)}, s32[32,128]{1,0:T(8,128)}, u32[]{:S(2)}) copy-start(s32[32,128]{1,0:T(8,128)} %get-tuple-element.53.rest_0_.first_ref) | copy-start | bytes 49156

commit v6 on v5

--- a/solution.py
+++ b/solution.py
@@ -11,7 +11,7 @@
 LEVELS = 8
 LANES = 128
 HALO = 2
-UNROLL = 10
+UNROLL = 20
 PACKED = 9
 TAIL = 32
 ROOM = PACKED * LANES - TAIL
@@ -449,7 +449,7 @@
 
 def mix_kernel(data0_ref, data1_ref, out_ref, high, low):
     widen(jnp.sum(data1_ref[:, PACKED], axis=0), high, low)
-    blocks = 3
+    blocks = PACKED
     for f, data_ref in ((0, data0_ref), (1, data1_ref)):
 
         def strip(i, _, f=f, data_ref=data_ref):

time: 171 us -> 170 us (level)
  no operation moved by 1% of the time
where the time goes in v6:
time: 170 us; the launch traced here: 169 us
  blocking collectives  101 us (59%)
  Pallas kernels  23.9 us (14%)
  waiting for transfers between devices  22.2 us (13%)
  starting transfers between devices  17 us (10%)
  local copies, waits for them, and re-layouts  3.27 us (2%)
    all_to_all x2, blocking collectives, exchanged(): lax.all_to_all(array, 'member', split_axis=0, concat_axis=0, tiled=True)  101 us
    all_to_all x1, waiting for transfers between devices, exchanged(): lax.all_to_all(array, 'member', split_axis=0, concat_axis=0, tiled=True)  22.2 us
    all_to_all x1, starting transfers between devices, exchanged(): lax.all_to_all(array, 'member', split_axis=0, concat_axis=0, tiled=True)  11.5 us
    pallas_call x2, Pallas kernels, forecast(): pl.pallas_call(functools.partial(forecast_kernel, field), out_shape=out_s...  10.4 us
    pallas_call x1, Pallas kernels, shards(): pl.pallas_call(settle_kernel, grid=(rows // 16,), out_shape=jax.ShapeDtyp...  4.24 us
    ppermute x1, starting transfers between devices, shards(): after = lax.ppermute(edge(0, 0), 'domain', down)  3.64 us
  transfers between devices with their start and end apart: 3, of which 1 were waited for; matrix products, arithmetic and copies ran while one was open for 1% of the time, Pallas kernels for 6%

profile of v6, /device:TPU:8, one launch (start us, length us, event | category | flops | bytes accessed | tf_op | source)
XLA Modules:
  0.0 169.5 jit_solution(14528442367497334216)
XLA Ops:
  0.0 0.8 fusion.2
  0.8 1.2 slice_bitcast_fusion
  2.0 1.9 %collective-permute-start = (f32[2,17,640]{2,1,0:T(8,128)S(1)}, f32[2,17,640]{2,1,0:T(8,128)S(1)}, u32[]{:S(2)}, u32[]{:S(2)}) collective-permute-start(f32[2,17,640]{2,1,0:T(8,128)S(1)} %pad_maximum_fusion.1), channel_id=1, source_target_pairs={{0,1},{1,2},{2,3},{3,4},{4,5},{5,6},{6,7},{8,9},{9,10},{10,11},{11... | collective-permute-start | bytes 261128 | tf_op jit(solution)/shard_map/ppermute | solution.py:563
  4.0 3.6 %collective-permute-start.1 = (f32[2,17,640]{2,1,0:T(8,128)S(1)}, f32[2,17,640]{2,1,0:T(8,128)S(1)}, u32[]{:S(2)}, u32[]{:S(2)}) collective-permute-start(f32[2,17,640]{2,1,0:T(8,128)S(1)} %pad_maximum_fusion.2), channel_id=1, source_target_pairs={{1,0},{2,1},{3,2},{4,3},{5,4},{6,5},{7,6},{9,8},{10,9},{11,10},{12... | collective-permute-start | bytes 261128 | tf_op jit(solution)/shard_map/ppermute | solution.py:564
  7.7 1.0 fusion.mask_ref
  8.6 1.3 survey.1
  9.9 0.0 copy-done.2
  9.9 0.0 copy-start.7
  9.9 0.0 copy-start.10
  10.0 0.0 copy-start.11
  10.0 1.5 prepare_0.1
  11.5 0.0 collective-permute-done.before_ref
  11.5 0.0 collective-permute-done.1.after_ref
  11.5 0.0 copy-done.7
  11.6 0.0 copy-done.10
  11.6 0.0 copy-done.11
  11.6 5.7 %forecast_0.1 = (f32[32,9,8,128]{3,2,1,0:T(8,128)}, f32[32,2,8,128]{3,2,1,0:T(8,128)}, f32[8,128]{1,0:T(8,128)S(1)}) custom-call(f32[64,8,640]{2,1,0:T(8,128)S(1)} %get-tuple-element.45.turned, f32[64,8,640]{2,1,0:T(8,128)S(1)} %get-tuple-element.46.wet, f32[64,8,640]{2,1,0:T(8,128)S(1)} %get-tuple-element.47.source, ...), custom_call_target="tpu_custom_call" | custom-call | flops 40000000 | bytes 3000000 | tf_op jit(solution)/shard_map/forecast_0/pallas_call | solution.py:640
  17.2 0.0 copy-start.1
  17.2 11.5 %all-to-all-start.3 = ((f32[32,9,8,128]{3,2,1,0:T(8,128)}), f32[32,9,8,128]{3,2,1,0:T(8,128)S(1)}, u32[]{:S(2)}, u32[]{:S(2)}) async-start(f32[32,9,8,128]{3,2,1,0:T(8,128)} %get-tuple-element.54), calls=%async_computation.3 | async-start | bytes 2359296 | tf_op jit(solution)/shard_map/all_to_all | solution.py:654
  28.7 0.0 copy-done.1
  28.7 0.2 census.1
  28.9 0.5 slice.25
  29.9 1.2 locate.1
  31.1 0.7 copy-done.5
  31.9 1.6 prepare_1.1
  33.5 0.0 copy-start.8
  33.5 0.0 copy-start.9
  33.5 0.0 copy-start.12
  33.5 4.7 %forecast_1.1 = (f32[32,10,8,128]{3,2,1,0:T(8,128)S(1)}, f32[32,2,8,128]{3,2,1,0:T(8,128)}) custom-call(f32[64,8,640]{2,1,0:T(8,128)S(1)} %get-tuple-element.55.turned, f32[64,8,640]{2,1,0:T(8,128)S(1)} %get-tuple-element.56.wet, f32[64,8,640]{2,1,0:T(8,128)S(1)} %get-tuple-element.57.source, f32[68,8,640]{2,1,0:T(8,128)S(1)} %get-tuple-element.58.sea8, ...), custom_call_target="tpu_custom_call" | custom-call | flops 40000000 | bytes 3000000 | tf_op jit(solution)/shard_map/forecast_1/pallas_call | solution.py:640
  38.3 0.0 copy-start.13
  38.3 22.2 %all-to-all-done.3.held_ref.data0_ref = f32[32,9,8,128]{3,2,1,0:T(8,128)S(1)} async-done(((f32[32,9,8,128]{3,2,1,0:T(8,128)}), f32[32,9,8,128]{3,2,1,0:T(8,128)S(1)}, u32[]{:S(2)}, u32[]{:S(2)}) %all-to-all-start.3) | async-done | bytes 1179680 | tf_op jit(solution)/shard_map/all_to_all | solution.py:654
  60.5 0.0 copy-done.8
  60.5 0.0 copy-done.9
  60.5 0.0 copy-done.12
  60.5 1.0 gram.1
  61.6 0.0 copy-done.13
  61.6 39.7 %all_to_all.29.data1_ref = f32[32,10,8,128]{3,2,1,0:T(8,128)S(1)} all-to-all(f32[32,10,8,128]{3,2,1,0:T(8,128)S(1)} %get-tuple-element.67), channel_id=1, replica_groups=mesh['member'=32,'domain'=8] {'member'}, dimensions={0} | all-to-all | bytes 2621440 | tf_op jit(solution)/shard_map/all_to_all | solution.py:654
  101.3 2.4 %mix.1 = f32[32,18,8,128]{3,2,1,0:T(8,128)S(1)} custom-call(f32[32,9,8,128]{3,2,1,0:T(8,128)S(1)} %all-to-all-done.3.held_ref.data0_ref, f32[32,10,8,128]{3,2,1,0:T(8,128)S(1)} %all_to_all.29.data1_ref), custom_call_target="tpu_custom_call" | custom-call | tf_op jit(solution)/shard_map/mix/pallas_call | solution.py:723
  103.6 0.0 copy-start
  103.6 0.0 copy-start.3
  103.7 0.0 copy-start.4
  103.7 0.0 copy-start.6
  103.7 61.6 %all_to_all.30 = f32[32,18,8,128]{3,2,1,0:T(8,128)S(1)} all-to-all(f32[32,18,8,128]{3,2,1,0:T(8,128)S(1)} %mix.1), channel_id=1, replica_groups=mesh['member'=32,'domain'=8] {'member'}, dimensions={0} | all-to-all | bytes 4718592 | tf_op jit(solution)/shard_map/all_to_all | solution.py:654
  165.2 0.0 copy-done
  165.2 0.0 copy-done.3
  165.2 0.0 copy-done.4
  165.2 0.0 copy-done.6
  165.2 4.2 %settle.1 = f32[1,2,8,64,640]{4,3,2,1,0:T(8,128)} custom-call(s32[32,128]{1,0:T(8,128)S(1)} %copy-done.6, f32[576,8,128]{2,1,0:T(8,128)S(1)} %bitcast.16, f32[32,2,8,128]{3,2,1,0:T(8,128)S(1)} %get-tuple-element.68.refs_1_, f32[32,2,8,128]{3,2,1,0:T(8,128)} %get-tuple-element.69.refs_2_, s32[32,1280]{1,0:T(8,128)S(1)} %copy-done.3, f32[64,640]{1,0:T(8,128)S(1)} %copy-done.4, ...), custom_call_target="tpu_custom_call" | custom-call | tf_op jit(solution)/shard_map/settle/pallas_call | solution.py:735
  (7 shorter events, 0.1 us)
Async XLA Ops:
  0.8 9.1 %copy-start.2 = (f32[1,2,64,640]{3,2,1,0:T(8,128)S(1)}, f32[1,2,64,640]{3,2,1,0:T(8,128)}, u32[]{:S(2)}) copy-start(f32[1,2,64,640]{3,2,1,0:T(8,128)} %flux_ref.3) | copy-start | bytes 983044
  2.0 9.5 %collective-permute-start = (f32[2,17,640]{2,1,0:T(8,128)S(1)}, f32[2,17,640]{2,1,0:T(8,128)S(1)}, u32[]{:S(2)}, u32[]{:S(2)}) collective-permute-start(f32[2,17,640]{2,1,0:T(8,128)S(1)} %pad_maximum_fusion.1), channel_id=1, source_target_pairs={{0,1},{1,2},{2,3},{3,4},{4,5},{5,6},{6,7},{8,9},{9,10},{10,11},{11... | collective-permute-start | bytes 261128 | tf_op jit(solution)/shard_map/ppermute | solution.py:563
  4.0 7.5 %collective-permute-start.1 = (f32[2,17,640]{2,1,0:T(8,128)S(1)}, f32[2,17,640]{2,1,0:T(8,128)S(1)}, u32[]{:S(2)}, u32[]{:S(2)}) collective-permute-start(f32[2,17,640]{2,1,0:T(8,128)S(1)} %pad_maximum_fusion.2), channel_id=1, source_target_pairs={{1,0},{2,1},{3,2},{4,3},{5,4},{6,5},{7,6},{9,8},{10,9},{11,10},{12... | collective-permute-start | bytes 261128 | tf_op jit(solution)/shard_map/ppermute | solution.py:564
  9.9 1.6 copy-start.7
  9.9 1.6 copy-start.10
  10.0 1.6 copy-start.11
  17.2 11.5 %copy-start.1 = (s32[512,640]{1,0:T(8,128)S(1)}, s32[512,640]{1,0:T(8,128)}, u32[]{:S(2)}) copy-start(s32[512,640]{1,0:T(8,128)} %mask_ref.1) | copy-start | bytes 3932164
  17.2 43.2 %all-to-all-start.3 = ((f32[32,9,8,128]{3,2,1,0:T(8,128)}), f32[32,9,8,128]{3,2,1,0:T(8,128)S(1)}, u32[]{:S(2)}, u32[]{:S(2)}) async-start(f32[32,9,8,128]{3,2,1,0:T(8,128)} %get-tuple-element.54), calls=%async_computation.3 | async-start | bytes 2359296 | tf_op jit(solution)/shard_map/all_to_all | solution.py:654
  31.1 0.7 copy-start.5
  33.5 27.0 %copy-start.8 = (f32[1,32,256]{2,1,0:T(8,128)S(1)}, f32[1,32,256]{2,1,0:T(8,128)}, u32[]{:S(2)}) copy-start(f32[1,32,256]{2,1,0:T(8,128)} %value_ref.1) | copy-start | bytes 98308
  33.5 27.0 %copy-start.9 = (f32[1,32,256]{2,1,0:T(8,128)S(1)}, f32[1,32,256]{2,1,0:T(8,128)}, u32[]{:S(2)}) copy-start(f32[1,32,256]{2,1,0:T(8,128)} %error_ref.1) | copy-start | bytes 98308
  33.5 27.0 %copy-start.12 = (s32[1,32]{1,0:T(1,128)S(1)}, s32[1,32]{1,0:T(1,128)}, u32[]{:S(2)}) copy-start(s32[1,32]{1,0:T(1,128)} %count_ref.1) | copy-start | bytes 388
  38.3 23.3 %copy-start.13 = (f32[32,2,8,128]{3,2,1,0:T(8,128)S(1)}, f32[32,2,8,128]{3,2,1,0:T(8,128)}, u32[]{:S(2)}) copy-start(f32[32,2,8,128]{3,2,1,0:T(8,128)} %get-tuple-element.62) | copy-start | bytes 786436
  103.6 61.6 %copy-start = (f32[1,2,8,64,640]{4,3,2,1,0:T(8,128)S(1)}, f32[1,2,8,64,640]{4,3,2,1,0:T(8,128)}, u32[]{:S(2)}) copy-start(f32[1,2,8,64,640]{4,3,2,1,0:T(8,128)} %refs_5_.1) | copy-start | bytes 7864324
  103.6 61.6 %copy-start.3 = (s32[32,1280]{1,0:T(8,128)S(1)}, s32[32,1280]{1,0:T(8,128)}, u32[]{:S(2)}) copy-start(s32[32,1280]{1,0:T(8,128)} %get-tuple-element.70.refs_3_) | copy-start | bytes 491524
  103.7 61.6 %copy-start.4 = (f32[64,640]{1,0:T(8,128)S(1)}, f32[64,640]{1,0:T(8,128)}, u32[]{:S(2)}) copy-start(f32[64,640]{1,0:T(8,128)} %get-tuple-element.71.refs_4_) | copy-start | bytes 491524
  103.7 61.6 %copy-start.6 = (s32[32,128]{1,0:T(8,128)S(1)}, s32[32,128]{1,0:T(8,128)}, u32[]{:S(2)}) copy-start(s32[32,128]{1,0:T(8,128)} %get-tuple-element.53.rest_0_.first_ref) | copy-start | bytes 49156
